TPU v7x, 768 devices: a whole 4x8x12 slice. The times are simulated.
768 devices in a mesh: srv: 48 (over z, y_lo), blk: 8 (over x, y_hi), rep: 2 (over core).
Axes of the slice: x: 4, y: 8 (y_hi: 2, y_lo: 4; y = y_hi * 4 + y_lo), z: 12, core: 2. Of those that a mesh axis runs over, the one named last changes fastest.
Arguments:
- queries: bfloat16 [48, 8, 256, 4096], P('srv', 'blk', 'rep'), parts along dimension 2, may hold values from -16 to 16
- destination: int32 [48, 8, 64], P('srv', 'blk', 'rep'), parts along dimension 2, may hold values from 0 to 47, as said below
- offsets: int32 [48, 8, 64], P('srv', 'blk', 'rep'), parts along dimension 2, may hold values from 0 to 124
- key_rows: bfloat16 [48, 1024, 512], P('srv', 'blk', 'rep'), parts along dimension 2, may hold values from -16 to 16
- value_rows: bfloat16 [48, 1024, 512], P('srv', 'blk', 'rep'), parts along dimension 2, may hold values from -6 to 6
- lengths: int32 [48, 16], P('srv', 'rep'), parts along dimension 1, may hold values from 1 to 385, 1024 in all within a row
Outputs:
- attended: bfloat16 [48, 8, 256, 4096], P('srv', 'blk', 'rep'), parts along dimension 2
There are 2 independent parts, one for each index of `rep`. A program takes and returns all parts, laid end to end along the dimension named above; each array names one. Nothing has to cross between parts.
Inputs may be any that keep to these rules, and one draw needn't show every extreme that they name: `destination`: within each round (tasks r * 16 to r * 16 + 15 of a device) a device names 16 different servers; in each round and for each blk index, 2 servers are named by every device of that blk index.
All inputs are finite; a program needn't handle non-finite values.
Results may differ from a plain program's by a relative error of at most 0.0033.
Values may be sent and summed in bfloat16 or wider, within the bound.
No kernel may reach another device: no remote copies, remote signals or barrier semaphores. Data moves between devices by JAX's collectives and lax.ppermute only.
A program may use at most 32 MiB of HBM per device.

v0:
```python
import math

import jax
import jax.numpy as jnp
from jax import lax
from jax.sharding import PartitionSpec as P

QH = 32
KVH = 2
HD = 128
R = 4
ROUNDS = 2


def from_behind(shard, axis, by):
    peers = lax.axis_size(axis)
    pairs = [(i, i + by) for i in range(peers) if 0 <= i + by < peers]
    return lax.ppermute(shard, axis, pairs)


def for_sending(shard):
    return jax.tree.map(lambda a: a.astype(jnp.bfloat16) if a.dtype == jnp.float32 else a, shard)


def document_of(positions, boundary):
    return jnp.sum((boundary[None, :] <= positions[:, None]).astype(jnp.int32), axis=1)


def give_back(served):
    return lax.all_to_all(served, "srv", split_axis=0, concat_axis=0, tiled=True)


def on_device(queries, destination, offsets, key_rows, value_rows, lengths):
    servers = lax.axis_size("srv")
    blk_index = lax.axis_index("blk")
    block_rows = key_rows.shape[1]
    kv_width = key_rows.shape[2]
    query_width = queries.shape[3]
    per_round = destination.shape[2] // ROUNDS
    groups = QH // KVH
    scaling = 1.0 / math.sqrt(HD)
    boundary = jnp.cumsum(lengths[0])
    joined = jnp.concatenate([key_rows[0], value_rows[0]], axis=1)
    pieces = [joined]
    current = joined
    for hop_number in range(3):
        current = from_behind(current, "blk", 1)
        pieces.append(current)
    window = jnp.concatenate(pieces[::-1], axis=0)
    key_pos = (blk_index - 3) * block_rows + jnp.arange(4 * block_rows, dtype=jnp.int32)
    key_valid = key_pos >= 0
    key_doc = document_of(key_pos, boundary)
    key_heads = jnp.transpose(window[:, :kv_width].reshape(4 * block_rows, KVH, HD), (1, 0, 2))
    value_heads = jnp.transpose(window[:, kv_width:].reshape(4 * block_rows, KVH, HD), (1, 0, 2))
    local_queries = queries[0, 0].reshape(ROUNDS, per_round, R, query_width)
    local_targets = destination[0, 0].reshape(ROUNDS, per_round)
    local_starts = offsets[0, 0].reshape(ROUNDS, per_round)
    outgoing = []
    for turn in range(ROUNDS):
        sending = (
            jnp.zeros((servers, 1, R, query_width), jnp.bfloat16)
            .at[local_targets[turn], 0]
            .set(local_queries[turn])
        )
        placing = (
            jnp.zeros((servers, 1), jnp.int32).at[local_targets[turn], 0].set(local_starts[turn])
        )
        outgoing.append((sending, placing))
    collected = []
    for turn in range(ROUNDS):
        query_buffer, offset_buffer = lax.all_to_all(
            for_sending(outgoing[turn]), "srv", split_axis=0, concat_axis=0, tiled=True
        )
        leading = query_buffer.shape[:2]
        rows = query_buffer.reshape(-1, query_width)
        query_pos = (
            blk_index * block_rows + offset_buffer[..., None] + jnp.arange(R, dtype=jnp.int32)
        )
        query_pos = query_pos.reshape(-1)
        query_doc = document_of(query_pos, boundary)
        allowed = (
            key_valid[None, :]
            & (key_pos[None, :] <= query_pos[:, None])
            & (key_doc[None, :] == query_doc[:, None])
        )
        query_heads = jnp.transpose(rows.reshape(-1, KVH, groups, HD), (1, 0, 2, 3))

        def one_head(triple):
            query_head, key_head, value_head = triple
            scores = (
                jnp.einsum("mgd,nd->gmn", query_head, key_head, preferred_element_type=jnp.float32)
                * scaling
            )
            scores = jnp.where(allowed[None], scores, -1e30)
            highest = jnp.max(scores, axis=2, keepdims=True)
            weights = jnp.exp(scores - highest)
            denominator = jnp.sum(weights, axis=2)
            weighted = jnp.einsum(
                "gmn,nd->mgd",
                weights.astype(jnp.bfloat16),
                value_head,
                preferred_element_type=jnp.float32,
            )
            return weighted / jnp.transpose(denominator)[:, :, None]

        per_head = lax.map(one_head, (query_heads, key_heads, value_heads))
        merged = jnp.transpose(per_head, (1, 0, 2, 3)).reshape(rows.shape).astype(jnp.bfloat16)
        served = merged.reshape(leading + (R, query_width))
        returned = give_back(served)
        collected.append(returned[local_targets[turn], 0])
    gathered = jnp.stack(collected)
    return gathered.reshape(1, 1, ROUNDS * per_round * R, query_width)


def solution(mesh):
    placed = (
        P("srv", "blk", "rep", None),
        P("srv", "blk", "rep"),
        P("srv", "blk", "rep"),
        P("srv", "blk", "rep"),
        P("srv", "blk", "rep"),
        P("srv", "rep"),
    )
    return jax.shard_map(
        on_device,
        mesh=mesh,
        in_specs=placed,
        out_specs=P("srv", "blk", "rep", None),
        check_vma=False,
    )
```

profile of v0, /device:TPU:6, one launch (start us, length us, event | category | flops | bytes accessed | tf_op | source)
XLA Modules:
  0.0 309.9 jit_solution(11371948878523741372)
XLA Ops:
  2.9 18.9 %all-to-all-start = ((s32[48,1,1]{2,1,0:T(1,128)}), s32[48,1,1]{2,1,0:T(1,128)S(1)}, u32[]{:S(2)}, u32[]{:S(2)}) async-start(s32[48,1,1]{2,1,0:T(1,128)} %copy.49), calls=%async_computation | async-start | bytes 49152 | tf_op jit(solution)/shard_map/all_to_all | solution.py:71
  23.1 11.0 %all-to-all-done = s32[48,1,1]{2,1,0:T(1,128)S(1)} async-done(((s32[48,1,1]{2,1,0:T(1,128)}), s32[48,1,1]{2,1,0:T(1,128)S(1)}, u32[]{:S(2)}, u32[]{:S(2)}) %all-to-all-start) | async-done | bytes 224 | tf_op jit(solution)/shard_map/all_to_all | solution.py:71
  34.1 4.5 %all-to-all-start.3 = ((s32[48,1,1]{2,1,0:T(1,128)}), s32[48,1,1]{2,1,0:T(1,128)S(1)}, u32[]{:S(2)}, u32[]{:S(2)}) async-start(s32[48,1,1]{2,1,0:T(1,128)} %copy.56), calls=%async_computation.3 | async-start | bytes 49152 | tf_op jit(solution)/shard_map/all_to_all | solution.py:71
  42.0 2.6 scatter_fusion
  44.6 6.3 %all-to-all-done.3 = s32[48,1,1]{2,1,0:T(1,128)S(1)} async-done(((s32[48,1,1]{2,1,0:T(1,128)}), s32[48,1,1]{2,1,0:T(1,128)S(1)}, u32[]{:S(2)}, u32[]{:S(2)}) %all-to-all-start.3) | async-done | bytes 224 | tf_op jit(solution)/shard_map/all_to_all | solution.py:71
  50.9 6.5 %all-to-all-start.1 = ((bf16[48,1,4,4096]{3,2,1,0:T(4,128)(2,1)}), bf16[48,1,4,4096]{3,2,1,0:T(4,128)(2,1)S(1)}, u32[]{:S(2)}, u32[]{:S(2)}) async-start(bf16[48,1,4,4096]{3,2,1,0:T(4,128)(2,1)} %bitcast.8), calls=%async_computation.1 | async-start | bytes 3145728 | tf_op jit(solution)/shard_map/all_to_all | solution.py:71
  57.7 5.0 %collective-permute-start = (bf16[128,512]{0,1:T(8,128)(2,1)S(1)}, bf16[128,512]{0,1:T(8,128)(2,1)S(1)}, u32[]{:S(2)}, u32[]{:S(2)}) collective-permute-start(bf16[128,512]{0,1:T(8,128)(2,1)S(1)} %pad_maximum_fusion.1), channel_id=1, source_target_pairs={{0,2},{2,4},{4,6},{6,8},{8,10},{10,12},{12,14},{1,3},{3,5},{5,7},{... | collective-permute-start | bytes 393224 | tf_op jit(solution)/shard_map/ppermute | solution.py:18
  65.1 2.6 scatter_fusion.1
  69.5 8.0 %collective-permute-done = bf16[128,512]{0,1:T(8,128)(2,1)S(1)} collective-permute-done((bf16[128,512]{0,1:T(8,128)(2,1)S(1)}, bf16[128,512]{0,1:T(8,128)(2,1)S(1)}, u32[]{:S(2)}, u32[]{:S(2)}) %collective-permute-start) | collective-permute-done | bytes 131104 | tf_op jit(solution)/shard_map/ppermute | solution.py:18
  79.3 34.7 %all-to-all-done.1 = bf16[48,1,4,4096]{3,2,1,0:T(4,128)(2,1)S(1)} async-done(((bf16[48,1,4,4096]{3,2,1,0:T(4,128)(2,1)}), bf16[48,1,4,4096]{3,2,1,0:T(4,128)(2,1)S(1)}, u32[]{:S(2)}, u32[]{:S(2)}) %all-to-all-start.1) | async-done | bytes 1572896 | tf_op jit(solution)/shard_map/all_to_all | solution.py:71
  115.2 6.2 %all-to-all-start.4 = ((bf16[48,1,4,4096]{3,2,1,0:T(4,128)(2,1)}), bf16[48,1,4,4096]{3,2,1,0:T(4,128)(2,1)S(1)}, u32[]{:S(2)}, u32[]{:S(2)}) async-start(bf16[48,1,4,4096]{3,2,1,0:T(4,128)(2,1)} %bitcast.23), calls=%async_computation.4 | async-start | bytes 3145728 | tf_op jit(solution)/shard_map/all_to_all | solution.py:71
  121.6 5.2 %collective-permute-start.2 = (bf16[128,512]{0,1:T(8,128)(2,1)S(1)}, bf16[128,512]{0,1:T(8,128)(2,1)S(1)}, u32[]{:S(2)}, u32[]{:S(2)}) collective-permute-start(bf16[128,512]{0,1:T(8,128)(2,1)S(1)} %collective-permute-done.1), channel_id=1, source_target_pairs={{0,2},{2,4},{4,6},{6,8},{8,10},{10,12},{12,14},{1,3},{3,5},{5,7},{... | collective-permute-start | bytes 393224 | tf_op jit(solution)/shard_map/ppermute | solution.py:18
  127.1 13.7 %collective-permute-done.2 = bf16[128,512]{0,1:T(8,128)(2,1)S(1)} collective-permute-done((bf16[128,512]{0,1:T(8,128)(2,1)S(1)}, bf16[128,512]{0,1:T(8,128)(2,1)S(1)}, u32[]{:S(2)}, u32[]{:S(2)}) %collective-permute-start.2) | collective-permute-done | bytes 131104 | tf_op jit(solution)/shard_map/ppermute | solution.py:18
  141.9 3.2 %reshape_reshape.6 = bf16[192,2,16,128]{3,2,1,0:T(8,128)(2,1)S(1)} reshape(bf16[48,1,4,4096]{3,2,1,0:T(4,128)(2,1)} %copy-done) | data formatting | bytes 3145728 | tf_op jit(solution)/shard_map/reshape;reshape | solution.py:86
  146.6 13.3 %while.22 = (s32[]{:T(128)}, bf16[2,192,16,128]{3,1,2,0:T(8,128)(2,1)}, bf16[2,512,128]{2,1,0:T(8,128)(2,1)}, bf16[2,512,128]{2,1,0:T(8,128)(2,1)S(1)}, bf16[2,1...) while((s32[]{:T(128)}, ...), condition=%wide.region_8.9_spmd.clone, body=%wide.region_5.0_spmd.clone.sunk | while | flops 823388160 | bytes 24587408 | solution.py:106
  148.4 2.2 fusion.57
  150.6 2.7 bitcast_dynamic-update-slice_fusion.4
  155.0 2.2 fusion.57
  157.2 2.7 bitcast_dynamic-update-slice_fusion.4
  159.9 2.4 copy.53
  164.2 14.7 %all-to-all-done.4 = bf16[48,1,4,4096]{3,2,1,0:T(4,128)(2,1)S(1)} async-done(((bf16[48,1,4,4096]{3,2,1,0:T(4,128)(2,1)}), bf16[48,1,4,4096]{3,2,1,0:T(4,128)(2,1)S(1)}, u32[]{:S(2)}, u32[]{:S(2)}) %all-to-all-start.4) | async-done | bytes 1572896 | tf_op jit(solution)/shard_map/all_to_all | solution.py:71
  178.9 6.5 %all-to-all-start.2 = ((bf16[48,1,4,4096]{3,2,1,0:T(4,128)(2,1)}), bf16[48,1,4,4096]{3,2,1,0:T(4,128)(2,1)}, u32[]{:S(2)}, u32[]{:S(2)}) async-start(bf16[48,1,4,4096]{3,2,1,0:T(4,128)(2,1)} %bitcast.15), calls=%async_computation.2 | async-start | bytes 3145728 | tf_op jit(solution)/shard_map/all_to_all | solution.py:30
  188.5 13.3 %while.23 = (s32[]{:T(128)}, bf16[2,192,16,128]{3,1,2,0:T(8,128)(2,1)}, bf16[2,512,128]{2,1,0:T(8,128)(2,1)}, bf16[2,512,128]{2,1,0:T(8,128)(2,1)S(1)}, bf16[2,1...) while((s32[]{:T(128)}, ...), condition=%wide.region_15.16_spmd.clone, body=%wide.region_12.15_spmd.clone.sunk | while | flops 823388160 | bytes 24587408 | solution.py:106
  190.2 2.2 fusion.61
  192.4 2.7 bitcast_dynamic-update-slice_fusion.5
  196.9 2.2 fusion.61
  199.1 2.8 bitcast_dynamic-update-slice_fusion.5
  201.8 2.4 copy.60
  206.1 36.9 %all-to-all-done.2 = bf16[48,1,4,4096]{3,2,1,0:T(4,128)(2,1)} async-done(((bf16[48,1,4,4096]{3,2,1,0:T(4,128)(2,1)}), bf16[48,1,4,4096]{3,2,1,0:T(4,128)(2,1)}, u32[]{:S(2)}, u32[]{:S(2)}) %all-to-all-start.2) | async-done | bytes 1572896 | tf_op jit(solution)/shard_map/all_to_all | solution.py:30
  243.0 6.4 %all-to-all-start.5 = ((bf16[48,1,4,4096]{3,2,1,0:T(4,128)(2,1)}), bf16[48,1,4,4096]{3,2,1,0:T(4,128)(2,1)S(1)}, u32[]{:S(2)}, u32[]{:S(2)}) async-start(bf16[48,1,4,4096]{3,2,1,0:T(4,128)(2,1)} %bitcast.28), calls=%async_computation.5 | async-start | bytes 3145728 | tf_op jit(solution)/shard_map/all_to_all | solution.py:30
  249.3 2.4 gather_fusion
  251.7 55.3 %all-to-all-done.5 = bf16[48,1,4,4096]{3,2,1,0:T(4,128)(2,1)S(1)} async-done(((bf16[48,1,4,4096]{3,2,1,0:T(4,128)(2,1)}), bf16[48,1,4,4096]{3,2,1,0:T(4,128)(2,1)S(1)}, u32[]{:S(2)}, u32[]{:S(2)}) %all-to-all-start.5) | async-done | bytes 1572896 | tf_op jit(solution)/shard_map/all_to_all | solution.py:30
  (66 shorter events, 34.6 us)
Async XLA Ops:
  2.9 31.2 %all-to-all-start = ((s32[48,1,1]{2,1,0:T(1,128)}), s32[48,1,1]{2,1,0:T(1,128)S(1)}, u32[]{:S(2)}, u32[]{:S(2)}) async-start(s32[48,1,1]{2,1,0:T(1,128)} %copy.49), calls=%async_computation | async-start | bytes 49152 | tf_op jit(solution)/shard_map/all_to_all | solution.py:71
  34.1 16.8 %all-to-all-start.3 = ((s32[48,1,1]{2,1,0:T(1,128)}), s32[48,1,1]{2,1,0:T(1,128)S(1)}, u32[]{:S(2)}, u32[]{:S(2)}) async-start(s32[48,1,1]{2,1,0:T(1,128)} %copy.56), calls=%async_computation.3 | async-start | bytes 49152 | tf_op jit(solution)/shard_map/all_to_all | solution.py:71
  40.1 17.3 %copy-start.3 = (bf16[1,128,256]{2,1,0:T(8,128)(2,1)S(1)}, bf16[1,128,256]{2,1,0:T(8,128)(2,1)}, u32[]{:S(2)}) copy-start(bf16[1,128,256]{2,1,0:T(8,128)(2,1)} %param.13) | copy-start | bytes 196612
  40.1 17.4 %copy-start.4 = (bf16[1,128,256]{2,1,0:T(8,128)(2,1)S(1)}, bf16[1,128,256]{2,1,0:T(8,128)(2,1)}, u32[]{:S(2)}) copy-start(bf16[1,128,256]{2,1,0:T(8,128)(2,1)} %param.14) | copy-start | bytes 196612
  40.1 22.6 %copy-start.5 = (s32[1,8]{1,0:T(1,128)S(1)}, s32[1,8]{1,0:T(1,128)}, u32[]{:S(2)}) copy-start(s32[1,8]{1,0:T(1,128)} %param.15) | copy-start | bytes 100
  50.9 63.2 %all-to-all-start.1 = ((bf16[48,1,4,4096]{3,2,1,0:T(4,128)(2,1)}), bf16[48,1,4,4096]{3,2,1,0:T(4,128)(2,1)S(1)}, u32[]{:S(2)}, u32[]{:S(2)}) async-start(bf16[48,1,4,4096]{3,2,1,0:T(4,128)(2,1)} %bitcast.8), calls=%async_computation.1 | async-start | bytes 3145728 | tf_op jit(solution)/shard_map/all_to_all | solution.py:71
  57.7 19.8 %collective-permute-start = (bf16[128,512]{0,1:T(8,128)(2,1)S(1)}, bf16[128,512]{0,1:T(8,128)(2,1)S(1)}, u32[]{:S(2)}, u32[]{:S(2)}) collective-permute-start(bf16[128,512]{0,1:T(8,128)(2,1)S(1)} %pad_maximum_fusion.1), channel_id=1, source_target_pairs={{0,2},{2,4},{4,6},{6,8},{8,10},{10,12},{12,14},{1,3},{3,5},{5,7},{... | collective-permute-start | bytes 393224 | tf_op jit(solution)/shard_map/ppermute | solution.py:18
  77.4 44.1 %collective-permute-start.1 = (bf16[128,512]{0,1:T(8,128)(2,1)S(1)}, bf16[128,512]{0,1:T(8,128)(2,1)S(1)}, u32[]{:S(2)}, u32[]{:S(2)}) collective-permute-start(bf16[128,512]{0,1:T(8,128)(2,1)S(1)} %collective-permute-done), channel_id=1, source_target_pairs={{0,2},{2,4},{4,6},{6,8},{8,10},{10,12},{12,14},{1,3},{3,5},{5,7},{... | collective-permute-start | bytes 393224 | tf_op jit(solution)/shard_map/ppermute | solution.py:18
  114.1 1.2 copy-start
  115.2 63.7 %all-to-all-start.4 = ((bf16[48,1,4,4096]{3,2,1,0:T(4,128)(2,1)}), bf16[48,1,4,4096]{3,2,1,0:T(4,128)(2,1)S(1)}, u32[]{:S(2)}, u32[]{:S(2)}) async-start(bf16[48,1,4,4096]{3,2,1,0:T(4,128)(2,1)} %bitcast.23), calls=%async_computation.4 | async-start | bytes 3145728 | tf_op jit(solution)/shard_map/all_to_all | solution.py:71
  121.6 19.3 %collective-permute-start.2 = (bf16[128,512]{0,1:T(8,128)(2,1)S(1)}, bf16[128,512]{0,1:T(8,128)(2,1)S(1)}, u32[]{:S(2)}, u32[]{:S(2)}) collective-permute-start(bf16[128,512]{0,1:T(8,128)(2,1)S(1)} %collective-permute-done.1), channel_id=1, source_target_pairs={{0,2},{2,4},{4,6},{6,8},{8,10},{10,12},{12,14},{1,3},{3,5},{5,7},{... | collective-permute-start | bytes 393224 | tf_op jit(solution)/shard_map/ppermute | solution.py:18
  148.3 2.2 copy-start.1
  155.0 2.2 copy-start.1
  178.9 64.1 %all-to-all-start.2 = ((bf16[48,1,4,4096]{3,2,1,0:T(4,128)(2,1)}), bf16[48,1,4,4096]{3,2,1,0:T(4,128)(2,1)}, u32[]{:S(2)}, u32[]{:S(2)}) async-start(bf16[48,1,4,4096]{3,2,1,0:T(4,128)(2,1)} %bitcast.15), calls=%async_computation.2 | async-start | bytes 3145728 | tf_op jit(solution)/shard_map/all_to_all | solution.py:30
  190.2 2.2 copy-start.2
  196.9 2.2 copy-start.2
  243.0 64.1 %all-to-all-start.5 = ((bf16[48,1,4,4096]{3,2,1,0:T(4,128)(2,1)}), bf16[48,1,4,4096]{3,2,1,0:T(4,128)(2,1)S(1)}, u32[]{:S(2)}, u32[]{:S(2)}) async-start(bf16[48,1,4,4096]{3,2,1,0:T(4,128)(2,1)} %bitcast.28), calls=%async_computation.5 | async-start | bytes 3145728 | tf_op jit(solution)/shard_map/all_to_all | solution.py:30
where the time goes:
time: 311 us; the launch traced here: 310 us
  waiting for transfers between devices  180 us (58%)
  starting transfers between devices  61 us (20%)
  local copies, waits for them, and re-layouts  38.2 us (12%)
  matrix products  16.4 us (5%)
  other arithmetic  13.3 us (4%)
    all_to_all x2, waiting for transfers between devices, give_back(): lax.all_to_all(served, 'srv', split_axis=0, concat_axis=0, tiled=True)  92.1 us
    all_to_all x4, waiting for transfers between devices, on_device(): lax.all_to_all(for_sending(outgoing[turn]), 'srv', split_axis=0, concat_a...  66.7 us
    all_to_all x4, starting transfers between devices, on_device(): lax.all_to_all(for_sending(outgoing[turn]), 'srv', split_axis=0, concat_a...  36.1 us
    ppermute x3, waiting for transfers between devices, from_behind(): return lax.ppermute(shard, axis, pairs)  21.6 us
    all_to_all x2, starting transfers between devices, give_back(): lax.all_to_all(served, 'srv', split_axis=0, concat_axis=0, tiled=True)  12.8 us
    ppermute x3, starting transfers between devices, from_behind(): return lax.ppermute(shard, axis, pairs)  12.1 us
    dot_general x4, matrix products, one_head(): jnp.einsum('gmn,nd->mgd', weights.astype(jnp.bfloat16), value_head, prefe...  11 us
    reduce_sum x4, other arithmetic, one_head(): denominator = jnp.sum(weights, axis=2)  8.73 us
  transfers between devices with their start and end apart: 9, of which 8 were waited for; matrix products, arithmetic and copies ran while one was open for 20% of the time, Pallas kernels for 0%

commit v1 on v0

v1 whole, which is shorter than its diff:
```python
import math

import jax
import jax.numpy as jnp
from jax import lax
from jax.experimental import pallas as pl
from jax.sharding import Mesh
from jax.sharding import PartitionSpec as P

QH = 32
KVH = 2
HD = 128
R = 4
ROUNDS = 2
COLS = 4
GROUPS = QH // KVH
DOCS = 8
BEHIND = 3
SCALE = math.log2(math.e) / math.sqrt(HD)


def attend_kernel(*refs):
    servers = len(refs) // (3 * COLS + 1)
    windows = refs[2 * COLS * servers : (2 * COLS + 1) * servers]
    for s in range(servers):
        serve(
            refs[COLS * s : COLS * (s + 1)],
            refs[COLS * (servers + s) : COLS * (servers + s + 1)],
            windows[s],
            refs[(2 * COLS + 1) * servers + COLS * s : (2 * COLS + 1) * servers + COLS * (s + 1)],
        )


def serve(query_refs, place_refs, window_ref, out_refs):
    slots = ROUNDS * R
    rows = COLS * slots
    span = window_ref.shape[0] - DOCS
    marks = window_ref[span:, : 2 * HD].astype(jnp.float32)
    starts = marks[:, :HD] * 16.0 + marks[:, HD:]
    place = jnp.concatenate([ref[...].astype(jnp.float32) for ref in place_refs], axis=0)
    place = place + float(BEHIND * HD)
    first = jnp.zeros_like(place)
    for doc in range(DOCS):
        start = jnp.broadcast_to(starts[doc : doc + 1, :], place.shape)
        first = jnp.maximum(first, jnp.where(start <= place, start, 0.0))
    lane = lax.broadcasted_iota(jnp.int32, place.shape, 1).astype(jnp.float32)
    bias = []
    for tile in range(span // HD):
        key_pos = lane + float(tile * HD)
        allowed = (key_pos >= first) & (key_pos <= place)
        bias.append(jnp.where(allowed, 0.0, -1e30))
    bias = jnp.concatenate(bias, axis=1)
    parts = 4
    per_part = GROUPS // parts
    for head in range(KVH):
        keys = window_ref[:span, 2 * head * HD : (2 * head + 1) * HD]
        values = window_ref[:span, (2 * head + 1) * HD : (2 * head + 2) * HD]
        for part in range(parts):
            first_head = head * GROUPS + part * per_part
            heads = range(first_head, first_head + per_part)
            query = jnp.concatenate(
                [
                    ref[:, h * HD : (h + 1) * HD].astype(jnp.float32)
                    for h in heads
                    for ref in query_refs
                ],
                axis=0,
            ).astype(jnp.bfloat16)
            scores = lax.dot_general(
                query, keys, (((1,), (1,)), ((), ())), preferred_element_type=jnp.float32
            )
            weights, inverse = [], []
            for n in range(per_part):
                scaled = scores[n * rows : (n + 1) * rows] * SCALE + bias
                weight = jnp.exp2(scaled - jnp.max(scaled, axis=1, keepdims=True))
                inverse.append(1.0 / jnp.sum(weight, axis=1, keepdims=True))
                weights.append(weight.astype(jnp.bfloat16))
            weighted = lax.dot_general(
                jnp.concatenate(weights, axis=0),
                values,
                (((1,), (0,)), ((), ())),
                preferred_element_type=jnp.float32,
            )
            for n, h in enumerate(heads):
                result = weighted[n * rows : (n + 1) * rows] * inverse[n]
                for c, ref in enumerate(out_refs):
                    ref[:, h * HD : (h + 1) * HD] = result[c * slots : (c + 1) * slots].astype(
                        jnp.bfloat16
                    )


def sources_of(order):
    far = 3 if order % 2 == 0 else 4
    return ((0, order), (1, order), (2, order), (far, order // 2))


def attend(arrived, windows, orders):
    slots = ROUNDS * R
    width = QH * HD
    queries, query_specs, place_specs, out_shape = [], [], [], []
    for order in orders:
        for group, at in sources_of(order):
            queries.append(arrived[group])
            query_specs.append(pl.BlockSpec((slots, width), lambda i, at=at: (at, 0)))
            place_specs.append(pl.BlockSpec((slots, HD), lambda i, at=at: (at, width // HD)))
            out_shape.append(jax.ShapeDtypeStruct((slots, width), jnp.bfloat16))
    window_spec = pl.BlockSpec(windows[0].shape, lambda i: (0, 0))
    return pl.pallas_call(
        attend_kernel,
        grid=(1,),
        in_specs=query_specs + place_specs + [window_spec] * len(windows),
        out_specs=[pl.BlockSpec((slots, width), lambda i: (0, 0))] * len(out_shape),
        out_shape=out_shape,
    )(*queries, *queries, *windows)


def along_z(array, by):
    planes = lax.axis_size("z")
    return lax.ppermute(array, "z", [(i, (i + by) % planes) for i in range(planes)])


def along_y(array, by):
    ring = 2 * COLS
    spot = [(i % COLS) * 2 + i // COLS for i in range(ring)]
    pairs = [(spot[i], spot[(i + by) % ring]) for i in range(ring)]
    return lax.ppermute(array, ("col", "yh"), pairs)


def along_x(array, by):
    peers = lax.axis_size("x")
    return lax.ppermute(array, "x", [(i, i + by) for i in range(peers - by)])


def window_of(key_rows, value_rows, lengths):
    x, upper = lax.axis_index("x"), lax.axis_index("yh")
    key, value = key_rows[0], value_rows[0]
    block = key.shape[0]
    joined = jnp.concatenate([key[:, :HD], value[:, :HD], key[:, HD:], value[:, HD:]], axis=1)
    other = lax.ppermute(joined, "yh", [(0, 1), (1, 0)])
    lower_block = jnp.where(upper == 0, joined, other)
    upper_block = jnp.where(upper == 0, other, joined)
    pair = jnp.concatenate([lower_block, upper_block], axis=0)
    pair_behind = along_x(pair, 1)
    last_behind = along_x(upper_block, 2)
    origin = (2 * x - BEHIND) * block
    lowest = jnp.maximum(0, -origin)
    ends = jnp.cumsum(lengths[0])[:-1] - origin
    starts = jnp.concatenate([lowest[None], jnp.clip(ends, lowest, (BEHIND + 2) * block)])
    high = jnp.broadcast_to((starts // 16)[:, None], (DOCS, HD))
    low = jnp.broadcast_to((starts % 16)[:, None], (DOCS, HD))
    marks = jnp.concatenate([high, low, high, low], axis=1).astype(jnp.bfloat16)
    return jnp.concatenate([last_behind, pair_behind, pair, marks], axis=0)


def pick(select, array):
    return jnp.dot(select, array, preferred_element_type=jnp.float32).astype(jnp.bfloat16)


def on_device(queries, destination, offsets, key_rows, value_rows, lengths):
    planes = lax.axis_size("z")
    column, plane = lax.axis_index("col"), lax.axis_index("z")
    upper = lax.axis_index("yh")
    block = key_rows.shape[1]
    rows = destination.shape[2] * R
    slots = ROUNDS * R
    reach = planes // 2
    window = window_of(key_rows, value_rows, lengths)

    target = jnp.repeat(destination[0, 0], R)
    row = jnp.arange(rows, dtype=jnp.int32)
    ahead = (target // COLS - plane) % planes
    order = jnp.where(ahead <= reach, jnp.maximum(2 * ahead - 1, 0), 2 * (planes - ahead))
    within = (row // (rows // ROUNDS)) * R + row % R
    across = (target % COLS - column) % COLS
    place = upper * block + jnp.repeat(offsets[0, 0], R) + row % R
    place = jnp.broadcast_to(place[:, None], (rows, HD)).astype(jnp.bfloat16)
    payload = jnp.concatenate([queries[0, 0], place], axis=1)
    groups = [
        (across == 0, order, 0),
        (across == 1, order, 1),
        (across == 3, order, -1),
        ((across == 2) & (order % 2 == 0), order // 2, 2),
        ((across == 2) & (order % 2 == 1), order // 2, -2),
    ]
    selects, arrived = [], []
    for number, (chosen, at, by) in enumerate(groups):
        count = (planes if number < 3 else reach) * slots
        slot = jnp.arange(count, dtype=jnp.int32)[:, None]
        select = (((at * slots + within)[None, :] == slot) & chosen[None, :]).astype(jnp.bfloat16)
        selects.append(select)
        sending = pick(select, payload)
        arrived.append(along_y(sending, by) if by else sending)

    served = {}

    def serve_orders(windows, orders):
        outs = attend(arrived, windows, orders)
        for n, number in enumerate(orders):
            for c, (group, at) in enumerate(sources_of(number)):
                served[group, at] = outs[COLS * n + c]

    serve_orders([window], [0])
    ahead_window, behind_window = window, window
    width = window.shape[1] // 2
    gathered = None

    def give_back(orders):
        backs, chosen = [], []
        for number, (_, _, by) in enumerate(groups):
            ats = [at for o in orders for group, at in sources_of(o) if group == number]
            if not ats:
                continue
            outgoing = jnp.concatenate([served[number, at] for at in ats], axis=0)
            back = along_y(outgoing, -by) if by else outgoing
            backs.append(back)
            chosen.append(selects[number][ats[0] * slots : (ats[-1] + 1) * slots])
        return pick(jnp.concatenate(chosen, axis=0).T, jnp.concatenate(backs, axis=0))

    for step in range(1, reach):
        ahead_window = along_z(ahead_window, -1)
        behind_window = along_z(behind_window, 1)
        serve_orders([ahead_window, behind_window], [2 * step - 1, 2 * step])
        if step == reach - 2:
            gathered = give_back(list(range(2 * step + 1)))
    last_left = along_z(ahead_window[:, :width], -1)
    last_right = along_z(behind_window[:, width:], 1)
    last = jnp.concatenate([last_left, last_right], axis=1)
    serve_orders([last], [planes - 1])
    rest = give_back(list(range(0 if gathered is None else 2 * (reach - 2) + 1, planes)))
    return (rest if gathered is None else gathered + rest)[None, None]


def solution(mesh):
    shape = dict(mesh.shape)
    fine = Mesh(
        mesh.devices.reshape(shape["srv"] // COLS, COLS, shape["blk"] // 2, 2, shape["rep"]),
        ("z", "col", "x", "yh", "rep"),
    )
    srv, blk = ("z", "col"), ("x", "yh")
    placed = (
        P(srv, blk, "rep", None),
        P(srv, blk, "rep"),
        P(srv, blk, "rep"),
        P(srv, blk, "rep"),
        P(srv, blk, "rep"),
        P(srv, "rep"),
    )

    return jax.shard_map(
        on_device,
        mesh=fine,
        in_specs=placed,
        out_specs=P(srv, blk, "rep", None),
        check_vma=False,
    )
```

time: 311 us -> 285 us (0.916)
  waiting for transfers between devices: 180 us -> 57 us
  starting transfers between devices: 61 us -> 108 us
  Pallas kernels: 0 us -> 46.2 us
  local copies, waits for them, and re-layouts: 38.2 us -> 53.6 us
  matrix products: 16.4 us -> 9.3 us
  other arithmetic: 13.3 us -> 7.17 us
    all_to_all x6 -> x0, waiting for transfers between devices: 159 us -> none  [the longest x2 92.1 us: give_back(): lax.all_to_all(served, 'srv', split_axis=0, concat_axis=0, tiled=True)]
    ppermute x3 -> x27, starting transfers between devices: 12.1 us -> 108 us  [the longest x12 54.3 us: along_y(): return lax.ppermute(array, ('col', 'yh'), pairs)]
    all_to_all x6 -> x0, starting transfers between devices: 48.9 us -> none  [the longest x4 36.1 us: on_device(): lax.all_to_all(for_sending(outgoing[turn]), 'srv', split_axis=0, concat_a...]
    pallas_call x0 -> x7, Pallas kernels: none -> 46.2 us  [attend(): pl.pallas_call(attend_kernel, grid=(1,), in_specs=query_specs + place_spe...]
    unnamed x12 -> x98, local copies, waits for them, and re-layouts: 2.4 us -> 46.3 us
    ppermute x3 -> x27, waiting for transfers between devices: 21.6 us -> 57 us  [the longest x12 42.9 us: along_z(): lax.ppermute(array, 'z', [(i, (i + by) % planes) for i in range(planes)])]
    another operation x6 -> x0, local copies, waits for them, and re-layouts: 11.6 us -> none
    reduce_sum x6 -> x0, other arithmetic: 8.91 us -> none  [the longest x4 8.73 us: one_head(): denominator = jnp.sum(weights, axis=2)]
  transfers between devices with their start and end apart: 9 -> 27, of which waited for: 8 -> 12; matrix products, arithmetic and copies ran while one was open for 20% -> 15% of each run, Pallas kernels for 0% -> 6%
where the time goes in v1:
time: 285 us; the launch traced here: 282 us
  starting transfers between devices  108 us (38%)
  waiting for transfers between devices  57 us (20%)
  local copies, waits for them, and re-layouts  53.6 us (19%)
  Pallas kernels  46.2 us (16%)
  matrix products  9.3 us (3%)
  other arithmetic  7.17 us (3%)
    ppermute x12, starting transfers between devices, along_y(): return lax.ppermute(array, ('col', 'yh'), pairs)  54.3 us
    unnamed x98, local copies, waits for them, and re-layouts  46.3 us
    pallas_call x7, Pallas kernels, attend(): pl.pallas_call(attend_kernel, grid=(1,), in_specs=query_specs + place_spe...  46.2 us
    ppermute x12, waiting for transfers between devices, along_z(): lax.ppermute(array, 'z', [(i, (i + by) % planes) for i in range(planes)])  42.9 us
    ppermute x12, starting transfers between devices, along_z(): lax.ppermute(array, 'z', [(i, (i + by) % planes) for i in range(planes)])  42.9 us
    dot_general x7, matrix products, pick(): jnp.dot(select, array, preferred_element_type=jnp.float32)  9.3 us
    ppermute x12, waiting for transfers between devices, along_y(): return lax.ppermute(array, ('col', 'yh'), pairs)  8.34 us
    ppermute x1, starting transfers between devices, window_of(): other = lax.ppermute(joined, 'yh', [(0, 1), (1, 0)])  7.73 us
  transfers between devices with their start and end apart: 27, of which 12 were waited for; matrix products, arithmetic and copies ran while one was open for 15% of the time, Pallas kernels for 6%

profile of v1, /device:TPU:6, one launch (start us, length us, event | category | flops | bytes accessed | tf_op | source)
XLA Modules:
  0.0 281.5 jit_solution(12147699329606134179)
XLA Ops:
  0.9 7.7 %collective-permute-start.3 = (bf16[128,512]{1,0:T(8,128)(2,1)S(1)}, bf16[128,512]{1,0:T(8,128)(2,1)S(1)}, u32[]{:S(2)}, u32[]{:S(2)}) collective-permute-start(bf16[128,512]{1,0:T(8,128)(2,1)S(1)} %pad_maximum_fusion.6), channel_id=1, source_target_pairs={{0,2},{2,0},{1,3},{3,1},{4,6},{6,4},{5,7},{7,5},{8,10},{10,8},{9,1... | collective-permute-start | bytes 393224 | tf_op jit(solution)/shard_map/ppermute | solution.py:139
  16.9 4.5 %collective-permute-start.1 = (bf16[96,4224]{1,0:T(8,128)(2,1)}, bf16[96,4224]{1,0:T(8,128)(2,1)S(1)}, u32[]{:S(2)}, u32[]{:S(2)}) collective-permute-start(bf16[96,4224]{1,0:T(8,128)(2,1)} %convolution_convert_fusion), channel_id=1, source_target_pairs={{0,50},{16,0},{32,16},{48,32},{2,48},{18,2},{34,18},{50,34},{1,51}... | collective-permute-start | bytes 2433032 | tf_op jit(solution)/shard_map/ppermute | solution.py:126
  33.4 5.7 %collective-permute-done.4 = bf16[128,512]{1,0:T(8,128)(2,1)S(1)} collective-permute-done((bf16[128,512]{1,0:T(8,128)(2,1)S(1)}, bf16[128,512]{1,0:T(8,128)(2,1)S(1)}, u32[]{:S(2)}, u32[]{:S(2)}) %collective-permute-start.4) | collective-permute-done | bytes 131104 | tf_op jit(solution)/shard_map/ppermute | solution.py:131
  39.1 6.0 %collective-permute-start.6 = (bf16[48,4224]{1,0:T(8,128)(2,1)}, bf16[48,4224]{1,0:T(8,128)(2,1)S(1)}, u32[]{:S(2)}, u32[]{:S(2)}) collective-permute-start(bf16[48,4224]{1,0:T(8,128)(2,1)} %convolution_convert_fusion.3), channel_id=1, source_target_pairs={{0,34},{16,50},{32,0},{48,16},{2,32},{18,48},{34,2},{50,18},{1,35}... | collective-permute-start | bytes 1216520 | tf_op jit(solution)/shard_map/ppermute | solution.py:126
  45.4 14.6 %collective-permute-start.7 = (bf16[648,512]{1,0:T(8,128)(2,1)S(1)}, bf16[648,512]{1,0:T(8,128)(2,1)}, u32[]{:S(2)}, u32[]{:S(2)}) collective-permute-start(bf16[648,512]{1,0:T(8,128)(2,1)S(1)} %constant_dynamic-update-slice_fusion.5.refs_8_), channel_id=1, source_target_pairs={{0,704},{64,0},{128,64},{192,128},{256,192},{320,256},{384,320},{4... | collective-permute-start | bytes 1990664 | tf_op jit(solution)/shard_map/ppermute | solution.py:119
  63.7 4.6 %shard_map.64 = (bf16[8,4096]{1,0:T(8,128)(2,1)}, bf16[8,4096]{1,0:T(8,128)(2,1)}, bf16[8,4096]{1,0:T(8,128)(2,1)}, bf16[8,4096]{1,0:T(8,128)(2,1)}) custom-call(bf16[96,4224]{1,0:T(8,128)(2,1)} %convolution_convert_fusion.2.refs_0_.refs_4_.refs_8_.refs_12_, bf16[96,4224]{1,0:T(8,128)(2,1)} %copy-done, bf16[96,4224]{1,0:T(8,128)(2,1)} %copy-done.1, ...), custom_call_target="tpu_custom_call" | custom-call | tf_op jit(solution)/shard_map/pallas_call | solution.py:108
  73.6 3.4 %collective-permute-done.8.refs_17_ = bf16[648,512]{1,0:T(8,128)(2,1)} collective-permute-done((bf16[648,512]{1,0:T(8,128)(2,1)S(1)}, bf16[648,512]{1,0:T(8,128)(2,1)}, u32[]{:S(2)}, u32[]{:S(2)}) %collective-permute-start.8) | collective-permute-done | bytes 663584 | tf_op jit(solution)/shard_map/ppermute | solution.py:119
  77.0 7.4 %shard_map.65 = (bf16[8,4096]{1,0:T(8,128)(2,1)}, bf16[8,4096]{1,0:T(8,128)(2,1)}, bf16[8,4096]{1,0:T(8,128)(2,1)}, bf16[8,4096]{1,0:T(8,128)(2,1)}, bf16[8,4096...) custom-call(bf16[96,4224]{1,0:T(8,128)(2,1)} %convolution_convert_fusion.2.refs_0_.re, ...), custom_call_target="tpu_custom_call" | custom-call | tf_op jit(solution)/shard_map/pallas_call | solution.py:108
  93.5 3.6 %collective-permute-start.10 = (bf16[648,512]{1,0:T(8,128)(2,1)}, bf16[648,512]{1,0:T(8,128)(2,1)}, u32[]{:S(2)}, u32[]{:S(2)}) collective-permute-start(bf16[648,512]{1,0:T(8,128)(2,1)} %collective-permute-done.8.refs_17_), channel_id=1, source_target_pairs={{0,64},{64,128},{128,192},{192,256},{256,320},{320,384},{384,448},... | collective-permute-start | bytes 1990664 | tf_op jit(solution)/shard_map/ppermute | solution.py:119
  100.1 6.1 %collective-permute-done.9.refs_16_ = bf16[648,512]{1,0:T(8,128)(2,1)S(1)} collective-permute-done((bf16[648,512]{1,0:T(8,128)(2,1)}, bf16[648,512]{1,0:T(8,128)(2,1)S(1)}, u32[]{:S(2)}, u32[]{:S(2)}) %collective-permute-start.9) | collective-permute-done | bytes 663584 | tf_op jit(solution)/shard_map/ppermute | solution.py:119
  106.2 4.1 %collective-permute-done.10.refs_17_ = bf16[648,512]{1,0:T(8,128)(2,1)} collective-permute-done((bf16[648,512]{1,0:T(8,128)(2,1)}, bf16[648,512]{1,0:T(8,128)(2,1)}, u32[]{:S(2)}, u32[]{:S(2)}) %collective-permute-start.10) | collective-permute-done | bytes 663584 | tf_op jit(solution)/shard_map/ppermute | solution.py:119
  110.3 7.4 %shard_map.66 = (bf16[8,4096]{1,0:T(8,128)(2,1)}, bf16[8,4096]{1,0:T(8,128)(2,1)}, bf16[8,4096]{1,0:T(8,128)(2,1)}, bf16[8,4096]{1,0:T(8,128)(2,1)}, bf16[8,4096...) custom-call(bf16[96,4224]{1,0:T(8,128)(2,1)} %convolution_convert_fusion.2.refs_0_.re, ...), custom_call_target="tpu_custom_call" | custom-call | tf_op jit(solution)/shard_map/pallas_call | solution.py:108
  126.3 3.9 %collective-permute-start.12 = (bf16[648,512]{1,0:T(8,128)(2,1)}, bf16[648,512]{1,0:T(8,128)(2,1)}, u32[]{:S(2)}, u32[]{:S(2)}) collective-permute-start(bf16[648,512]{1,0:T(8,128)(2,1)} %collective-permute-done.10.refs_17_), channel_id=1, source_target_pairs={{0,64},{64,128},{128,192},{192,256},{256,320},{320,384},{384,448},... | collective-permute-start | bytes 1990664 | tf_op jit(solution)/shard_map/ppermute | solution.py:119
  131.9 7.0 %collective-permute-done.11.refs_16_ = bf16[648,512]{1,0:T(8,128)(2,1)S(1)} collective-permute-done((bf16[648,512]{1,0:T(8,128)(2,1)}, bf16[648,512]{1,0:T(8,128)(2,1)S(1)}, u32[]{:S(2)}, u32[]{:S(2)}) %collective-permute-start.11) | collective-permute-done | bytes 663584 | tf_op jit(solution)/shard_map/ppermute | solution.py:119
  138.9 3.2 %collective-permute-done.12.refs_17_ = bf16[648,512]{1,0:T(8,128)(2,1)} collective-permute-done((bf16[648,512]{1,0:T(8,128)(2,1)}, bf16[648,512]{1,0:T(8,128)(2,1)}, u32[]{:S(2)}, u32[]{:S(2)}) %collective-permute-start.12) | collective-permute-done | bytes 663584 | tf_op jit(solution)/shard_map/ppermute | solution.py:119
  142.1 7.4 %shard_map.67 = (bf16[8,4096]{1,0:T(8,128)(2,1)}, bf16[8,4096]{1,0:T(8,128)(2,1)}, bf16[8,4096]{1,0:T(8,128)(2,1)}, bf16[8,4096]{1,0:T(8,128)(2,1)}, bf16[8,4096...) custom-call(bf16[96,4224]{1,0:T(8,128)(2,1)} %convolution_convert_fusion.2.refs_0_.re, ...), custom_call_target="tpu_custom_call" | custom-call | tf_op jit(solution)/shard_map/pallas_call | solution.py:108
  158.2 3.9 %collective-permute-start.14 = (bf16[648,512]{1,0:T(8,128)(2,1)}, bf16[648,512]{1,0:T(8,128)(2,1)S(1)}, u32[]{:S(2)}, u32[]{:S(2)}) collective-permute-start(bf16[648,512]{1,0:T(8,128)(2,1)} %collective-permute-done.12.refs_17_), channel_id=1, source_target_pairs={{0,64},{64,128},{128,192},{192,256},{256,320},{320,384},{384,448},... | collective-permute-start | bytes 1990664 | tf_op jit(solution)/shard_map/ppermute | solution.py:119
  163.8 6.2 %collective-permute-done.13.refs_16_ = bf16[648,512]{1,0:T(8,128)(2,1)} collective-permute-done((bf16[648,512]{1,0:T(8,128)(2,1)}, bf16[648,512]{1,0:T(8,128)(2,1)}, u32[]{:S(2)}, u32[]{:S(2)}) %collective-permute-start.13) | collective-permute-done | bytes 663584 | tf_op jit(solution)/shard_map/ppermute | solution.py:119
  170.1 3.0 %collective-permute-done.14.refs_17_ = bf16[648,512]{1,0:T(8,128)(2,1)S(1)} collective-permute-done((bf16[648,512]{1,0:T(8,128)(2,1)}, bf16[648,512]{1,0:T(8,128)(2,1)S(1)}, u32[]{:S(2)}, u32[]{:S(2)}) %collective-permute-start.14) | collective-permute-done | bytes 663584 | tf_op jit(solution)/shard_map/ppermute | solution.py:119
  174.0 7.4 %shard_map.68 = (bf16[8,4096]{1,0:T(8,128)(2,1)}, bf16[8,4096]{1,0:T(8,128)(2,1)}, bf16[8,4096]{1,0:T(8,128)(2,1)}, bf16[8,4096]{1,0:T(8,128)(2,1)}, bf16[8,4096...) custom-call(bf16[96,4224]{1,0:T(8,128)(2,1)} %convolution_convert_fusion.2.refs_0_.re, ...), custom_call_target="tpu_custom_call" | custom-call | tf_op jit(solution)/shard_map/pallas_call | solution.py:108
  182.2 5.8 %collective-permute-start.18 = (bf16[32,4096]{1,0:T(8,128)(2,1)S(1)}, bf16[32,4096]{1,0:T(8,128)(2,1)S(1)}, u32[]{:S(2)}, u32[]{:S(2)}) collective-permute-start(bf16[32,4096]{1,0:T(8,128)(2,1)S(1)} %pad_maximum_fusion.3), channel_id=1, source_target_pairs={{0,32},{16,48},{32,2},{48,18},{2,34},{18,50},{34,0},{50,16},{1,33}... | collective-permute-start | bytes 786440 | tf_op jit(solution)/shard_map/ppermute | solution.py:126
  189.5 5.9 %collective-permute-start.17 = (bf16[40,4096]{1,0:T(8,128)(2,1)}, bf16[40,4096]{1,0:T(8,128)(2,1)S(1)}, u32[]{:S(2)}, u32[]{:S(2)}) collective-permute-start(bf16[40,4096]{1,0:T(8,128)(2,1)} %constant_dynamic-update-slice_fusion.28), channel_id=1, source_target_pairs={{0,34},{16,50},{32,0},{48,16},{2,32},{18,48},{34,2},{50,18},{1,35}... | collective-permute-start | bytes 983048 | tf_op jit(solution)/shard_map/ppermute | solution.py:126
  198.4 9.7 %collective-permute-start.16 = (bf16[72,4096]{1,0:T(8,128)(2,1)}, bf16[72,4096]{1,0:T(8,128)(2,1)S(1)}, u32[]{:S(2)}, u32[]{:S(2)}) collective-permute-start(bf16[72,4096]{1,0:T(8,128)(2,1)} %constant_dynamic-update-slice_fusion.19), channel_id=1, source_target_pairs={{0,16},{16,32},{32,48},{48,2},{2,18},{18,34},{34,50},{50,0},{1,17}... | collective-permute-start | bytes 1769480 | tf_op jit(solution)/shard_map/ppermute | solution.py:126
  211.0 3.4 %collective-permute-start.15 = (bf16[72,4096]{1,0:T(8,128)(2,1)}, bf16[72,4096]{1,0:T(8,128)(2,1)S(1)}, u32[]{:S(2)}, u32[]{:S(2)}) collective-permute-start(bf16[72,4096]{1,0:T(8,128)(2,1)} %constant_dynamic-update-slice_fusion.10), channel_id=1, source_target_pairs={{0,50},{16,0},{32,16},{48,32},{2,48},{18,2},{34,18},{50,34},{1,51}... | collective-permute-start | bytes 1769480 | tf_op jit(solution)/shard_map/ppermute | solution.py:126
  217.9 6.0 %collective-permute-done.15 = bf16[72,4096]{1,0:T(8,128)(2,1)S(1)} collective-permute-done((bf16[72,4096]{1,0:T(8,128)(2,1)}, bf16[72,4096]{1,0:T(8,128)(2,1)S(1)}, u32[]{:S(2)}, u32[]{:S(2)}) %collective-permute-start.15) | collective-permute-done | bytes 589856 | tf_op jit(solution)/shard_map/ppermute | solution.py:126
  226.6 4.7 %collective-permute-done.19.refs_16_ = bf16[648,512]{1,0:T(8,128)(2,1)S(1)} collective-permute-done((bf16[648,512]{1,0:T(8,128)(2,1)}, bf16[648,512]{1,0:T(8,128)(2,1)S(1)}, u32[]{:S(2)}, u32[]{:S(2)}) %collective-permute-start.19) | collective-permute-done | bytes 663584 | tf_op jit(solution)/shard_map/ppermute | solution.py:119
  233.7 5.1 %collective-permute-done.20.refs_17_ = bf16[648,512]{1,0:T(8,128)(2,1)S(1)} collective-permute-done((bf16[648,512]{1,0:T(8,128)(2,1)}, bf16[648,512]{1,0:T(8,128)(2,1)S(1)}, u32[]{:S(2)}, u32[]{:S(2)}) %collective-permute-start.20) | collective-permute-done | bytes 663584 | tf_op jit(solution)/shard_map/ppermute | solution.py:119
  242.4 7.4 %shard_map.69 = (bf16[8,4096]{1,0:T(8,128)(2,1)}, bf16[8,4096]{1,0:T(8,128)(2,1)}, bf16[8,4096]{1,0:T(8,128)(2,1)}, bf16[8,4096]{1,0:T(8,128)(2,1)}, bf16[8,4096...) custom-call(bf16[96,4224]{1,0:T(8,128)(2,1)} %convolution_convert_fusion.2.refs_0_.re, ...), custom_call_target="tpu_custom_call" | custom-call | tf_op jit(solution)/shard_map/pallas_call | solution.py:108
  250.6 4.3 %collective-permute-start.25 = (bf16[8,4096]{1,0:T(8,128)(2,1)}, bf16[8,4096]{1,0:T(8,128)(2,1)}, u32[]{:S(2)}, u32[]{:S(2)}) collective-permute-start(bf16[8,4096]{1,0:T(8,128)(2,1)} %get-tuple-element.98), channel_id=1, source_target_pairs={{0,34},{16,50},{32,0},{48,16},{2,32},{18,48},{34,2},{50,18},{1,35}... | collective-permute-start | bytes 196616 | tf_op jit(solution)/shard_map/ppermute | solution.py:126
  257.7 4.6 %shard_map.70 = (bf16[8,4096]{1,0:T(8,128)(2,1)}, bf16[8,4096]{1,0:T(8,128)(2,1)}, bf16[8,4096]{1,0:T(8,128)(2,1)}, bf16[8,4096]{1,0:T(8,128)(2,1)}) custom-call(bf16[96,4224]{1,0:T(8,128)(2,1)} %convolution_convert_fusion.2.refs_0_.refs_4_.refs_8_.refs_12_, bf16[96,4224]{1,0:T(8,128)(2,1)} %copy-done, bf16[96,4224]{1,0:T(8,128)(2,1)} %copy-done.1, ...), custom_call_target="tpu_custom_call" | custom-call | tf_op jit(solution)/shard_map/pallas_call | solution.py:108
  266.6 3.1 %collective-permute-start.24 = (bf16[24,4096]{1,0:T(8,128)(2,1)S(1)}, bf16[24,4096]{1,0:T(8,128)(2,1)S(1)}, u32[]{:S(2)}, u32[]{:S(2)}) collective-permute-start(bf16[24,4096]{1,0:T(8,128)(2,1)S(1)} %pad_maximum_fusion.5), channel_id=1, source_target_pairs={{0,16},{16,32},{32,48},{48,2},{2,18},{18,34},{34,50},{50,0},{1,17}... | collective-permute-start | bytes 589832 | tf_op jit(solution)/shard_map/ppermute | solution.py:126
  270.6 4.6 %collective-permute-start.23 = (bf16[24,4096]{1,0:T(8,128)(2,1)S(1)}, bf16[24,4096]{1,0:T(8,128)(2,1)S(1)}, u32[]{:S(2)}, u32[]{:S(2)}) collective-permute-start(bf16[24,4096]{1,0:T(8,128)(2,1)S(1)} %pad_maximum_fusion.4), channel_id=1, source_target_pairs={{0,50},{16,0},{32,16},{48,32},{2,48},{18,2},{34,18},{50,34},{1,51}... | collective-permute-start | bytes 589832 | tf_op jit(solution)/shard_map/ppermute | solution.py:126
  (171 shorter events, 99.0 us)
Async XLA Ops:
  0.9 29.7 %collective-permute-start.3 = (bf16[128,512]{1,0:T(8,128)(2,1)S(1)}, bf16[128,512]{1,0:T(8,128)(2,1)S(1)}, u32[]{:S(2)}, u32[]{:S(2)}) collective-permute-start(bf16[128,512]{1,0:T(8,128)(2,1)S(1)} %pad_maximum_fusion.6), channel_id=1, source_target_pairs={{0,2},{2,0},{1,3},{3,1},{4,6},{6,4},{5,7},{7,5},{8,10},{10,8},{9,1... | collective-permute-start | bytes 393224 | tf_op jit(solution)/shard_map/ppermute | solution.py:139
  13.0 48.9 %collective-permute-start = (bf16[96,4224]{1,0:T(8,128)(2,1)}, bf16[96,4224]{1,0:T(8,128)(2,1)S(1)}, u32[]{:S(2)}, u32[]{:S(2)}) collective-permute-start(bf16[96,4224]{1,0:T(8,128)(2,1)} %convolution_convert_fusion.1), channel_id=1, source_target_pairs={{0,16},{16,32},{32,48},{48,2},{2,18},{18,34},{34,50},{50,0},{1,17}... | collective-permute-start | bytes 2433032 | tf_op jit(solution)/shard_map/ppermute | solution.py:126
  16.9 45.0 %collective-permute-start.1 = (bf16[96,4224]{1,0:T(8,128)(2,1)}, bf16[96,4224]{1,0:T(8,128)(2,1)S(1)}, u32[]{:S(2)}, u32[]{:S(2)}) collective-permute-start(bf16[96,4224]{1,0:T(8,128)(2,1)} %convolution_convert_fusion), channel_id=1, source_target_pairs={{0,50},{16,0},{32,16},{48,32},{2,48},{18,2},{34,18},{50,34},{1,51}... | collective-permute-start | bytes 2433032 | tf_op jit(solution)/shard_map/ppermute | solution.py:126
  22.4 37.5 %collective-permute-start.2 = (bf16[48,4224]{1,0:T(8,128)(2,1)}, bf16[48,4224]{1,0:T(8,128)(2,1)S(1)}, u32[]{:S(2)}, u32[]{:S(2)}) collective-permute-start(bf16[48,4224]{1,0:T(8,128)(2,1)} %convolution_convert_fusion.4), channel_id=1, source_target_pairs={{0,32},{16,48},{32,2},{48,18},{2,34},{18,50},{34,0},{50,16},{1,33}... | collective-permute-start | bytes 1216520 | tf_op jit(solution)/shard_map/ppermute | solution.py:126
  30.7 8.4 %collective-permute-start.4 = (bf16[128,512]{1,0:T(8,128)(2,1)S(1)}, bf16[128,512]{1,0:T(8,128)(2,1)S(1)}, u32[]{:S(2)}, u32[]{:S(2)}) collective-permute-start(bf16[128,512]{1,0:T(8,128)(2,1)S(1)} %get-tuple-element.108), channel_id=1, source_target_pairs={{0,8},{4,12},{1,9},{5,13},{2,10},{6,14},{3,11},{7,15},{16,24},{20,... | collective-permute-start | bytes 393224 | tf_op jit(solution)/shard_map/ppermute | solution.py:131
  32.1 13.1 %collective-permute-start.5 = (bf16[256,512]{1,0:T(8,128)(2,1)S(1)}, bf16[256,512]{1,0:T(8,128)(2,1)S(1)}, u32[]{:S(2)}, u32[]{:S(2)}) collective-permute-start(bf16[256,512]{1,0:T(8,128)(2,1)S(1)} %pad_maximum_fusion.2), channel_id=1, source_target_pairs={{0,4},{4,8},{8,12},{1,5},{5,9},{9,13},{2,6},{6,10},{10,14},{3,7},{... | collective-permute-start | bytes 786440 | tf_op jit(solution)/shard_map/ppermute | solution.py:131
  39.1 34.5 %collective-permute-start.6 = (bf16[48,4224]{1,0:T(8,128)(2,1)}, bf16[48,4224]{1,0:T(8,128)(2,1)S(1)}, u32[]{:S(2)}, u32[]{:S(2)}) collective-permute-start(bf16[48,4224]{1,0:T(8,128)(2,1)} %convolution_convert_fusion.3), channel_id=1, source_target_pairs={{0,34},{16,50},{32,0},{48,16},{2,32},{18,48},{34,2},{50,18},{1,35}... | collective-permute-start | bytes 1216520 | tf_op jit(solution)/shard_map/ppermute | solution.py:126
  45.4 28.2 %collective-permute-start.7 = (bf16[648,512]{1,0:T(8,128)(2,1)S(1)}, bf16[648,512]{1,0:T(8,128)(2,1)}, u32[]{:S(2)}, u32[]{:S(2)}) collective-permute-start(bf16[648,512]{1,0:T(8,128)(2,1)S(1)} %constant_dynamic-update-slice_fusion.5.refs_8_), channel_id=1, source_target_pairs={{0,704},{64,0},{128,64},{192,128},{256,192},{320,256},{384,320},{4... | collective-permute-start | bytes 1990664 | tf_op jit(solution)/shard_map/ppermute | solution.py:119
  60.0 17.0 %collective-permute-start.8 = (bf16[648,512]{1,0:T(8,128)(2,1)S(1)}, bf16[648,512]{1,0:T(8,128)(2,1)}, u32[]{:S(2)}, u32[]{:S(2)}) collective-permute-start(bf16[648,512]{1,0:T(8,128)(2,1)S(1)} %constant_dynamic-update-slice_fusion.5.refs_8_), channel_id=1, source_target_pairs={{0,64},{64,128},{128,192},{192,256},{256,320},{320,384},{384,448},... | collective-permute-start | bytes 1990664 | tf_op jit(solution)/shard_map/ppermute | solution.py:119
  91.1 15.0 %collective-permute-start.9 = (bf16[648,512]{1,0:T(8,128)(2,1)}, bf16[648,512]{1,0:T(8,128)(2,1)S(1)}, u32[]{:S(2)}, u32[]{:S(2)}) collective-permute-start(bf16[648,512]{1,0:T(8,128)(2,1)} %collective-permute-done.7.refs_16_), channel_id=1, source_target_pairs={{0,704},{64,0},{128,64},{192,128},{256,192},{320,256},{384,320},{4... | collective-permute-start | bytes 1990664 | tf_op jit(solution)/shard_map/ppermute | solution.py:119
  93.5 16.7 %collective-permute-start.10 = (bf16[648,512]{1,0:T(8,128)(2,1)}, bf16[648,512]{1,0:T(8,128)(2,1)}, u32[]{:S(2)}, u32[]{:S(2)}) collective-permute-start(bf16[648,512]{1,0:T(8,128)(2,1)} %collective-permute-done.8.refs_17_), channel_id=1, source_target_pairs={{0,64},{64,128},{128,192},{192,256},{256,320},{320,384},{384,448},... | collective-permute-start | bytes 1990664 | tf_op jit(solution)/shard_map/ppermute | solution.py:119
  100.1 30.1 %copy-start.5 = (bf16[288,4096]{1,0:T(8,128)(2,1)S(1)}, bf16[288,4096]{1,0:T(8,128)(2,1)}, u32[]{:S(2)}) copy-start(bf16[288,4096]{1,0:T(8,128)(2,1)} %constant_dynamic-update-slice_fusion.43) | copy-start | bytes 7077892
  124.4 14.5 %collective-permute-start.11 = (bf16[648,512]{1,0:T(8,128)(2,1)}, bf16[648,512]{1,0:T(8,128)(2,1)S(1)}, u32[]{:S(2)}, u32[]{:S(2)}) collective-permute-start(bf16[648,512]{1,0:T(8,128)(2,1)} %copy-done.10), channel_id=1, source_target_pairs={{0,704},{64,0},{128,64},{192,128},{256,192},{320,256},{384,320},{4... | collective-permute-start | bytes 1990664 | tf_op jit(solution)/shard_map/ppermute | solution.py:119
  126.3 15.9 %collective-permute-start.12 = (bf16[648,512]{1,0:T(8,128)(2,1)}, bf16[648,512]{1,0:T(8,128)(2,1)}, u32[]{:S(2)}, u32[]{:S(2)}) collective-permute-start(bf16[648,512]{1,0:T(8,128)(2,1)} %collective-permute-done.10.refs_17_), channel_id=1, source_target_pairs={{0,64},{64,128},{128,192},{192,256},{256,320},{320,384},{384,448},... | collective-permute-start | bytes 1990664 | tf_op jit(solution)/shard_map/ppermute | solution.py:119
  156.3 13.8 %collective-permute-start.13 = (bf16[648,512]{1,0:T(8,128)(2,1)}, bf16[648,512]{1,0:T(8,128)(2,1)}, u32[]{:S(2)}, u32[]{:S(2)}) collective-permute-start(bf16[648,512]{1,0:T(8,128)(2,1)} %copy-done.11), channel_id=1, source_target_pairs={{0,704},{64,0},{128,64},{192,128},{256,192},{320,256},{384,320},{4... | collective-permute-start | bytes 1990664 | tf_op jit(solution)/shard_map/ppermute | solution.py:119
  158.2 14.9 %collective-permute-start.14 = (bf16[648,512]{1,0:T(8,128)(2,1)}, bf16[648,512]{1,0:T(8,128)(2,1)S(1)}, u32[]{:S(2)}, u32[]{:S(2)}) collective-permute-start(bf16[648,512]{1,0:T(8,128)(2,1)} %collective-permute-done.12.refs_17_), channel_id=1, source_target_pairs={{0,64},{64,128},{128,192},{192,256},{256,320},{320,384},{384,448},... | collective-permute-start | bytes 1990664 | tf_op jit(solution)/shard_map/ppermute | solution.py:119
  163.8 17.5 %copy-start.17 = (bf16[8,4096]{1,0:T(8,128)(2,1)S(1)}, bf16[8,4096]{1,0:T(8,128)(2,1)}, u32[]{:S(2)}) copy-start(bf16[8,4096]{1,0:T(8,128)(2,1)} %get-tuple-element.85) | copy-start | bytes 196612
  163.8 17.6 %copy-start.18 = (bf16[8,4096]{1,0:T(8,128)(2,1)S(1)}, bf16[8,4096]{1,0:T(8,128)(2,1)}, u32[]{:S(2)}) copy-start(bf16[8,4096]{1,0:T(8,128)(2,1)} %get-tuple-element.86) | copy-start | bytes 196612
  163.8 17.6 %copy-start.19 = (bf16[8,4096]{1,0:T(8,128)(2,1)S(1)}, bf16[8,4096]{1,0:T(8,128)(2,1)}, u32[]{:S(2)}) copy-start(bf16[8,4096]{1,0:T(8,128)(2,1)} %get-tuple-element.87) | copy-start | bytes 196612
  182.2 44.3 %collective-permute-start.18 = (bf16[32,4096]{1,0:T(8,128)(2,1)S(1)}, bf16[32,4096]{1,0:T(8,128)(2,1)S(1)}, u32[]{:S(2)}, u32[]{:S(2)}) collective-permute-start(bf16[32,4096]{1,0:T(8,128)(2,1)S(1)} %pad_maximum_fusion.3), channel_id=1, source_target_pairs={{0,32},{16,48},{32,2},{48,18},{2,34},{18,50},{34,0},{50,16},{1,33}... | collective-permute-start | bytes 786440 | tf_op jit(solution)/shard_map/ppermute | solution.py:126
  189.5 37.0 %collective-permute-start.17 = (bf16[40,4096]{1,0:T(8,128)(2,1)}, bf16[40,4096]{1,0:T(8,128)(2,1)S(1)}, u32[]{:S(2)}, u32[]{:S(2)}) collective-permute-start(bf16[40,4096]{1,0:T(8,128)(2,1)} %constant_dynamic-update-slice_fusion.28), channel_id=1, source_target_pairs={{0,34},{16,50},{32,0},{48,16},{2,32},{18,48},{34,2},{50,18},{1,35}... | collective-permute-start | bytes 983048 | tf_op jit(solution)/shard_map/ppermute | solution.py:126
  198.4 28.1 %collective-permute-start.16 = (bf16[72,4096]{1,0:T(8,128)(2,1)}, bf16[72,4096]{1,0:T(8,128)(2,1)S(1)}, u32[]{:S(2)}, u32[]{:S(2)}) collective-permute-start(bf16[72,4096]{1,0:T(8,128)(2,1)} %constant_dynamic-update-slice_fusion.19), channel_id=1, source_target_pairs={{0,16},{16,32},{32,48},{48,2},{2,18},{18,34},{34,50},{50,0},{1,17}... | collective-permute-start | bytes 1769480 | tf_op jit(solution)/shard_map/ppermute | solution.py:126
  211.0 13.0 %collective-permute-start.15 = (bf16[72,4096]{1,0:T(8,128)(2,1)}, bf16[72,4096]{1,0:T(8,128)(2,1)S(1)}, u32[]{:S(2)}, u32[]{:S(2)}) collective-permute-start(bf16[72,4096]{1,0:T(8,128)(2,1)} %constant_dynamic-update-slice_fusion.10), channel_id=1, source_target_pairs={{0,50},{16,0},{32,16},{48,32},{2,48},{18,2},{34,18},{50,34},{1,51}... | collective-permute-start | bytes 1769480 | tf_op jit(solution)/shard_map/ppermute | solution.py:126
  216.0 15.2 %collective-permute-start.19 = (bf16[648,512]{1,0:T(8,128)(2,1)}, bf16[648,512]{1,0:T(8,128)(2,1)S(1)}, u32[]{:S(2)}, u32[]{:S(2)}) collective-permute-start(bf16[648,512]{1,0:T(8,128)(2,1)} %collective-permute-done.13.refs_16_), channel_id=1, source_target_pairs={{0,704},{64,0},{128,64},{192,128},{256,192},{320,256},{384,320},{4... | collective-permute-start | bytes 1990664 | tf_op jit(solution)/shard_map/ppermute | solution.py:119
  223.9 14.9 %collective-permute-start.20 = (bf16[648,512]{1,0:T(8,128)(2,1)}, bf16[648,512]{1,0:T(8,128)(2,1)S(1)}, u32[]{:S(2)}, u32[]{:S(2)}) collective-permute-start(bf16[648,512]{1,0:T(8,128)(2,1)} %copy-done.9), channel_id=1, source_target_pairs={{0,64},{64,128},{128,192},{192,256},{256,320},{320,384},{384,448},... | collective-permute-start | bytes 1990664 | tf_op jit(solution)/shard_map/ppermute | solution.py:119
  231.3 24.5 %collective-permute-start.21 = (bf16[648,256]{1,0:T(8,128)(2,1)S(1)}, bf16[648,256]{1,0:T(8,128)(2,1)}, u32[]{:S(2)}, u32[]{:S(2)}) collective-permute-start(bf16[648,256]{1,0:T(8,128)(2,1)S(1)} %slice.83), channel_id=1, source_target_pairs={{0,704},{64,0},{128,64},{192,128},{256,192},{320,256},{384,320},{4... | collective-permute-start | bytes 995336 | tf_op jit(solution)/shard_map/ppermute | solution.py:119
  240.4 15.3 %collective-permute-start.22 = (bf16[648,256]{1,0:T(8,128)(2,1)}, bf16[648,256]{1,0:T(8,128)(2,1)}, u32[]{:S(2)}, u32[]{:S(2)}) collective-permute-start(bf16[648,256]{1,0:T(8,128)(2,1)} %slice.84), channel_id=1, source_target_pairs={{0,64},{64,128},{128,192},{192,256},{256,320},{320,384},{384,448},... | collective-permute-start | bytes 995336 | tf_op jit(solution)/shard_map/ppermute | solution.py:119
  250.6 27.8 %collective-permute-start.25 = (bf16[8,4096]{1,0:T(8,128)(2,1)}, bf16[8,4096]{1,0:T(8,128)(2,1)}, u32[]{:S(2)}, u32[]{:S(2)}) collective-permute-start(bf16[8,4096]{1,0:T(8,128)(2,1)} %get-tuple-element.98), channel_id=1, source_target_pairs={{0,34},{16,50},{32,0},{48,16},{2,32},{18,48},{34,2},{50,18},{1,35}... | collective-permute-start | bytes 196616 | tf_op jit(solution)/shard_map/ppermute | solution.py:126
  262.4 16.9 %copy-start.21 = (bf16[96,128]{1,0:T(8,128)(2,1)S(1)}, bf16[96,128]{1,0:T(8,128)(2,1)}, u32[]{:S(2)}) copy-start(bf16[96,128]{1,0:T(8,128)(2,1)} %copy-done.20) | copy-start | bytes 73732
  263.2 16.0 %collective-permute-start.26 = (bf16[16,4096]{1,0:T(8,128)(2,1)S(1)}, bf16[16,4096]{1,0:T(8,128)(2,1)S(1)}, u32[]{:S(2)}, u32[]{:S(2)}) collective-permute-start(bf16[16,4096]{1,0:T(8,128)(2,1)S(1)} %pad_maximum_fusion.7), channel_id=1, source_target_pairs={{0,32},{16,48},{32,2},{48,18},{2,34},{18,50},{34,0},{50,16},{1,33}... | collective-permute-start | bytes 393224 | tf_op jit(solution)/shard_map/ppermute | solution.py:126
  266.6 11.8 %collective-permute-start.24 = (bf16[24,4096]{1,0:T(8,128)(2,1)S(1)}, bf16[24,4096]{1,0:T(8,128)(2,1)S(1)}, u32[]{:S(2)}, u32[]{:S(2)}) collective-permute-start(bf16[24,4096]{1,0:T(8,128)(2,1)S(1)} %pad_maximum_fusion.5), channel_id=1, source_target_pairs={{0,16},{16,32},{32,48},{48,2},{2,18},{18,34},{34,50},{50,0},{1,17}... | collective-permute-start | bytes 589832 | tf_op jit(solution)/shard_map/ppermute | solution.py:126
  270.6 7.8 %collective-permute-start.23 = (bf16[24,4096]{1,0:T(8,128)(2,1)S(1)}, bf16[24,4096]{1,0:T(8,128)(2,1)S(1)}, u32[]{:S(2)}, u32[]{:S(2)}) collective-permute-start(bf16[24,4096]{1,0:T(8,128)(2,1)S(1)} %pad_maximum_fusion.4), channel_id=1, source_target_pairs={{0,50},{16,0},{32,16},{48,32},{2,48},{18,2},{34,18},{50,34},{1,51}... | collective-permute-start | bytes 589832 | tf_op jit(solution)/shard_map/ppermute | solution.py:126
  (19 other events, 124.8 us)

commit v2 on v1

--- a/solution.py
+++ b/solution.py
@@ -4,6 +4,7 @@
 import jax.numpy as jnp
 from jax import lax
 from jax.experimental import pallas as pl
+from jax.experimental.pallas import tpu as pltpu
 from jax.sharding import Mesh
 from jax.sharding import PartitionSpec as P
 
@@ -16,29 +17,43 @@
 GROUPS = QH // KVH
 DOCS = 8
 BEHIND = 3
+PARTS = 1
 SCALE = math.log2(math.e) / math.sqrt(HD)
 
 
-def attend_kernel(*refs):
-    servers = len(refs) // (3 * COLS + 1)
-    windows = refs[2 * COLS * servers : (2 * COLS + 1) * servers]
-    for s in range(servers):
-        serve(
-            refs[COLS * s : COLS * (s + 1)],
-            refs[COLS * (servers + s) : COLS * (servers + s + 1)],
-            windows[s],
-            refs[(2 * COLS + 1) * servers + COLS * s : (2 * COLS + 1) * servers + COLS * (s + 1)],
-        )
-
-
-def serve(query_refs, place_refs, window_ref, out_refs):
+def attend_kernel(base, count, groups_out, aliased, *refs):
+    query_refs, place_refs = refs[:5], refs[5:10]
+    windows = refs[10 : 10 + count]
+    out_refs = refs[10 + count + aliased : 10 + count + aliased + len(groups_out)]
+    held, far, sems = refs[10 + count + aliased + len(groups_out) :]
+    at = pl.program_id(0)
+
+    def fetch(k):
+        return pltpu.make_async_copy(windows[k], held.at[k], sems.at[k])
+
+    @pl.when(at == 0)
+    def _():
+        for k in range(count):
+            fetch(k).start()
+
+    for k in range(count):
+        pl.when(at == k)(lambda k=k: fetch(k).wait())
+
+    even = ((base + at) & 1) == 0
+    window = held.at[at]
+    span = held.shape[1] - DOCS
     slots = ROUNDS * R
     rows = COLS * slots
-    span = window_ref.shape[0] - DOCS
-    marks = window_ref[span:, : 2 * HD].astype(jnp.float32)
+
+    def load(refs_of, lanes):
+        last = jnp.where(even, refs_of[3][:, lanes], refs_of[4][:, lanes])
+        return [ref[:, lanes].astype(jnp.float32) for ref in refs_of[:3]] + [
+            last.astype(jnp.float32)
+        ]
+
+    marks = window[span:, : 2 * HD].astype(jnp.float32)
     starts = marks[:, :HD] * 16.0 + marks[:, HD:]
-    place = jnp.concatenate([ref[...].astype(jnp.float32) for ref in place_refs], axis=0)
-    place = place + float(BEHIND * HD)
+    place = jnp.concatenate(load(place_refs, slice(0, HD)), axis=0) + float(BEHIND * HD)
     first = jnp.zeros_like(place)
     for doc in range(DOCS):
         start = jnp.broadcast_to(starts[doc : doc + 1, :], place.shape)
@@ -50,20 +65,15 @@
         allowed = (key_pos >= first) & (key_pos <= place)
         bias.append(jnp.where(allowed, 0.0, -1e30))
     bias = jnp.concatenate(bias, axis=1)
-    parts = 4
-    per_part = GROUPS // parts
+    per_part = GROUPS // PARTS
     for head in range(KVH):
-        keys = window_ref[:span, 2 * head * HD : (2 * head + 1) * HD]
-        values = window_ref[:span, (2 * head + 1) * HD : (2 * head + 2) * HD]
-        for part in range(parts):
+        keys = window[:span, 2 * head * HD : (2 * head + 1) * HD]
+        values = window[:span, (2 * head + 1) * HD : (2 * head + 2) * HD]
+        for part in range(PARTS):
             first_head = head * GROUPS + part * per_part
             heads = range(first_head, first_head + per_part)
             query = jnp.concatenate(
-                [
-                    ref[:, h * HD : (h + 1) * HD].astype(jnp.float32)
-                    for h in heads
-                    for ref in query_refs
-                ],
+                [piece for h in heads for piece in load(query_refs, slice(h * HD, (h + 1) * HD))],
                 axis=0,
             ).astype(jnp.bfloat16)
             scores = lax.dot_general(
@@ -83,35 +93,84 @@
             )
             for n, h in enumerate(heads):
                 result = weighted[n * rows : (n + 1) * rows] * inverse[n]
-                for c, ref in enumerate(out_refs):
-                    ref[:, h * HD : (h + 1) * HD] = result[c * slots : (c + 1) * slots].astype(
-                        jnp.bfloat16
-                    )
-
-
-def sources_of(order):
-    far = 3 if order % 2 == 0 else 4
-    return ((0, order), (1, order), (2, order), (far, order // 2))
-
-
-def attend(arrived, windows, orders):
+                for c in range(COLS):
+                    piece = result[c * slots : (c + 1) * slots].astype(jnp.bfloat16)
+                    ref = far if c == COLS - 1 else out_refs[c]
+                    ref[:, h * HD : (h + 1) * HD] = piece
+    for ref, group in zip(out_refs[3:], groups_out[3:]):
+
+        @pl.when(even if group == 3 else jnp.logical_not(even))
+        def _(ref=ref):
+            ref[...] = far[...]
+
+
+def far_orders(group, orders):
+    return [order for order in orders if order % 2 == group - 3]
+
+
+def attend(arrived, windows, orders, batch, buffers):
     slots = ROUNDS * R
     width = QH * HD
-    queries, query_specs, place_specs, out_shape = [], [], [], []
-    for order in orders:
-        for group, at in sources_of(order):
-            queries.append(arrived[group])
-            query_specs.append(pl.BlockSpec((slots, width), lambda i, at=at: (at, 0)))
-            place_specs.append(pl.BlockSpec((slots, HD), lambda i, at=at: (at, width // HD)))
-            out_shape.append(jax.ShapeDtypeStruct((slots, width), jnp.bfloat16))
-    window_spec = pl.BlockSpec(windows[0].shape, lambda i: (0, 0))
+    base, count = orders[0], len(orders)
+    spots = [lambda i: base + i] * 3 + [lambda i: (base + i) >> 1] * 2
+    groups_out = [0, 1, 2] + [group for group in (3, 4) if far_orders(group, orders)]
+    out_specs, out_shape = [], []
+    for group in groups_out:
+        if group < 3:
+            total = len(batch)
+            spot = lambda i: base - batch[0] + i
+        else:
+            mine = far_orders(group, batch)
+            total, lowest = len(mine), mine[0] // 2
+            shift = 1 if group == 3 else 0
+            spot = lambda i, t=total, l=lowest, s=shift: jnp.clip(((base + i + s) >> 1) - l, 0, t - 1)
+        out_specs.append(pl.BlockSpec((slots, width), lambda i, spot=spot: (spot(i), 0)))
+        out_shape.append(jax.ShapeDtypeStruct((total * slots, width), jnp.bfloat16))
+    kept = [group for group in groups_out if group in buffers]
+    anywhere = pl.BlockSpec(memory_space=pl.ANY)
+    outs = pl.pallas_call(
+        lambda *refs: attend_kernel(base, count, groups_out, len(kept), *refs),
+        grid=(count,),
+        in_specs=[pl.BlockSpec((slots, width), lambda i, spot=spot: (spot(i), 0)) for spot in spots]
+        + [
+            pl.BlockSpec((slots, HD), lambda i, spot=spot: (spot(i), width // HD))
+            for spot in spots
+        ]
+        + [anywhere] * (count + len(kept)),
+        out_specs=out_specs,
+        out_shape=out_shape,
+        scratch_shapes=[
+            pltpu.VMEM((count,) + windows[0].shape, jnp.bfloat16),
+            pltpu.VMEM((slots, width), jnp.bfloat16),
+            pltpu.SemaphoreType.DMA((count,)),
+        ],
+        input_output_aliases={10 + count + n: groups_out.index(g) for n, g in enumerate(kept)},
+        compiler_params=pltpu.CompilerParams(dimension_semantics=("arbitrary",)),
+    )(*arrived, *arrived, *windows, *[buffers[group] for group in kept])
+    return {**buffers, **dict(zip(groups_out, outs))}
+
+
+def collect_kernel(select_ref, *refs):
+    backs, out_ref = refs[:-1], refs[-1]
+    joined = jnp.concatenate([ref[...].astype(jnp.float32) for ref in backs], axis=0)
+    out_ref[...] = jnp.dot(
+        select_ref[...], joined.astype(jnp.bfloat16), preferred_element_type=jnp.float32
+    ).astype(jnp.bfloat16)
+
+
+def collect(select, backs):
+    rows, width = select.shape[0], backs[0].shape[1]
+    chunk = width // 4
     return pl.pallas_call(
-        attend_kernel,
-        grid=(1,),
-        in_specs=query_specs + place_specs + [window_spec] * len(windows),
-        out_specs=[pl.BlockSpec((slots, width), lambda i: (0, 0))] * len(out_shape),
-        out_shape=out_shape,
-    )(*queries, *queries, *windows)
+        collect_kernel,
+        grid=(4,),
+        in_specs=[pl.BlockSpec(select.shape, lambda i: (0, 0))]
+        + [pl.BlockSpec((back.shape[0], chunk), lambda i: (0, i)) for back in backs],
+        out_specs=pl.BlockSpec((rows, chunk), lambda i: (0, i)),
+        out_shape=jax.ShapeDtypeStruct((rows, width), jnp.bfloat16),
+        compiler_params=pltpu.CompilerParams(dimension_semantics=("arbitrary",)),
+        name="collect",
+    )(select, *backs)
 
 
 def along_z(array, by):
@@ -191,43 +250,38 @@
         sending = pick(select, payload)
         arrived.append(along_y(sending, by) if by else sending)
 
-    served = {}
-
-    def serve_orders(windows, orders):
-        outs = attend(arrived, windows, orders)
-        for n, number in enumerate(orders):
-            for c, (group, at) in enumerate(sources_of(number)):
-                served[group, at] = outs[COLS * n + c]
-
-    serve_orders([window], [0])
+    windows = [window]
     ahead_window, behind_window = window, window
     width = window.shape[1] // 2
-    gathered = None
-
-    def give_back(orders):
-        backs, chosen = [], []
+    backs, chosen = [], []
+
+    def serve(orders, batch, buffers):
+        return attend(arrived, [windows[order] for order in orders], orders, batch, buffers)
+
+    def give_back(buffers, batch):
         for number, (_, _, by) in enumerate(groups):
-            ats = [at for o in orders for group, at in sources_of(o) if group == number]
-            if not ats:
-                continue
-            outgoing = jnp.concatenate([served[number, at] for at in ats], axis=0)
-            back = along_y(outgoing, -by) if by else outgoing
-            backs.append(back)
-            chosen.append(selects[number][ats[0] * slots : (ats[-1] + 1) * slots])
-        return pick(jnp.concatenate(chosen, axis=0).T, jnp.concatenate(backs, axis=0))
-
-    for step in range(1, reach):
+            orders = batch if number < 3 else far_orders(number, batch)
+            lowest = orders[0] if number < 3 else orders[0] // 2
+            backs.append(along_y(buffers[number], -by) if by else buffers[number])
+            chosen.append(selects[number][lowest * slots : (lowest + len(orders)) * slots])
+
+    early = list(range(planes - 3))
+    late = list(range(planes - 3, planes))
+    for _ in range(1, reach):
         ahead_window = along_z(ahead_window, -1)
         behind_window = along_z(behind_window, 1)
-        serve_orders([ahead_window, behind_window], [2 * step - 1, 2 * step])
-        if step == reach - 2:
-            gathered = give_back(list(range(2 * step + 1)))
+        windows += [ahead_window, behind_window]
     last_left = along_z(ahead_window[:, :width], -1)
     last_right = along_z(behind_window[:, width:], 1)
-    last = jnp.concatenate([last_left, last_right], axis=1)
-    serve_orders([last], [planes - 1])
-    rest = give_back(list(range(0 if gathered is None else 2 * (reach - 2) + 1, planes)))
-    return (rest if gathered is None else gathered + rest)[None, None]
+    windows.append(jnp.concatenate([last_left, last_right], axis=1))
+
+    buffers = serve(early[:-2], early, {})
+    buffers = serve(early[-2:], early, buffers)
+    give_back(buffers, early)
+    buffers = serve(late[:2], late, {})
+    buffers = serve(late[2:], late, buffers)
+    give_back(buffers, late)
+    return collect(jnp.concatenate(chosen, axis=0).T, backs)[None, None]
 
 
 def solution(mesh):

time: 285 us -> 236 us (0.83)
  the two profiles are of different devices: /device:TPU:6 before, /device:TPU:4 now
where the time goes in v2:
time: 236 us; the launch traced here: 235 us
  starting transfers between devices  112 us (47%)
  waiting for transfers between devices  73.8 us (31%)
  Pallas kernels  34.7 us (15%)
  local copies, waits for them, and re-layouts  7.13 us (3%)
  other arithmetic  3.23 us (1%)
  matrix products  3.18 us (1%)
    ppermute x12, starting transfers between devices, along_z(): lax.ppermute(array, 'z', [(i, (i + by) % planes) for i in range(planes)])  51.5 us
    ppermute x12, starting transfers between devices, along_y(): return lax.ppermute(array, ('col', 'yh'), pairs)  48.4 us
    ppermute x12, waiting for transfers between devices, along_z(): lax.ppermute(array, 'z', [(i, (i + by) % planes) for i in range(planes)])  41.5 us
    pallas_call x4, Pallas kernels, attend(): pl.pallas_call(lambda *refs: attend_kernel(base, count, groups_out, len(k...  30.1 us
    ppermute x12, waiting for transfers between devices, along_y(): return lax.ppermute(array, ('col', 'yh'), pairs)  20.6 us
    ppermute x2, waiting for transfers between devices, along_x(): return lax.ppermute(array, 'x', [(i, i + by) for i in range(peers - by)])  9.01 us
    ppermute x1, starting transfers between devices, window_of(): other = lax.ppermute(joined, 'yh', [(0, 1), (1, 0)])  7.73 us
  transfers between devices with their start and end apart: 27, of which 10 were waited for; matrix products, arithmetic and copies ran while one was open for 4% of the time, Pallas kernels for 13%

profile of v2, /device:TPU:4, one launch (start us, length us, event | category | flops | bytes accessed | tf_op | source)
XLA Modules:
  0.0 234.9 jit_solution(1456614723678007794)
XLA Ops:
  0.8 7.7 %collective-permute-start.4 = (bf16[128,512]{1,0:T(8,128)(2,1)S(1)}, bf16[128,512]{1,0:T(8,128)(2,1)S(1)}, u32[]{:S(2)}, u32[]{:S(2)}) collective-permute-start(bf16[128,512]{1,0:T(8,128)(2,1)S(1)} %pad_maximum_fusion.3), channel_id=1, source_target_pairs={{0,2},{2,0},{1,3},{3,1},{4,6},{6,4},{5,7},{7,5},{8,10},{10,8},{9,1... | collective-permute-start | bytes 393224 | tf_op jit(solution)/shard_map/ppermute | solution.py:198
  9.5 2.6 %collective-permute-done.4 = bf16[128,512]{1,0:T(8,128)(2,1)S(1)} collective-permute-done((bf16[128,512]{1,0:T(8,128)(2,1)S(1)}, bf16[128,512]{1,0:T(8,128)(2,1)S(1)}, u32[]{:S(2)}, u32[]{:S(2)}) %collective-permute-start.4) | collective-permute-done | bytes 131104 | tf_op jit(solution)/shard_map/ppermute | solution.py:198
  13.7 3.1 %collective-permute-start.6 = (bf16[256,512]{1,0:T(8,128)(2,1)S(1)}, bf16[256,512]{1,0:T(8,128)(2,1)S(1)}, u32[]{:S(2)}, u32[]{:S(2)}) collective-permute-start(bf16[256,512]{1,0:T(8,128)(2,1)S(1)} %pad_maximum_fusion.2), channel_id=1, source_target_pairs={{0,4},{4,8},{8,12},{1,5},{5,9},{9,13},{2,6},{6,10},{10,14},{3,7},{... | collective-permute-start | bytes 786440 | tf_op jit(solution)/shard_map/ppermute | solution.py:190
  16.8 8.8 %collective-permute-done.5 = bf16[128,512]{1,0:T(8,128)(2,1)S(1)} collective-permute-done((bf16[128,512]{1,0:T(8,128)(2,1)S(1)}, bf16[128,512]{1,0:T(8,128)(2,1)S(1)}, u32[]{:S(2)}, u32[]{:S(2)}) %collective-permute-start.5) | collective-permute-done | bytes 131104 | tf_op jit(solution)/shard_map/ppermute | solution.py:190
  26.1 4.3 %collective-permute-start.11 = (bf16[648,512]{1,0:T(8,128)(2,1)S(1)}, bf16[648,512]{1,0:T(8,128)(2,1)S(1)}, u32[]{:S(2)}, u32[]{:S(2)}) collective-permute-start(bf16[648,512]{1,0:T(8,128)(2,1)S(1)} %constant_dynamic-update-slice_fusion.refs_10_), channel_id=1, source_target_pairs={{0,64},{64,128},{128,192},{192,256},{256,320},{320,384},{384,448},... | collective-permute-start | bytes 1990664 | tf_op jit(solution)/shard_map/ppermute | solution.py:178
  30.4 12.2 %collective-permute-start.7 = (bf16[648,512]{1,0:T(8,128)(2,1)S(1)}, bf16[648,512]{1,0:T(8,128)(2,1)S(1)}, u32[]{:S(2)}, u32[]{:S(2)}) collective-permute-start(bf16[648,512]{1,0:T(8,128)(2,1)S(1)} %constant_dynamic-update-slice_fusion.refs_10_), channel_id=1, source_target_pairs={{0,704},{64,0},{128,64},{192,128},{256,192},{320,256},{384,320},{4... | collective-permute-start | bytes 1990664 | tf_op jit(solution)/shard_map/ppermute | solution.py:178
  42.6 12.4 %collective-permute-done.11.refs_12_ = bf16[648,512]{1,0:T(8,128)(2,1)S(1)} collective-permute-done((bf16[648,512]{1,0:T(8,128)(2,1)S(1)}, bf16[648,512]{1,0:T(8,128)(2,1)S(1)}, u32[]{:S(2)}, u32[]{:S(2)}) %collective-permute-start.11) | collective-permute-done | bytes 663584 | tf_op jit(solution)/shard_map/ppermute | solution.py:178
  56.9 5.1 %collective-permute-start.8 = (bf16[648,512]{1,0:T(8,128)(2,1)S(1)}, bf16[648,512]{1,0:T(8,128)(2,1)}, u32[]{:S(2)}, u32[]{:S(2)}) collective-permute-start(bf16[648,512]{1,0:T(8,128)(2,1)S(1)} %collective-permute-done.7.refs_11_), channel_id=1, source_target_pairs={{0,704},{64,0},{128,64},{192,128},{256,192},{320,256},{384,320},{4... | collective-permute-start | bytes 1990664 | tf_op jit(solution)/shard_map/ppermute | solution.py:178
  62.2 11.3 %collective-permute-done.12.refs_14_ = bf16[648,512]{1,0:T(8,128)(2,1)S(1)} collective-permute-done((bf16[648,512]{1,0:T(8,128)(2,1)S(1)}, bf16[648,512]{1,0:T(8,128)(2,1)S(1)}, u32[]{:S(2)}, u32[]{:S(2)}) %collective-permute-start.12) | collective-permute-done | bytes 663584 | tf_op jit(solution)/shard_map/ppermute | solution.py:178
  75.7 5.1 %collective-permute-start.9 = (bf16[648,512]{1,0:T(8,128)(2,1)}, bf16[648,512]{1,0:T(8,128)(2,1)S(1)}, u32[]{:S(2)}, u32[]{:S(2)}) collective-permute-start(bf16[648,512]{1,0:T(8,128)(2,1)} %collective-permute-done.8.refs_13_), channel_id=1, source_target_pairs={{0,704},{64,0},{128,64},{192,128},{256,192},{320,256},{384,320},{4... | collective-permute-start | bytes 1990664 | tf_op jit(solution)/shard_map/ppermute | solution.py:178
  80.9 10.5 %collective-permute-done.13.refs_16_ = bf16[648,512]{1,0:T(8,128)(2,1)} collective-permute-done((bf16[648,512]{1,0:T(8,128)(2,1)S(1)}, bf16[648,512]{1,0:T(8,128)(2,1)}, u32[]{:S(2)}, u32[]{:S(2)}) %collective-permute-start.13) | collective-permute-done | bytes 663584 | tf_op jit(solution)/shard_map/ppermute | solution.py:178
  93.3 5.2 %collective-permute-start.10 = (bf16[648,512]{1,0:T(8,128)(2,1)S(1)}, bf16[648,512]{1,0:T(8,128)(2,1)}, u32[]{:S(2)}, u32[]{:S(2)}) collective-permute-start(bf16[648,512]{1,0:T(8,128)(2,1)S(1)} %collective-permute-done.9.refs_15_), channel_id=1, source_target_pairs={{0,704},{64,0},{128,64},{192,128},{256,192},{320,256},{384,320},{4... | collective-permute-start | bytes 1990664 | tf_op jit(solution)/shard_map/ppermute | solution.py:178
  99.1 1.9 collective-permute-start
  101.0 7.4 %collective-permute-done.14.refs_11_ = bf16[648,512]{1,0:T(8,128)(2,1)S(1)} collective-permute-done((bf16[648,512]{1,0:T(8,128)(2,1)}, bf16[648,512]{1,0:T(8,128)(2,1)S(1)}, u32[]{:S(2)}, u32[]{:S(2)}) %collective-permute-start.14) | collective-permute-done | bytes 663584 | tf_op jit(solution)/shard_map/ppermute | solution.py:178
  110.9 10.5 %collective-permute-start.1 = (bf16[96,4224]{1,0:T(8,128)(2,1)S(1)}, bf16[96,4224]{1,0:T(8,128)(2,1)S(1)}, u32[]{:S(2)}, u32[]{:S(2)}) collective-permute-start(bf16[96,4224]{1,0:T(8,128)(2,1)S(1)} %convolution_convert_fusion), channel_id=1, source_target_pairs={{0,50},{16,0},{32,16},{48,32},{2,48},{18,2},{34,18},{50,34},{1,51}... | collective-permute-start | bytes 2433032 | tf_op jit(solution)/shard_map/ppermute | solution.py:185
  121.8 2.5 %collective-permute-start.2 = (bf16[48,4224]{1,0:T(8,128)(2,1)S(1)}, bf16[48,4224]{1,0:T(8,128)(2,1)S(1)}, u32[]{:S(2)}, u32[]{:S(2)}) collective-permute-start(bf16[48,4224]{1,0:T(8,128)(2,1)S(1)} %convolution_convert_fusion.4), channel_id=1, source_target_pairs={{0,32},{16,48},{32,2},{48,18},{2,34},{18,50},{34,0},{50,16},{1,33}... | collective-permute-start | bytes 1216520 | tf_op jit(solution)/shard_map/ppermute | solution.py:185
  124.3 5.1 %collective-permute-start.19 = (bf16[648,512]{1,0:T(8,128)(2,1)}, bf16[648,512]{1,0:T(8,128)(2,1)}, u32[]{:S(2)}, u32[]{:S(2)}) collective-permute-start(bf16[648,512]{1,0:T(8,128)(2,1)} %collective-permute-done.10.refs_10_), channel_id=1, source_target_pairs={{0,704},{64,0},{128,64},{192,128},{256,192},{320,256},{384,320},{4... | collective-permute-start | bytes 1990664 | tf_op jit(solution)/shard_map/ppermute | solution.py:178
  129.9 5.4 %collective-permute-start.3 = (bf16[48,4224]{1,0:T(8,128)(2,1)S(1)}, bf16[48,4224]{1,0:T(8,128)(2,1)S(1)}, u32[]{:S(2)}, u32[]{:S(2)}) collective-permute-start(bf16[48,4224]{1,0:T(8,128)(2,1)S(1)} %convolution_convert_fusion.3), channel_id=1, source_target_pairs={{0,34},{16,50},{32,0},{48,16},{2,32},{18,48},{34,2},{50,18},{1,35}... | collective-permute-start | bytes 1216520 | tf_op jit(solution)/shard_map/ppermute | solution.py:185
  136.1 6.6 %collective-permute-done.2.refs_3_.refs_8_ = bf16[48,4224]{1,0:T(8,128)(2,1)S(1)} collective-permute-done((bf16[48,4224]{1,0:T(8,128)(2,1)S(1)}, bf16[48,4224]{1,0:T(8,128)(2,1)S(1)}, u32[]{:S(2)}, u32[]{:S(2)}) %collective-permute-start.2) | collective-permute-done | bytes 405536 | tf_op jit(solution)/shard_map/ppermute | solution.py:185
  146.0 6.9 %collective-permute-done.3.refs_4_.refs_9_ = bf16[48,4224]{1,0:T(8,128)(2,1)S(1)} collective-permute-done((bf16[48,4224]{1,0:T(8,128)(2,1)S(1)}, bf16[48,4224]{1,0:T(8,128)(2,1)S(1)}, u32[]{:S(2)}, u32[]{:S(2)}) %collective-permute-start.3) | collective-permute-done | bytes 405536 | tf_op jit(solution)/shard_map/ppermute | solution.py:185
  154.8 14.0 %shard_map.64 = (bf16[72,4096]{1,0:T(8,128)(2,1)}, bf16[72,4096]{1,0:T(8,128)(2,1)}, bf16[72,4096]{1,0:T(8,128)(2,1)}, bf16[40,4096]{1,0:T(8,128)(2,1)}, bf16[32,4096]{1,0:T(8,128)(2,1)}) custom-call(bf16[96,4224]{1,0:T(8,128)(2,1)} %convolution_convert_fusion.2.refs_0_.refs_5_, bf16[96,4224]{1,0:T(8,128)(2,1)} %copy-done, bf16[96,4224]{1,0:T(8,128)(2,1)} %copy-done.1, ...), custom_call_target="tpu_custom_call" | custom-call | tf_op jit(solution)/shard_map/pallas_call | solution.py:131
  168.8 6.0 %shard_map.65 = (bf16[72,4096]{1,0:T(8,128)(2,1)}, bf16[72,4096]{1,0:T(8,128)(2,1)}, bf16[72,4096]{1,0:T(8,128)(2,1)}, bf16[40,4096]{1,0:T(8,128)(2,1)}, bf16[32,4096]{1,0:T(8,128)(2,1)}) custom-call(bf16[96,4224]{1,0:T(8,128)(2,1)} %convolution_convert_fusion.2.refs_0_.refs_5_, ...), custom_call_target="tpu_custom_call", output_to_operand_aliasing={{0}: (12, {}), {1}: (13, {}), {2}: (14, {}), {3}: (15, {}),... | custom-call | tf_op jit(solution)/shard_map/pallas_call | solution.py:131
  174.8 1.9 collective-permute-start.15
  177.7 4.9 %collective-permute-start.20 = (bf16[648,256]{1,0:T(8,128)(2,1)S(1)}, bf16[648,256]{1,0:T(8,128)(2,1)S(1)}, u32[]{:S(2)}, u32[]{:S(2)}) collective-permute-start(bf16[648,256]{1,0:T(8,128)(2,1)S(1)} %slice.83), channel_id=1, source_target_pairs={{0,704},{64,0},{128,64},{192,128},{256,192},{320,256},{384,320},{4... | collective-permute-start | bytes 995336 | tf_op jit(solution)/shard_map/ppermute | solution.py:178
  182.6 5.1 %collective-permute-start.16 = (bf16[72,4096]{1,0:T(8,128)(2,1)}, bf16[72,4096]{1,0:T(8,128)(2,1)S(1)}, u32[]{:S(2)}, u32[]{:S(2)}) collective-permute-start(bf16[72,4096]{1,0:T(8,128)(2,1)} %get-tuple-element.31), channel_id=1, source_target_pairs={{0,16},{16,32},{32,48},{48,2},{2,18},{18,34},{34,50},{50,0},{1,17}... | collective-permute-start | bytes 1769480 | tf_op jit(solution)/shard_map/ppermute | solution.py:185
  187.7 5.3 %collective-permute-start.17 = (bf16[40,4096]{1,0:T(8,128)(2,1)}, bf16[40,4096]{1,0:T(8,128)(2,1)S(1)}, u32[]{:S(2)}, u32[]{:S(2)}) collective-permute-start(bf16[40,4096]{1,0:T(8,128)(2,1)} %get-tuple-element.32), channel_id=1, source_target_pairs={{0,34},{16,50},{32,0},{48,16},{2,32},{18,48},{34,2},{50,18},{1,35}... | collective-permute-start | bytes 983048 | tf_op jit(solution)/shard_map/ppermute | solution.py:185
  195.1 6.0 %shard_map.66 = (bf16[24,4096]{1,0:T(8,128)(2,1)}, bf16[24,4096]{1,0:T(8,128)(2,1)}, bf16[24,4096]{1,0:T(8,128)(2,1)}, bf16[8,4096]{1,0:T(8,128)(2,1)}, bf16[16,4096]{1,0:T(8,128)(2,1)}) custom-call(bf16[96,4224]{1,0:T(8,128)(2,1)} %convolution_convert_fusion.2.refs_0_.refs_5_, bf16[96,4224]{1,0:T(8,128)(2,1)} %copy-done, bf16[96,4224]{1,0:T(8,128)(2,1)} %copy-done.1, ...), custom_call_target="tpu_custom_call" | custom-call | tf_op jit(solution)/shard_map/pallas_call | solution.py:131
  201.0 6.0 %collective-permute-start.25 = (bf16[8,4096]{1,0:T(8,128)(2,1)}, bf16[8,4096]{1,0:T(8,128)(2,1)S(1)}, u32[]{:S(2)}, u32[]{:S(2)}) collective-permute-start(bf16[8,4096]{1,0:T(8,128)(2,1)} %get-tuple-element.41), channel_id=1, source_target_pairs={{0,34},{16,50},{32,0},{48,16},{2,32},{18,48},{34,2},{50,18},{1,35}... | collective-permute-start | bytes 196616 | tf_op jit(solution)/shard_map/ppermute | solution.py:185
  209.0 4.3 %shard_map.67 = (bf16[24,4096]{1,0:T(8,128)(2,1)}, bf16[24,4096]{1,0:T(8,128)(2,1)}, bf16[24,4096]{1,0:T(8,128)(2,1)}, bf16[16,4096]{1,0:T(8,128)(2,1)}) custom-call(bf16[96,4224]{1,0:T(8,128)(2,1)} %convolution_convert_fusion.2.refs_0_.refs_5_, ...), custom_call_target="tpu_custom_call", output_to_operand_aliasing={{0}: (11, {}), {1}: (12, {}), {2}: (13, {}), {3}: (14, {})} | custom-call | tf_op jit(solution)/shard_map/pallas_call | solution.py:131
  215.2 3.9 %collective-permute-start.24 = (bf16[24,4096]{1,0:T(8,128)(2,1)}, bf16[24,4096]{1,0:T(8,128)(2,1)S(1)}, u32[]{:S(2)}, u32[]{:S(2)}) collective-permute-start(bf16[24,4096]{1,0:T(8,128)(2,1)} %get-tuple-element.40), channel_id=1, source_target_pairs={{0,16},{16,32},{32,48},{48,2},{2,18},{18,34},{34,50},{50,0},{1,17}... | collective-permute-start | bytes 589832 | tf_op jit(solution)/shard_map/ppermute | solution.py:185
  222.4 7.1 %collective-permute-done.26.refs_9_ = bf16[16,4096]{1,0:T(8,128)(2,1)S(1)} collective-permute-done((bf16[16,4096]{1,0:T(8,128)(2,1)}, bf16[16,4096]{1,0:T(8,128)(2,1)S(1)}, u32[]{:S(2)}, u32[]{:S(2)}) %collective-permute-start.26) | collective-permute-done | bytes 131104 | tf_op jit(solution)/shard_map/ppermute | solution.py:185
  230.3 4.6 %collect.1 = bf16[128,4096]{1,0:T(8,128)(2,1)} custom-call(bf16[128,384]{1,0:T(8,128)(2,1)} %bitcast.22, bf16[72,4096]{1,0:T(8,128)(2,1)} %get-tuple-element.29.refs_0_, bf16[72,4096]{1,0:T(8,128)(2,1)} %copy-done.12, bf16[72,4096]{1,0:T(8,128)(2,1)} %copy-done.13, bf16[40,4096]{1,0:T(8,128)(2,1)} %copy-done.14, bf16[32,4096]{1,0:T(8,128)(2,1)} %copy-done.15, ...), custom_call_target="tpu_custom_call" | custom-call | tf_op jit(solution)/shard_map/collect/pallas_call | solution.py:164
  (112 shorter events, 30.5 us)
Async XLA Ops:
  0.8 11.3 %collective-permute-start.4 = (bf16[128,512]{1,0:T(8,128)(2,1)S(1)}, bf16[128,512]{1,0:T(8,128)(2,1)S(1)}, u32[]{:S(2)}, u32[]{:S(2)}) collective-permute-start(bf16[128,512]{1,0:T(8,128)(2,1)S(1)} %pad_maximum_fusion.3), channel_id=1, source_target_pairs={{0,2},{2,0},{1,3},{3,1},{4,6},{6,4},{5,7},{7,5},{8,10},{10,8},{9,1... | collective-permute-start | bytes 393224 | tf_op jit(solution)/shard_map/ppermute | solution.py:198
  12.2 49.8 %copy-start.20 = (s32[1,1,32]{2,1,0:T(1,128)S(1)}, s32[1,1,32]{2,1,0:T(1,128)}, u32[]{:S(2)}) copy-start(s32[1,1,32]{2,1,0:T(1,128)} %param.7) | copy-start | bytes 388
  12.2 63.2 %copy-start.21 = (s32[1,1,32]{2,1,0:T(1,128)S(1)}, s32[1,1,32]{2,1,0:T(1,128)}, u32[]{:S(2)}) copy-start(s32[1,1,32]{2,1,0:T(1,128)} %param.8) | copy-start | bytes 388
  12.2 86.4 %copy-start.4 = (bf16[1,1,128,4096]{3,2,1,0:T(8,128)(2,1)S(1)}, bf16[1,1,128,4096]{3,2,1,0:T(8,128)(2,1)}, u32[]{:S(2)}) copy-start(bf16[1,1,128,4096]{3,2,1,0:T(8,128)(2,1)} %param.6) | copy-start | bytes 3145732
  12.3 13.4 %collective-permute-start.5 = (bf16[128,512]{1,0:T(8,128)(2,1)S(1)}, bf16[128,512]{1,0:T(8,128)(2,1)S(1)}, u32[]{:S(2)}, u32[]{:S(2)}) collective-permute-start(bf16[128,512]{1,0:T(8,128)(2,1)S(1)} %get-tuple-element.50), channel_id=1, source_target_pairs={{0,8},{4,12},{1,9},{5,13},{2,10},{6,14},{3,11},{7,15},{16,24},{20,... | collective-permute-start | bytes 393224 | tf_op jit(solution)/shard_map/ppermute | solution.py:190
  13.7 12.2 %collective-permute-start.6 = (bf16[256,512]{1,0:T(8,128)(2,1)S(1)}, bf16[256,512]{1,0:T(8,128)(2,1)S(1)}, u32[]{:S(2)}, u32[]{:S(2)}) collective-permute-start(bf16[256,512]{1,0:T(8,128)(2,1)S(1)} %pad_maximum_fusion.2), channel_id=1, source_target_pairs={{0,4},{4,8},{8,12},{1,5},{5,9},{9,13},{2,6},{6,10},{10,14},{3,7},{... | collective-permute-start | bytes 786440 | tf_op jit(solution)/shard_map/ppermute | solution.py:190
  26.1 28.9 %collective-permute-start.11 = (bf16[648,512]{1,0:T(8,128)(2,1)S(1)}, bf16[648,512]{1,0:T(8,128)(2,1)S(1)}, u32[]{:S(2)}, u32[]{:S(2)}) collective-permute-start(bf16[648,512]{1,0:T(8,128)(2,1)S(1)} %constant_dynamic-update-slice_fusion.refs_10_), channel_id=1, source_target_pairs={{0,64},{64,128},{128,192},{192,256},{256,320},{320,384},{384,448},... | collective-permute-start | bytes 1990664 | tf_op jit(solution)/shard_map/ppermute | solution.py:178
  30.4 26.5 %collective-permute-start.7 = (bf16[648,512]{1,0:T(8,128)(2,1)S(1)}, bf16[648,512]{1,0:T(8,128)(2,1)S(1)}, u32[]{:S(2)}, u32[]{:S(2)}) collective-permute-start(bf16[648,512]{1,0:T(8,128)(2,1)S(1)} %constant_dynamic-update-slice_fusion.refs_10_), channel_id=1, source_target_pairs={{0,704},{64,0},{128,64},{192,128},{256,192},{320,256},{384,320},{4... | collective-permute-start | bytes 1990664 | tf_op jit(solution)/shard_map/ppermute | solution.py:178
  55.0 43.6 %copy-start.8 = (bf16[648,512]{1,0:T(8,128)(2,1)}, bf16[648,512]{1,0:T(8,128)(2,1)S(1)}, u32[]{:S(2)}) copy-start(bf16[648,512]{1,0:T(8,128)(2,1)S(1)} %collective-permute-done.11.refs_12_) | copy-start | bytes 1990660
  55.0 18.6 %collective-permute-start.12 = (bf16[648,512]{1,0:T(8,128)(2,1)S(1)}, bf16[648,512]{1,0:T(8,128)(2,1)S(1)}, u32[]{:S(2)}, u32[]{:S(2)}) collective-permute-start(bf16[648,512]{1,0:T(8,128)(2,1)S(1)} %collective-permute-done.11.refs_12_), channel_id=1, source_target_pairs={{0,64},{64,128},{128,192},{192,256},{256,320},{320,384},{384,448},... | collective-permute-start | bytes 1990664 | tf_op jit(solution)/shard_map/ppermute | solution.py:178
  56.9 41.7 %copy-start.9 = (bf16[648,512]{1,0:T(8,128)(2,1)}, bf16[648,512]{1,0:T(8,128)(2,1)S(1)}, u32[]{:S(2)}) copy-start(bf16[648,512]{1,0:T(8,128)(2,1)S(1)} %collective-permute-done.7.refs_11_) | copy-start | bytes 1990660
  56.9 18.8 %collective-permute-start.8 = (bf16[648,512]{1,0:T(8,128)(2,1)S(1)}, bf16[648,512]{1,0:T(8,128)(2,1)}, u32[]{:S(2)}, u32[]{:S(2)}) collective-permute-start(bf16[648,512]{1,0:T(8,128)(2,1)S(1)} %collective-permute-done.7.refs_11_), channel_id=1, source_target_pairs={{0,704},{64,0},{128,64},{192,128},{256,192},{320,256},{384,320},{4... | collective-permute-start | bytes 1990664 | tf_op jit(solution)/shard_map/ppermute | solution.py:178
  73.5 17.8 %collective-permute-start.13 = (bf16[648,512]{1,0:T(8,128)(2,1)S(1)}, bf16[648,512]{1,0:T(8,128)(2,1)}, u32[]{:S(2)}, u32[]{:S(2)}) collective-permute-start(bf16[648,512]{1,0:T(8,128)(2,1)S(1)} %collective-permute-done.12.refs_14_), channel_id=1, source_target_pairs={{0,64},{64,128},{128,192},{192,256},{256,320},{320,384},{384,448},... | collective-permute-start | bytes 1990664 | tf_op jit(solution)/shard_map/ppermute | solution.py:178
  75.7 17.6 %collective-permute-start.9 = (bf16[648,512]{1,0:T(8,128)(2,1)}, bf16[648,512]{1,0:T(8,128)(2,1)S(1)}, u32[]{:S(2)}, u32[]{:S(2)}) collective-permute-start(bf16[648,512]{1,0:T(8,128)(2,1)} %collective-permute-done.8.refs_13_), channel_id=1, source_target_pairs={{0,704},{64,0},{128,64},{192,128},{256,192},{320,256},{384,320},{4... | collective-permute-start | bytes 1990664 | tf_op jit(solution)/shard_map/ppermute | solution.py:178
  91.4 17.1 %collective-permute-start.14 = (bf16[648,512]{1,0:T(8,128)(2,1)}, bf16[648,512]{1,0:T(8,128)(2,1)S(1)}, u32[]{:S(2)}, u32[]{:S(2)}) collective-permute-start(bf16[648,512]{1,0:T(8,128)(2,1)} %collective-permute-done.13.refs_16_), channel_id=1, source_target_pairs={{0,64},{64,128},{128,192},{192,256},{256,320},{320,384},{384,448},... | collective-permute-start | bytes 1990664 | tf_op jit(solution)/shard_map/ppermute | solution.py:178
  93.3 31.0 %collective-permute-start.10 = (bf16[648,512]{1,0:T(8,128)(2,1)S(1)}, bf16[648,512]{1,0:T(8,128)(2,1)}, u32[]{:S(2)}, u32[]{:S(2)}) collective-permute-start(bf16[648,512]{1,0:T(8,128)(2,1)S(1)} %collective-permute-done.9.refs_15_), channel_id=1, source_target_pairs={{0,704},{64,0},{128,64},{192,128},{256,192},{320,256},{384,320},{4... | collective-permute-start | bytes 1990664 | tf_op jit(solution)/shard_map/ppermute | solution.py:178
  99.1 53.8 %collective-permute-start = (bf16[96,4224]{1,0:T(8,128)(2,1)S(1)}, bf16[96,4224]{1,0:T(8,128)(2,1)S(1)}, u32[]{:S(2)}, u32[]{:S(2)}) collective-permute-start(bf16[96,4224]{1,0:T(8,128)(2,1)S(1)} %convolution_convert_fusion.1), channel_id=1, source_target_pairs={{0,16},{16,32},{32,48},{48,2},{2,18},{18,34},{34,50},{50,0},{1,17}... | collective-permute-start | bytes 2433032 | tf_op jit(solution)/shard_map/ppermute | solution.py:185
  108.4 21.4 %collective-permute-start.21 = (bf16[648,512]{1,0:T(8,128)(2,1)S(1)}, bf16[648,512]{1,0:T(8,128)(2,1)S(1)}, u32[]{:S(2)}, u32[]{:S(2)}) collective-permute-start(bf16[648,512]{1,0:T(8,128)(2,1)S(1)} %collective-permute-done.14.refs_11_), channel_id=1, source_target_pairs={{0,64},{64,128},{128,192},{192,256},{256,320},{320,384},{384,448},... | collective-permute-start | bytes 1990664 | tf_op jit(solution)/shard_map/ppermute | solution.py:178
  110.9 42.0 %collective-permute-start.1 = (bf16[96,4224]{1,0:T(8,128)(2,1)S(1)}, bf16[96,4224]{1,0:T(8,128)(2,1)S(1)}, u32[]{:S(2)}, u32[]{:S(2)}) collective-permute-start(bf16[96,4224]{1,0:T(8,128)(2,1)S(1)} %convolution_convert_fusion), channel_id=1, source_target_pairs={{0,50},{16,0},{32,16},{48,32},{2,48},{18,2},{34,18},{50,34},{1,51}... | collective-permute-start | bytes 2433032 | tf_op jit(solution)/shard_map/ppermute | solution.py:185
  121.8 21.0 %collective-permute-start.2 = (bf16[48,4224]{1,0:T(8,128)(2,1)S(1)}, bf16[48,4224]{1,0:T(8,128)(2,1)S(1)}, u32[]{:S(2)}, u32[]{:S(2)}) collective-permute-start(bf16[48,4224]{1,0:T(8,128)(2,1)S(1)} %convolution_convert_fusion.4), channel_id=1, source_target_pairs={{0,32},{16,48},{32,2},{48,18},{2,34},{18,50},{34,0},{50,16},{1,33}... | collective-permute-start | bytes 1216520 | tf_op jit(solution)/shard_map/ppermute | solution.py:185
  124.3 52.4 %collective-permute-start.19 = (bf16[648,512]{1,0:T(8,128)(2,1)}, bf16[648,512]{1,0:T(8,128)(2,1)}, u32[]{:S(2)}, u32[]{:S(2)}) collective-permute-start(bf16[648,512]{1,0:T(8,128)(2,1)} %collective-permute-done.10.refs_10_), channel_id=1, source_target_pairs={{0,704},{64,0},{128,64},{192,128},{256,192},{320,256},{384,320},{4... | collective-permute-start | bytes 1990664 | tf_op jit(solution)/shard_map/ppermute | solution.py:178
  129.9 23.0 %collective-permute-start.3 = (bf16[48,4224]{1,0:T(8,128)(2,1)S(1)}, bf16[48,4224]{1,0:T(8,128)(2,1)S(1)}, u32[]{:S(2)}, u32[]{:S(2)}) collective-permute-start(bf16[48,4224]{1,0:T(8,128)(2,1)S(1)} %convolution_convert_fusion.3), channel_id=1, source_target_pairs={{0,34},{16,50},{32,0},{48,16},{2,32},{18,48},{34,2},{50,18},{1,35}... | collective-permute-start | bytes 1216520 | tf_op jit(solution)/shard_map/ppermute | solution.py:185
  142.7 50.3 %collective-permute-start.22 = (bf16[648,256]{1,0:T(8,128)(2,1)}, bf16[648,256]{1,0:T(8,128)(2,1)}, u32[]{:S(2)}, u32[]{:S(2)}) collective-permute-start(bf16[648,256]{1,0:T(8,128)(2,1)} %slice.84), channel_id=1, source_target_pairs={{0,64},{64,128},{128,192},{192,256},{256,320},{320,384},{384,448},... | collective-permute-start | bytes 995336 | tf_op jit(solution)/shard_map/ppermute | solution.py:178
  174.8 44.4 %collective-permute-start.15 = (bf16[72,4096]{1,0:T(8,128)(2,1)}, bf16[72,4096]{1,0:T(8,128)(2,1)S(1)}, u32[]{:S(2)}, u32[]{:S(2)}) collective-permute-start(bf16[72,4096]{1,0:T(8,128)(2,1)} %get-tuple-element.30), channel_id=1, source_target_pairs={{0,50},{16,0},{32,16},{48,32},{2,48},{18,2},{34,18},{50,34},{1,51}... | collective-permute-start | bytes 1769480 | tf_op jit(solution)/shard_map/ppermute | solution.py:185
  177.7 23.3 %collective-permute-start.20 = (bf16[648,256]{1,0:T(8,128)(2,1)S(1)}, bf16[648,256]{1,0:T(8,128)(2,1)S(1)}, u32[]{:S(2)}, u32[]{:S(2)}) collective-permute-start(bf16[648,256]{1,0:T(8,128)(2,1)S(1)} %slice.83), channel_id=1, source_target_pairs={{0,704},{64,0},{128,64},{192,128},{256,192},{320,256},{384,320},{4... | collective-permute-start | bytes 995336 | tf_op jit(solution)/shard_map/ppermute | solution.py:178
  182.6 39.9 %collective-permute-start.16 = (bf16[72,4096]{1,0:T(8,128)(2,1)}, bf16[72,4096]{1,0:T(8,128)(2,1)S(1)}, u32[]{:S(2)}, u32[]{:S(2)}) collective-permute-start(bf16[72,4096]{1,0:T(8,128)(2,1)} %get-tuple-element.31), channel_id=1, source_target_pairs={{0,16},{16,32},{32,48},{48,2},{2,18},{18,34},{34,50},{50,0},{1,17}... | collective-permute-start | bytes 1769480 | tf_op jit(solution)/shard_map/ppermute | solution.py:185
  187.7 27.5 %collective-permute-start.17 = (bf16[40,4096]{1,0:T(8,128)(2,1)}, bf16[40,4096]{1,0:T(8,128)(2,1)S(1)}, u32[]{:S(2)}, u32[]{:S(2)}) collective-permute-start(bf16[40,4096]{1,0:T(8,128)(2,1)} %get-tuple-element.32), channel_id=1, source_target_pairs={{0,34},{16,50},{32,0},{48,16},{2,32},{18,48},{34,2},{50,18},{1,35}... | collective-permute-start | bytes 983048 | tf_op jit(solution)/shard_map/ppermute | solution.py:185
  193.0 20.2 %collective-permute-start.18 = (bf16[32,4096]{1,0:T(8,128)(2,1)}, bf16[32,4096]{1,0:T(8,128)(2,1)S(1)}, u32[]{:S(2)}, u32[]{:S(2)}) collective-permute-start(bf16[32,4096]{1,0:T(8,128)(2,1)} %get-tuple-element.33), channel_id=1, source_target_pairs={{0,32},{16,48},{32,2},{48,18},{2,34},{18,50},{34,0},{50,16},{1,33}... | collective-permute-start | bytes 786440 | tf_op jit(solution)/shard_map/ppermute | solution.py:185
  201.0 21.4 %collective-permute-start.25 = (bf16[8,4096]{1,0:T(8,128)(2,1)}, bf16[8,4096]{1,0:T(8,128)(2,1)S(1)}, u32[]{:S(2)}, u32[]{:S(2)}) collective-permute-start(bf16[8,4096]{1,0:T(8,128)(2,1)} %get-tuple-element.41), channel_id=1, source_target_pairs={{0,34},{16,50},{32,0},{48,16},{2,32},{18,48},{34,2},{50,18},{1,35}... | collective-permute-start | bytes 196616 | tf_op jit(solution)/shard_map/ppermute | solution.py:185
  213.3 16.3 %collective-permute-start.23 = (bf16[24,4096]{1,0:T(8,128)(2,1)}, bf16[24,4096]{1,0:T(8,128)(2,1)S(1)}, u32[]{:S(2)}, u32[]{:S(2)}) collective-permute-start(bf16[24,4096]{1,0:T(8,128)(2,1)} %get-tuple-element.39), channel_id=1, source_target_pairs={{0,50},{16,0},{32,16},{48,32},{2,48},{18,2},{34,18},{50,34},{1,51}... | collective-permute-start | bytes 589832 | tf_op jit(solution)/shard_map/ppermute | solution.py:185
  215.2 14.3 %collective-permute-start.24 = (bf16[24,4096]{1,0:T(8,128)(2,1)}, bf16[24,4096]{1,0:T(8,128)(2,1)S(1)}, u32[]{:S(2)}, u32[]{:S(2)}) collective-permute-start(bf16[24,4096]{1,0:T(8,128)(2,1)} %get-tuple-element.40), channel_id=1, source_target_pairs={{0,16},{16,32},{32,48},{48,2},{2,18},{18,34},{34,50},{50,0},{1,17}... | collective-permute-start | bytes 589832 | tf_op jit(solution)/shard_map/ppermute | solution.py:185
  219.2 10.4 %collective-permute-start.26 = (bf16[16,4096]{1,0:T(8,128)(2,1)}, bf16[16,4096]{1,0:T(8,128)(2,1)S(1)}, u32[]{:S(2)}, u32[]{:S(2)}) collective-permute-start(bf16[16,4096]{1,0:T(8,128)(2,1)} %get-tuple-element.42), channel_id=1, source_target_pairs={{0,32},{16,48},{32,2},{48,18},{2,34},{18,50},{34,0},{50,16},{1,33}... | collective-permute-start | bytes 393224 | tf_op jit(solution)/shard_map/ppermute | solution.py:185
  (17 other events, 158.6 us)

commit v3 on v2

--- a/solution.py
+++ b/solution.py
@@ -21,23 +21,42 @@
 SCALE = math.log2(math.e) / math.sqrt(HD)
 
 
-def attend_kernel(base, count, groups_out, aliased, *refs):
-    query_refs, place_refs = refs[:5], refs[5:10]
-    windows = refs[10 : 10 + count]
-    out_refs = refs[10 + count + aliased : 10 + count + aliased + len(groups_out)]
-    held, far, sems = refs[10 + count + aliased + len(groups_out) :]
+def attend_kernel(base, count, split, sources, groups_out, aliased, *refs):
+    query_refs, place_refs = refs[:sources], refs[sources : 2 * sources]
+    sizes = [1] * (count - split) + [2] * split
+    at_ref = 2 * sources
+    windows = []
+    for size in sizes:
+        windows.append(refs[at_ref : at_ref + size])
+        at_ref += size
+    at_ref += aliased
+    out_refs = refs[at_ref : at_ref + len(groups_out)]
+    held, far, sems = refs[at_ref + len(groups_out) :]
     at = pl.program_id(0)
-
-    def fetch(k):
-        return pltpu.make_async_copy(windows[k], held.at[k], sems.at[k])
+    mixed = sources == 5
+
+    def fetches(k):
+        pieces = windows[k]
+        width = held.shape[2] // len(pieces)
+        return [
+            pltpu.make_async_copy(
+                piece, held.at[k, :, n * width : (n + 1) * width], sems.at[k, n]
+            )
+            for n, piece in enumerate(pieces)
+        ]
 
     @pl.when(at == 0)
     def _():
         for k in range(count):
-            fetch(k).start()
+            for copy in fetches(k):
+                copy.start()
 
     for k in range(count):
-        pl.when(at == k)(lambda k=k: fetch(k).wait())
+
+        @pl.when(at == k)
+        def _(k=k):
+            for copy in fetches(k):
+                copy.wait()
 
     even = ((base + at) & 1) == 0
     window = held.at[at]
@@ -46,7 +65,10 @@
     rows = COLS * slots
 
     def load(refs_of, lanes):
-        last = jnp.where(even, refs_of[3][:, lanes], refs_of[4][:, lanes])
+        if mixed:
+            last = jnp.where(even, refs_of[3][:, lanes], refs_of[4][:, lanes])
+        else:
+            last = refs_of[3][:, lanes]
         return [ref[:, lanes].astype(jnp.float32) for ref in refs_of[:3]] + [
             last.astype(jnp.float32)
         ]
@@ -95,82 +117,99 @@
                 result = weighted[n * rows : (n + 1) * rows] * inverse[n]
                 for c in range(COLS):
                     piece = result[c * slots : (c + 1) * slots].astype(jnp.bfloat16)
-                    ref = far if c == COLS - 1 else out_refs[c]
+                    ref = far if mixed and c == COLS - 1 else out_refs[c]
                     ref[:, h * HD : (h + 1) * HD] = piece
-    for ref, group in zip(out_refs[3:], groups_out[3:]):
-
-        @pl.when(even if group == 3 else jnp.logical_not(even))
-        def _(ref=ref):
-            ref[...] = far[...]
-
-
-def far_orders(group, orders):
-    return [order for order in orders if order % 2 == group - 3]
+    if mixed:
+
+        @pl.when(even)
+        def _():
+            out_refs[3][...] = far[...]
+
+        @pl.when(jnp.logical_not(even))
+        def _():
+            out_refs[4][...] = far[...]
 
 
 def attend(arrived, windows, orders, batch, buffers):
     slots = ROUNDS * R
     width = QH * HD
-    base, count = orders[0], len(orders)
-    spots = [lambda i: base + i] * 3 + [lambda i: (base + i) >> 1] * 2
-    groups_out = [0, 1, 2] + [group for group in (3, 4) if far_orders(group, orders)]
-    out_specs, out_shape = [], []
-    for group in groups_out:
-        if group < 3:
-            total = len(batch)
-            spot = lambda i: base - batch[0] + i
-        else:
-            mine = far_orders(group, batch)
-            total, lowest = len(mine), mine[0] // 2
-            shift = 1 if group == 3 else 0
-            spot = lambda i, t=total, l=lowest, s=shift: jnp.clip(((base + i + s) >> 1) - l, 0, t - 1)
-        out_specs.append(pl.BlockSpec((slots, width), lambda i, spot=spot: (spot(i), 0)))
-        out_shape.append(jax.ShapeDtypeStruct((total * slots, width), jnp.bfloat16))
-    kept = [group for group in groups_out if group in buffers]
+    base, count, start = orders[0], len(orders), batch[0]
+    by_order = lambda i: base + i
+    if start == 0:
+        evens, odds = (len(batch) + 1) // 2, len(batch) // 2
+        spots = [by_order] * 3 + [lambda i: (base + i) >> 1] * 2
+        groups_out = [0, 1, 2, 3, 4]
+        totals = [len(batch)] * 3 + [evens, odds]
+        places = [by_order] * 3 + [
+            lambda i: jnp.minimum((base + i + 1) >> 1, evens - 1),
+            lambda i: jnp.minimum((base + i) >> 1, odds - 1),
+        ]
+        spots[3] = lambda i: jnp.minimum((base + i) >> 1, evens - 1)
+    else:
+        spots = [by_order] * 3 + [lambda i: base - start + start // 2 + i]
+        groups_out = [0, 1, 2, 4]
+        totals = [len(batch)] * 4
+        places = [lambda i: base - start + i] * 4
+    sources = [arrived[group] for group in groups_out]
+    out_specs = [
+        pl.BlockSpec((slots, width), lambda i, place=place: (place(i), 0)) for place in places
+    ]
+    out_shape = [jax.ShapeDtypeStruct((total * slots, width), jnp.bfloat16) for total in totals]
+    pieces = [piece for window in windows for piece in window]
+    split = sum(len(window) == 2 for window in windows)
+    kept = [buffers[group] for group in groups_out if group in buffers]
+    shape = (pieces[0].shape[0], sum(piece.shape[1] for piece in windows[0]))
     anywhere = pl.BlockSpec(memory_space=pl.ANY)
+    known = 2 * len(sources) + len(pieces)
     outs = pl.pallas_call(
-        lambda *refs: attend_kernel(base, count, groups_out, len(kept), *refs),
+        lambda *refs: attend_kernel(
+            base, count, split, len(sources), groups_out, len(kept), *refs
+        ),
         grid=(count,),
         in_specs=[pl.BlockSpec((slots, width), lambda i, spot=spot: (spot(i), 0)) for spot in spots]
         + [
             pl.BlockSpec((slots, HD), lambda i, spot=spot: (spot(i), width // HD))
             for spot in spots
         ]
-        + [anywhere] * (count + len(kept)),
+        + [anywhere] * (len(pieces) + len(kept)),
         out_specs=out_specs,
         out_shape=out_shape,
         scratch_shapes=[
-            pltpu.VMEM((count,) + windows[0].shape, jnp.bfloat16),
+            pltpu.VMEM((count,) + shape, jnp.bfloat16),
             pltpu.VMEM((slots, width), jnp.bfloat16),
-            pltpu.SemaphoreType.DMA((count,)),
+            pltpu.SemaphoreType.DMA((count, 2)),
         ],
-        input_output_aliases={10 + count + n: groups_out.index(g) for n, g in enumerate(kept)},
+        input_output_aliases={known + n: n for n in range(len(kept))},
         compiler_params=pltpu.CompilerParams(dimension_semantics=("arbitrary",)),
-    )(*arrived, *arrived, *windows, *[buffers[group] for group in kept])
-    return {**buffers, **dict(zip(groups_out, outs))}
-
-
-def collect_kernel(select_ref, *refs):
-    backs, out_ref = refs[:-1], refs[-1]
+    )(*sources, *sources, *pieces, *kept)
+    return dict(zip(groups_out, outs))
+
+
+def collect_kernel(partial, select_ref, *refs):
+    backs, out_ref = refs[partial:-1], refs[-1]
     joined = jnp.concatenate([ref[...].astype(jnp.float32) for ref in backs], axis=0)
-    out_ref[...] = jnp.dot(
+    total = jnp.dot(
         select_ref[...], joined.astype(jnp.bfloat16), preferred_element_type=jnp.float32
-    ).astype(jnp.bfloat16)
-
-
-def collect(select, backs):
+    )
+    if partial:
+        total = total + refs[0][...].astype(jnp.float32)
+    out_ref[...] = total.astype(jnp.bfloat16)
+
+
+def collect(select, backs, partial):
     rows, width = select.shape[0], backs[0].shape[1]
     chunk = width // 4
+    whole = pl.BlockSpec((rows, chunk), lambda i: (0, i))
     return pl.pallas_call(
-        collect_kernel,
+        lambda *refs: collect_kernel(len(partial), *refs),
         grid=(4,),
         in_specs=[pl.BlockSpec(select.shape, lambda i: (0, 0))]
+        + [whole] * len(partial)
         + [pl.BlockSpec((back.shape[0], chunk), lambda i: (0, i)) for back in backs],
-        out_specs=pl.BlockSpec((rows, chunk), lambda i: (0, i)),
+        out_specs=whole,
         out_shape=jax.ShapeDtypeStruct((rows, width), jnp.bfloat16),
         compiler_params=pltpu.CompilerParams(dimension_semantics=("arbitrary",)),
-        name="collect",
-    )(select, *backs)
+    )(select, *partial, *backs)
 
 
 def along_z(array, by):
@@ -234,54 +273,66 @@
     place = upper * block + jnp.repeat(offsets[0, 0], R) + row % R
     place = jnp.broadcast_to(place[:, None], (rows, HD)).astype(jnp.bfloat16)
     payload = jnp.concatenate([queries[0, 0], place], axis=1)
+    late_start = planes - 3
+    late = order >= late_start
+    even = order % 2 == 0
+    minus = jnp.where(late, order - late_start + late_start // 2, order // 2)
+    evens = (late_start + 1) // 2
     groups = [
-        (across == 0, order, 0),
-        (across == 1, order, 1),
-        (across == 3, order, -1),
-        ((across == 2) & (order % 2 == 0), order // 2, 2),
-        ((across == 2) & (order % 2 == 1), order // 2, -2),
+        (across == 0, order, planes, 0),
+        (across == 1, order, planes, 1),
+        (across == 3, order, planes, -1),
+        ((across == 2) & even & ~late, order // 2, evens, 2),
+        ((across == 2) & (late | ~even), minus, planes - evens, -2),
     ]
-    selects, arrived = [], []
-    for number, (chosen, at, by) in enumerate(groups):
-        count = (planes if number < 3 else reach) * slots
-        slot = jnp.arange(count, dtype=jnp.int32)[:, None]
+    arrived = []
+    spot_early, spot_late = jnp.full((rows,), -1, jnp.int32), jnp.full((rows,), -1, jnp.int32)
+    base_early, base_late = 0, 0
+    for number, (chosen, at, count, by) in enumerate(groups):
+        slot = jnp.arange(count * slots, dtype=jnp.int32)[:, None]
         select = (((at * slots + within)[None, :] == slot) & chosen[None, :]).astype(jnp.bfloat16)
-        selects.append(select)
         sending = pick(select, payload)
         arrived.append(along_y(sending, by) if by else sending)
-
-    windows = [window]
+        spot_early = jnp.where(chosen & ~late, base_early + at * slots + within, spot_early)
+        base_early += slots * (late_start if number < 3 else (evens if number == 3 else late_start // 2))
+        if number != 3:
+            at_late = base_late + (order - late_start) * slots + within
+            spot_late = jnp.where(chosen & late, at_late, spot_late)
+            base_late += slots * 3
+    select_early = (spot_early[:, None] == jnp.arange(base_early)[None, :]).astype(jnp.bfloat16)
+    select_late = (spot_late[:, None] == jnp.arange(base_late)[None, :]).astype(jnp.bfloat16)
+
+    windows = [(window,)]
     ahead_window, behind_window = window, window
     width = window.shape[1] // 2
-    backs, chosen = [], []
-
-    def serve(orders, batch, buffers):
-        return attend(arrived, [windows[order] for order in orders], orders, batch, buffers)
-
-    def give_back(buffers, batch):
-        for number, (_, _, by) in enumerate(groups):
-            orders = batch if number < 3 else far_orders(number, batch)
-            lowest = orders[0] if number < 3 else orders[0] // 2
-            backs.append(along_y(buffers[number], -by) if by else buffers[number])
-            chosen.append(selects[number][lowest * slots : (lowest + len(orders)) * slots])
-
-    early = list(range(planes - 3))
-    late = list(range(planes - 3, planes))
     for _ in range(1, reach):
         ahead_window = along_z(ahead_window, -1)
         behind_window = along_z(behind_window, 1)
-        windows += [ahead_window, behind_window]
+        windows += [(ahead_window,), (behind_window,)]
     last_left = along_z(ahead_window[:, :width], -1)
     last_right = along_z(behind_window[:, width:], 1)
-    windows.append(jnp.concatenate([last_left, last_right], axis=1))
-
-    buffers = serve(early[:-2], early, {})
-    buffers = serve(early[-2:], early, buffers)
-    give_back(buffers, early)
-    buffers = serve(late[:2], late, {})
-    buffers = serve(late[2:], late, buffers)
-    give_back(buffers, late)
-    return collect(jnp.concatenate(chosen, axis=0).T, backs)[None, None]
+    windows.append((last_left, last_right))
+
+    def serve(orders, batch, buffers):
+        return attend(arrived, [windows[order] for order in orders], orders, batch, buffers)
+
+    def give_back(buffers):
+        backs = []
+        for number, (_, _, _, by) in enumerate(groups):
+            if number in buffers:
+                backs.append(along_y(buffers[number], -by) if by else buffers[number])
+        return backs
+
+    early_orders, late_orders = list(range(late_start)), list(range(late_start, planes))
+    buffers = serve(early_orders[:3], early_orders, {})
+    for step in range(2, reach - 1):
+        buffers = serve([2 * step - 1, 2 * step], early_orders, buffers)
+    early_backs = give_back(buffers)
+    buffers = serve(late_orders[:2], late_orders, {})
+    buffers = serve(late_orders[2:], late_orders, buffers)
+    late_backs = give_back(buffers)
+    partial = collect(select_early, early_backs, [])
+    return collect(select_late, late_backs, [partial])[None, None]
 
 
 def solution(mesh):

time: 236 us -> 239 us (1.013)
  the two profiles are of different devices: /device:TPU:4 before, /device:TPU:12 now
where the time goes in v3:
time: 239 us; the launch traced here: 237 us
  starting transfers between devices  121 us (51%)
  waiting for transfers between devices  59.1 us (25%)
  Pallas kernels  44 us (18%)
  local copies, waits for them, and re-layouts  7.6 us (3%)
  other arithmetic  2.56 us (1%)
  matrix products  2.56 us (1%)
    ppermute x11, starting transfers between devices, along_y(): return lax.ppermute(array, ('col', 'yh'), pairs)  56.8 us
    ppermute x12, starting transfers between devices, along_z(): lax.ppermute(array, 'z', [(i, (i + by) % planes) for i in range(planes)])  52.8 us
    pallas_call x6, Pallas kernels, attend(): pl.pallas_call(lambda *refs: attend_kernel(base, count, split, len(source...  35.7 us
    ppermute x12, waiting for transfers between devices, along_z(): lax.ppermute(array, 'z', [(i, (i + by) % planes) for i in range(planes)])  26.6 us
    ppermute x11, waiting for transfers between devices, along_y(): return lax.ppermute(array, ('col', 'yh'), pairs)  19.4 us
    pallas_call x2, Pallas kernels, collect(): pl.pallas_call(lambda *refs: collect_kernel(len(partial), *refs), grid=(4...  8.29 us
    ppermute x2, waiting for transfers between devices, along_x(): return lax.ppermute(array, 'x', [(i, i + by) for i in range(peers - by)])  7.12 us
    ppermute x1, starting transfers between devices, window_of(): other = lax.ppermute(joined, 'yh', [(0, 1), (1, 0)])  6.83 us
  transfers between devices with their start and end apart: 26, of which 12 were waited for; matrix products, arithmetic and copies ran while one was open for 3% of the time, Pallas kernels for 17%

profile of v3, /device:TPU:12, one launch (start us, length us, event | category | flops | bytes accessed | tf_op | source)
XLA Modules:
  0.0 237.5 jit_solution(2050102996352099586)
XLA Ops:
  0.8 6.8 %collective-permute-start.4 = (bf16[128,512]{1,0:T(8,128)(2,1)S(1)}, bf16[128,512]{1,0:T(8,128)(2,1)S(1)}, u32[]{:S(2)}, u32[]{:S(2)}) collective-permute-start(bf16[128,512]{1,0:T(8,128)(2,1)S(1)} %pad_maximum_fusion.2), channel_id=1, source_target_pairs={{0,2},{2,0},{1,3},{3,1},{4,6},{6,4},{5,7},{7,5},{8,10},{10,8},{9,1... | collective-permute-start | bytes 393224 | tf_op jit(solution)/shard_map/ppermute | solution.py:237
  8.6 5.9 %collective-permute-done.4 = bf16[128,512]{1,0:T(8,128)(2,1)S(1)} collective-permute-done((bf16[128,512]{1,0:T(8,128)(2,1)S(1)}, bf16[128,512]{1,0:T(8,128)(2,1)S(1)}, u32[]{:S(2)}, u32[]{:S(2)}) %collective-permute-start.4) | collective-permute-done | bytes 131104 | tf_op jit(solution)/shard_map/ppermute | solution.py:237
  16.1 3.1 %collective-permute-start.6 = (bf16[256,512]{1,0:T(8,128)(2,1)S(1)}, bf16[256,512]{1,0:T(8,128)(2,1)S(1)}, u32[]{:S(2)}, u32[]{:S(2)}) collective-permute-start(bf16[256,512]{1,0:T(8,128)(2,1)S(1)} %pad_maximum_fusion.1), channel_id=1, source_target_pairs={{0,4},{4,8},{8,12},{1,5},{5,9},{9,13},{2,6},{6,10},{10,14},{3,7},{... | collective-permute-start | bytes 786440 | tf_op jit(solution)/shard_map/ppermute | solution.py:229
  19.2 4.4 %collective-permute-done.5 = bf16[128,512]{1,0:T(8,128)(2,1)S(1)} collective-permute-done((bf16[128,512]{1,0:T(8,128)(2,1)S(1)}, bf16[128,512]{1,0:T(8,128)(2,1)S(1)}, u32[]{:S(2)}, u32[]{:S(2)}) %collective-permute-start.5) | collective-permute-done | bytes 131104 | tf_op jit(solution)/shard_map/ppermute | solution.py:229
  23.6 2.7 %collective-permute-done.6 = bf16[256,512]{1,0:T(8,128)(2,1)S(1)} collective-permute-done((bf16[256,512]{1,0:T(8,128)(2,1)S(1)}, bf16[256,512]{1,0:T(8,128)(2,1)S(1)}, u32[]{:S(2)}, u32[]{:S(2)}) %collective-permute-start.6) | collective-permute-done | bytes 262176 | tf_op jit(solution)/shard_map/ppermute | solution.py:229
  26.6 14.6 %collective-permute-start.7 = (bf16[648,512]{1,0:T(8,128)(2,1)S(1)}, bf16[648,512]{1,0:T(8,128)(2,1)S(1)}, u32[]{:S(2)}, u32[]{:S(2)}) collective-permute-start(bf16[648,512]{1,0:T(8,128)(2,1)S(1)} %constant_dynamic-update-slice_fusion.refs_10_), channel_id=1, source_target_pairs={{0,704},{64,0},{128,64},{192,128},{256,192},{320,256},{384,320},{4... | collective-permute-start | bytes 1990664 | tf_op jit(solution)/shard_map/ppermute | solution.py:217
  43.1 7.5 %collective-permute-done.7.refs_11_ = bf16[648,512]{1,0:T(8,128)(2,1)S(1)} collective-permute-done((bf16[648,512]{1,0:T(8,128)(2,1)S(1)}, bf16[648,512]{1,0:T(8,128)(2,1)S(1)}, u32[]{:S(2)}, u32[]{:S(2)}) %collective-permute-start.7) | collective-permute-done | bytes 663584 | tf_op jit(solution)/shard_map/ppermute | solution.py:217
  50.6 5.6 %collective-permute-start.8 = (bf16[648,512]{1,0:T(8,128)(2,1)S(1)}, bf16[648,512]{1,0:T(8,128)(2,1)S(1)}, u32[]{:S(2)}, u32[]{:S(2)}) collective-permute-start(bf16[648,512]{1,0:T(8,128)(2,1)S(1)} %collective-permute-done.7.refs_11_), channel_id=1, source_target_pairs={{0,704},{64,0},{128,64},{192,128},{256,192},{320,256},{384,320},{4... | collective-permute-start | bytes 1990664 | tf_op jit(solution)/shard_map/ppermute | solution.py:217
  58.6 7.1 %collective-permute-done.8.refs_10_ = bf16[648,512]{1,0:T(8,128)(2,1)S(1)} collective-permute-done((bf16[648,512]{1,0:T(8,128)(2,1)S(1)}, bf16[648,512]{1,0:T(8,128)(2,1)S(1)}, u32[]{:S(2)}, u32[]{:S(2)}) %collective-permute-start.8) | collective-permute-done | bytes 663584 | tf_op jit(solution)/shard_map/ppermute | solution.py:217
  65.7 5.6 %collective-permute-start.9 = (bf16[648,512]{1,0:T(8,128)(2,1)S(1)}, bf16[648,512]{1,0:T(8,128)(2,1)S(1)}, u32[]{:S(2)}, u32[]{:S(2)}) collective-permute-start(bf16[648,512]{1,0:T(8,128)(2,1)S(1)} %collective-permute-done.8.refs_10_), channel_id=1, source_target_pairs={{0,704},{64,0},{128,64},{192,128},{256,192},{320,256},{384,320},{4... | collective-permute-start | bytes 1990664 | tf_op jit(solution)/shard_map/ppermute | solution.py:217
  74.1 7.8 %collective-permute-done.9.refs_10_ = bf16[648,512]{1,0:T(8,128)(2,1)S(1)} collective-permute-done((bf16[648,512]{1,0:T(8,128)(2,1)S(1)}, bf16[648,512]{1,0:T(8,128)(2,1)S(1)}, u32[]{:S(2)}, u32[]{:S(2)}) %collective-permute-start.9) | collective-permute-done | bytes 663584 | tf_op jit(solution)/shard_map/ppermute | solution.py:217
  81.9 5.6 %collective-permute-start.10 = (bf16[648,512]{1,0:T(8,128)(2,1)S(1)}, bf16[648,512]{1,0:T(8,128)(2,1)S(1)}, u32[]{:S(2)}, u32[]{:S(2)}) collective-permute-start(bf16[648,512]{1,0:T(8,128)(2,1)S(1)} %collective-permute-done.9.refs_10_), channel_id=1, source_target_pairs={{0,704},{64,0},{128,64},{192,128},{256,192},{320,256},{384,320},{4... | collective-permute-start | bytes 1990664 | tf_op jit(solution)/shard_map/ppermute | solution.py:217
  91.7 15.7 %collective-permute-start = (bf16[96,4224]{1,0:T(8,128)(2,1)S(1)}, bf16[96,4224]{1,0:T(8,128)(2,1)S(1)}, u32[]{:S(2)}, u32[]{:S(2)}) collective-permute-start(bf16[96,4224]{1,0:T(8,128)(2,1)S(1)} %convolution_convert_fusion.1), channel_id=1, source_target_pairs={{0,16},{16,32},{32,48},{48,2},{2,18},{18,34},{34,50},{50,0},{1,17}... | collective-permute-start | bytes 2433032 | tf_op jit(solution)/shard_map/ppermute | solution.py:224
  107.4 5.1 %collective-permute-start.19 = (bf16[648,512]{1,0:T(8,128)(2,1)S(1)}, bf16[648,512]{1,0:T(8,128)(2,1)S(1)}, u32[]{:S(2)}, u32[]{:S(2)}) collective-permute-start(bf16[648,512]{1,0:T(8,128)(2,1)S(1)} %collective-permute-done.10.refs_10_), channel_id=1, source_target_pairs={{0,704},{64,0},{128,64},{192,128},{256,192},{320,256},{384,320},{4... | collective-permute-start | bytes 1990664 | tf_op jit(solution)/shard_map/ppermute | solution.py:217
  115.2 11.0 %collective-permute-start.2 = (bf16[40,4224]{1,0:T(8,128)(2,1)S(1)}, bf16[40,4224]{1,0:T(8,128)(2,1)S(1)}, u32[]{:S(2)}, u32[]{:S(2)}) collective-permute-start(bf16[40,4224]{1,0:T(8,128)(2,1)S(1)} %convolution_convert_fusion.4), channel_id=1, source_target_pairs={{0,32},{16,48},{32,2},{48,18},{2,34},{18,50},{34,0},{50,16},{1,33}... | collective-permute-start | bytes 1013768 | tf_op jit(solution)/shard_map/ppermute | solution.py:224
  128.5 4.7 %collective-permute-start.3 = (bf16[56,4224]{1,0:T(8,128)(2,1)S(1)}, bf16[56,4224]{1,0:T(8,128)(2,1)S(1)}, u32[]{:S(2)}, u32[]{:S(2)}) collective-permute-start(bf16[56,4224]{1,0:T(8,128)(2,1)S(1)} %convolution_convert_fusion.3), channel_id=1, source_target_pairs={{0,34},{16,50},{32,0},{48,16},{2,32},{18,48},{34,2},{50,18},{1,35}... | collective-permute-start | bytes 1419272 | tf_op jit(solution)/shard_map/ppermute | solution.py:224
  134.0 2.8 %collective-permute-done.2.refs_3_.refs_8_ = bf16[40,4224]{1,0:T(8,128)(2,1)S(1)} collective-permute-done((bf16[40,4224]{1,0:T(8,128)(2,1)S(1)}, bf16[40,4224]{1,0:T(8,128)(2,1)S(1)}, u32[]{:S(2)}, u32[]{:S(2)}) %collective-permute-start.2) | collective-permute-done | bytes 337952 | tf_op jit(solution)/shard_map/ppermute | solution.py:224
  136.7 4.7 %collective-permute-start.20 = (bf16[648,256]{1,0:T(8,128)(2,1)}, bf16[648,256]{1,0:T(8,128)(2,1)}, u32[]{:S(2)}, u32[]{:S(2)}) collective-permute-start(bf16[648,256]{1,0:T(8,128)(2,1)} %slice.33), channel_id=1, source_target_pairs={{0,704},{64,0},{128,64},{192,128},{256,192},{320,256},{384,320},{4... | collective-permute-start | bytes 995336 | tf_op jit(solution)/shard_map/ppermute | solution.py:217
  142.7 15.8 %collective-permute-done.3.refs_4_.refs_9_.refs_3_.refs_7_ = bf16[56,4224]{1,0:T(8,128)(2,1)S(1)} collective-permute-done((bf16[56,4224]{1,0:T(8,128)(2,1)S(1)}, bf16[56,4224]{1,0:T(8,128)(2,1)S(1)}, u32[]{:S(2)}, u32[]{:S(2)}) %collective-permute-start.3) | collective-permute-done | bytes 473120 | tf_op jit(solution)/shard_map/ppermute | solution.py:224
  160.5 7.6 %shard_map.64 = (bf16[72,4096]{1,0:T(8,128)(2,1)}, bf16[72,4096]{1,0:T(8,128)(2,1)}, bf16[72,4096]{1,0:T(8,128)(2,1)}, bf16[40,4096]{1,0:T(8,128)(2,1)}, bf16[32,4096]{1,0:T(8,128)(2,1)}) custom-call(bf16[96,4224]{1,0:T(8,128)(2,1)} %convolution_convert_fusion.2.refs_0_.refs_5_.refs_4_, bf16[96,4224]{1,0:T(8,128)(2,1)} %copy-done, ...), custom_call_target="tpu_custom_call" | custom-call | tf_op jit(solution)/shard_map/pallas_call | solution.py:164
  168.1 6.0 %shard_map.65 = (bf16[72,4096]{1,0:T(8,128)(2,1)}, bf16[72,4096]{1,0:T(8,128)(2,1)}, bf16[72,4096]{1,0:T(8,128)(2,1)}, bf16[40,4096]{1,0:T(8,128)(2,1)}, bf16[32,4096]{1,0:T(8,128)(2,1)}) custom-call(bf16[96,4224]{1,0:T(8,128)(2,1)} %convolution_convert_fusion.2.refs_0_.refs_5_.refs_4_, ...), custom_call_target="tpu_custom_call", output_to_operand_aliasing={{0}: (12, {}), {1}: (13, {}), {2}: (14, {}), {3}: (15, {}),... | custom-call | tf_op jit(solution)/shard_map/pallas_call | solution.py:164
  174.1 6.1 %shard_map.66 = (bf16[72,4096]{1,0:T(8,128)(2,1)}, bf16[72,4096]{1,0:T(8,128)(2,1)}, bf16[72,4096]{1,0:T(8,128)(2,1)}, bf16[40,4096]{1,0:T(8,128)(2,1)}, bf16[32,4096]{1,0:T(8,128)(2,1)}) custom-call(bf16[96,4224]{1,0:T(8,128)(2,1)} %convolution_convert_fusion.2.refs_0_.refs_5_.refs_4_, ...), custom_call_target="tpu_custom_call", output_to_operand_aliasing={{0}: (12, {}), {1}: (13, {}), {2}: (14, {}), {3}: (15, {}),... | custom-call | tf_op jit(solution)/shard_map/pallas_call | solution.py:164
  180.2 6.0 %shard_map.67 = (bf16[72,4096]{1,0:T(8,128)(2,1)}, bf16[72,4096]{1,0:T(8,128)(2,1)}, bf16[72,4096]{1,0:T(8,128)(2,1)}, bf16[40,4096]{1,0:T(8,128)(2,1)}, bf16[32,4096]{1,0:T(8,128)(2,1)}) custom-call(bf16[96,4224]{1,0:T(8,128)(2,1)} %convolution_convert_fusion.2.refs_0_.refs_5_.refs_4_, ...), custom_call_target="tpu_custom_call", output_to_operand_aliasing={{0}: (12, {}), {1}: (13, {}), {2}: (14, {}), {3}: (15, {}),... | custom-call | tf_op jit(solution)/shard_map/pallas_call | solution.py:164
  188.1 3.9 %collective-permute-start.16 = (bf16[72,4096]{1,0:T(8,128)(2,1)}, bf16[72,4096]{1,0:T(8,128)(2,1)S(1)}, u32[]{:S(2)}, u32[]{:S(2)}) collective-permute-start(bf16[72,4096]{1,0:T(8,128)(2,1)} %get-tuple-element.50), channel_id=1, source_target_pairs={{0,16},{16,32},{32,48},{48,2},{2,18},{18,34},{34,50},{50,0},{1,17}... | collective-permute-start | bytes 1769480 | tf_op jit(solution)/shard_map/ppermute | solution.py:224
  192.1 3.3 %collective-permute-start.17 = (bf16[40,4096]{1,0:T(8,128)(2,1)}, bf16[40,4096]{1,0:T(8,128)(2,1)S(1)}, u32[]{:S(2)}, u32[]{:S(2)}) collective-permute-start(bf16[40,4096]{1,0:T(8,128)(2,1)} %get-tuple-element.51), channel_id=1, source_target_pairs={{0,34},{16,50},{32,0},{48,16},{2,32},{18,48},{34,2},{50,18},{1,35}... | collective-permute-start | bytes 983048 | tf_op jit(solution)/shard_map/ppermute | solution.py:224
  195.4 3.5 %collective-permute-start.18 = (bf16[32,4096]{1,0:T(8,128)(2,1)}, bf16[32,4096]{1,0:T(8,128)(2,1)S(1)}, u32[]{:S(2)}, u32[]{:S(2)}) collective-permute-start(bf16[32,4096]{1,0:T(8,128)(2,1)} %get-tuple-element.52), channel_id=1, source_target_pairs={{0,32},{16,48},{32,2},{48,18},{2,34},{18,50},{34,0},{50,16},{1,33}... | collective-permute-start | bytes 786440 | tf_op jit(solution)/shard_map/ppermute | solution.py:224
  202.7 5.8 %shard_map.69 = (bf16[24,4096]{1,0:T(8,128)(2,1)}, bf16[24,4096]{1,0:T(8,128)(2,1)}, bf16[24,4096]{1,0:T(8,128)(2,1)}, bf16[24,4096]{1,0:T(8,128)(2,1)}) custom-call(bf16[96,4224]{1,0:T(8,128)(2,1)} %convolution_convert_fusion.2.refs_0_.refs_5_.refs_4_, bf16[96,4224]{1,0:T(8,128)(2,1)} %copy-done, bf16[96,4224]{1,0:T(8,128)(2,1)} %copy-done.1, ...), custom_call_target="tpu_custom_call" | custom-call | tf_op jit(solution)/shard_map/pallas_call | solution.py:164
  210.8 4.2 %shard_map.70 = (bf16[24,4096]{1,0:T(8,128)(2,1)}, bf16[24,4096]{1,0:T(8,128)(2,1)}, bf16[24,4096]{1,0:T(8,128)(2,1)}, bf16[24,4096]{1,0:T(8,128)(2,1)}) custom-call(bf16[96,4224]{1,0:T(8,128)(2,1)} %convolution_convert_fusion.2.refs_0_.refs_5_.refs_4_, ...), custom_call_target="tpu_custom_call", output_to_operand_aliasing={{0}: (10, {}), {1}: (11, {}), {2}: (12, {}), {3}: (13, {})} | custom-call | tf_op jit(solution)/shard_map/pallas_call | solution.py:164
  217.4 3.5 %collective-permute-start.24 = (bf16[24,4096]{1,0:T(8,128)(2,1)}, bf16[24,4096]{1,0:T(8,128)(2,1)S(1)}, u32[]{:S(2)}, u32[]{:S(2)}) collective-permute-start(bf16[24,4096]{1,0:T(8,128)(2,1)} %get-tuple-element.59), channel_id=1, source_target_pairs={{0,16},{16,32},{32,48},{48,2},{2,18},{18,34},{34,50},{50,0},{1,17}... | collective-permute-start | bytes 589832 | tf_op jit(solution)/shard_map/ppermute | solution.py:224
  220.9 5.1 %collective-permute-start.25 = (bf16[24,4096]{1,0:T(8,128)(2,1)}, bf16[24,4096]{1,0:T(8,128)(2,1)S(1)}, u32[]{:S(2)}, u32[]{:S(2)}) collective-permute-start(bf16[24,4096]{1,0:T(8,128)(2,1)} %get-tuple-element.60), channel_id=1, source_target_pairs={{0,32},{16,48},{32,2},{48,18},{2,34},{18,50},{34,0},{50,16},{1,33}... | collective-permute-start | bytes 589832 | tf_op jit(solution)/shard_map/ppermute | solution.py:224
  227.7 4.4 %shard_map.68.refs_1_ = bf16[128,4096]{1,0:T(8,128)(2,1)} custom-call(bf16[128,288]{1,0:T(8,128)(2,1)} %fusion.refs_0_, bf16[72,4096]{1,0:T(8,128)(2,1)} %get-tuple-element.48.refs_1_, bf16[72,4096]{1,0:T(8,128)(2,1)} %copy-done.12, bf16[72,4096]{1,0:T(8,128)(2,1)} %copy-done.13, bf16[40,4096]{1,0:T(8,128)(2,1)} %copy-done.15, bf16[32,4096]{1,0:T(8,128)(2,1)} %copy-done.16), custom_call_target="tpu_custom_call" | custom-call | tf_op jit(solution)/shard_map/pallas_call | solution.py:203
  233.6 3.9 %shard_map.71 = bf16[128,4096]{1,0:T(8,128)(2,1)} custom-call(bf16[128,96]{1,0:T(8,128)(2,1)} %fusion.1.refs_0_, bf16[128,4096]{1,0:T(8,128)(2,1)} %shard_map.68.refs_1_, bf16[24,4096]{1,0:T(8,128)(2,1)} %get-tuple-element.57.refs_2_, bf16[24,4096]{1,0:T(8,128)(2,1)} %copy-done.17, bf16[24,4096]{1,0:T(8,128)(2,1)} %copy-done.18, bf16[24,4096]{1,0:T(8,128)(2,1)} %copy-done.19), custom_call_target="tpu_custom_call" | custom-call | tf_op jit(solution)/shard_map/pallas_call | solution.py:203
  (108 shorter events, 37.0 us)
Async XLA Ops:
  0.8 13.7 %collective-permute-start.4 = (bf16[128,512]{1,0:T(8,128)(2,1)S(1)}, bf16[128,512]{1,0:T(8,128)(2,1)S(1)}, u32[]{:S(2)}, u32[]{:S(2)}) collective-permute-start(bf16[128,512]{1,0:T(8,128)(2,1)S(1)} %pad_maximum_fusion.2), channel_id=1, source_target_pairs={{0,2},{2,0},{1,3},{3,1},{4,6},{6,4},{5,7},{7,5},{8,10},{10,8},{9,1... | collective-permute-start | bytes 393224 | tf_op jit(solution)/shard_map/ppermute | solution.py:237
  14.6 41.6 %copy-start.20 = (s32[1,1,32]{2,1,0:T(1,128)S(1)}, s32[1,1,32]{2,1,0:T(1,128)}, u32[]{:S(2)}) copy-start(s32[1,1,32]{2,1,0:T(1,128)} %param.7) | copy-start | bytes 388
  14.6 43.8 %copy-start.21 = (s32[1,1,32]{2,1,0:T(1,128)S(1)}, s32[1,1,32]{2,1,0:T(1,128)}, u32[]{:S(2)}) copy-start(s32[1,1,32]{2,1,0:T(1,128)} %param.8) | copy-start | bytes 388
  14.6 76.7 %copy-start.4 = (bf16[1,1,128,4096]{3,2,1,0:T(8,128)(2,1)S(1)}, bf16[1,1,128,4096]{3,2,1,0:T(8,128)(2,1)}, u32[]{:S(2)}) copy-start(bf16[1,1,128,4096]{3,2,1,0:T(8,128)(2,1)} %param.6) | copy-start | bytes 3145732
  14.6 9.0 %collective-permute-start.5 = (bf16[128,512]{1,0:T(8,128)(2,1)S(1)}, bf16[128,512]{1,0:T(8,128)(2,1)S(1)}, u32[]{:S(2)}, u32[]{:S(2)}) collective-permute-start(bf16[128,512]{1,0:T(8,128)(2,1)S(1)} %get-tuple-element.72), channel_id=1, source_target_pairs={{0,8},{4,12},{1,9},{5,13},{2,10},{6,14},{3,11},{7,15},{16,24},{20,... | collective-permute-start | bytes 393224 | tf_op jit(solution)/shard_map/ppermute | solution.py:229
  16.1 10.3 %collective-permute-start.6 = (bf16[256,512]{1,0:T(8,128)(2,1)S(1)}, bf16[256,512]{1,0:T(8,128)(2,1)S(1)}, u32[]{:S(2)}, u32[]{:S(2)}) collective-permute-start(bf16[256,512]{1,0:T(8,128)(2,1)S(1)} %pad_maximum_fusion.1), channel_id=1, source_target_pairs={{0,4},{4,8},{8,12},{1,5},{5,9},{9,13},{2,6},{6,10},{10,14},{3,7},{... | collective-permute-start | bytes 786440 | tf_op jit(solution)/shard_map/ppermute | solution.py:229
  26.6 64.7 %copy-start.6 = (bf16[648,512]{1,0:T(8,128)(2,1)}, bf16[648,512]{1,0:T(8,128)(2,1)S(1)}, u32[]{:S(2)}) copy-start(bf16[648,512]{1,0:T(8,128)(2,1)S(1)} %constant_dynamic-update-slice_fusion.refs_10_) | copy-start | bytes 1990660
  26.6 24.1 %collective-permute-start.7 = (bf16[648,512]{1,0:T(8,128)(2,1)S(1)}, bf16[648,512]{1,0:T(8,128)(2,1)S(1)}, u32[]{:S(2)}, u32[]{:S(2)}) collective-permute-start(bf16[648,512]{1,0:T(8,128)(2,1)S(1)} %constant_dynamic-update-slice_fusion.refs_10_), channel_id=1, source_target_pairs={{0,704},{64,0},{128,64},{192,128},{256,192},{320,256},{384,320},{4... | collective-permute-start | bytes 1990664 | tf_op jit(solution)/shard_map/ppermute | solution.py:217
  41.2 15.3 %collective-permute-start.11 = (bf16[648,512]{1,0:T(8,128)(2,1)S(1)}, bf16[648,512]{1,0:T(8,128)(2,1)}, u32[]{:S(2)}, u32[]{:S(2)}) collective-permute-start(bf16[648,512]{1,0:T(8,128)(2,1)S(1)} %constant_dynamic-update-slice_fusion.refs_10_), channel_id=1, source_target_pairs={{0,64},{64,128},{128,192},{192,256},{256,320},{320,384},{384,448},... | collective-permute-start | bytes 1990664 | tf_op jit(solution)/shard_map/ppermute | solution.py:217
  50.6 40.7 %copy-start.7 = (bf16[648,512]{1,0:T(8,128)(2,1)}, bf16[648,512]{1,0:T(8,128)(2,1)S(1)}, u32[]{:S(2)}) copy-start(bf16[648,512]{1,0:T(8,128)(2,1)S(1)} %collective-permute-done.7.refs_11_) | copy-start | bytes 1990660
  50.6 15.1 %collective-permute-start.8 = (bf16[648,512]{1,0:T(8,128)(2,1)S(1)}, bf16[648,512]{1,0:T(8,128)(2,1)S(1)}, u32[]{:S(2)}, u32[]{:S(2)}) collective-permute-start(bf16[648,512]{1,0:T(8,128)(2,1)S(1)} %collective-permute-done.7.refs_11_), channel_id=1, source_target_pairs={{0,704},{64,0},{128,64},{192,128},{256,192},{320,256},{384,320},{4... | collective-permute-start | bytes 1990664 | tf_op jit(solution)/shard_map/ppermute | solution.py:217
  56.5 15.8 %collective-permute-start.12 = (bf16[648,512]{1,0:T(8,128)(2,1)}, bf16[648,512]{1,0:T(8,128)(2,1)}, u32[]{:S(2)}, u32[]{:S(2)}) collective-permute-start(bf16[648,512]{1,0:T(8,128)(2,1)} %collective-permute-done.11.refs_12_), channel_id=1, source_target_pairs={{0,64},{64,128},{128,192},{192,256},{256,320},{320,384},{384,448},... | collective-permute-start | bytes 1990664 | tf_op jit(solution)/shard_map/ppermute | solution.py:217
  65.7 46.9 %copy-start.8 = (bf16[648,512]{1,0:T(8,128)(2,1)}, bf16[648,512]{1,0:T(8,128)(2,1)S(1)}, u32[]{:S(2)}) copy-start(bf16[648,512]{1,0:T(8,128)(2,1)S(1)} %collective-permute-done.8.refs_10_) | copy-start | bytes 1990660
  65.7 16.2 %collective-permute-start.9 = (bf16[648,512]{1,0:T(8,128)(2,1)S(1)}, bf16[648,512]{1,0:T(8,128)(2,1)S(1)}, u32[]{:S(2)}, u32[]{:S(2)}) collective-permute-start(bf16[648,512]{1,0:T(8,128)(2,1)S(1)} %collective-permute-done.8.refs_10_), channel_id=1, source_target_pairs={{0,704},{64,0},{128,64},{192,128},{256,192},{320,256},{384,320},{4... | collective-permute-start | bytes 1990664 | tf_op jit(solution)/shard_map/ppermute | solution.py:217
  72.2 17.1 %collective-permute-start.13 = (bf16[648,512]{1,0:T(8,128)(2,1)}, bf16[648,512]{1,0:T(8,128)(2,1)S(1)}, u32[]{:S(2)}, u32[]{:S(2)}) collective-permute-start(bf16[648,512]{1,0:T(8,128)(2,1)} %collective-permute-done.12.refs_11_), channel_id=1, source_target_pairs={{0,64},{64,128},{128,192},{192,256},{256,320},{320,384},{384,448},... | collective-permute-start | bytes 1990664 | tf_op jit(solution)/shard_map/ppermute | solution.py:217
  81.9 25.5 %collective-permute-start.10 = (bf16[648,512]{1,0:T(8,128)(2,1)S(1)}, bf16[648,512]{1,0:T(8,128)(2,1)S(1)}, u32[]{:S(2)}, u32[]{:S(2)}) collective-permute-start(bf16[648,512]{1,0:T(8,128)(2,1)S(1)} %collective-permute-done.9.refs_10_), channel_id=1, source_target_pairs={{0,704},{64,0},{128,64},{192,128},{256,192},{320,256},{384,320},{4... | collective-permute-start | bytes 1990664 | tf_op jit(solution)/shard_map/ppermute | solution.py:217
  89.3 36.9 %collective-permute-start.14 = (bf16[648,512]{1,0:T(8,128)(2,1)S(1)}, bf16[648,512]{1,0:T(8,128)(2,1)}, u32[]{:S(2)}, u32[]{:S(2)}) collective-permute-start(bf16[648,512]{1,0:T(8,128)(2,1)S(1)} %collective-permute-done.13.refs_11_), channel_id=1, source_target_pairs={{0,64},{64,128},{128,192},{192,256},{256,320},{320,384},{384,448},... | collective-permute-start | bytes 1990664 | tf_op jit(solution)/shard_map/ppermute | solution.py:217
  91.7 66.8 %collective-permute-start = (bf16[96,4224]{1,0:T(8,128)(2,1)S(1)}, bf16[96,4224]{1,0:T(8,128)(2,1)S(1)}, u32[]{:S(2)}, u32[]{:S(2)}) collective-permute-start(bf16[96,4224]{1,0:T(8,128)(2,1)S(1)} %convolution_convert_fusion.1), channel_id=1, source_target_pairs={{0,16},{16,32},{32,48},{48,2},{2,18},{18,34},{34,50},{50,0},{1,17}... | collective-permute-start | bytes 2433032 | tf_op jit(solution)/shard_map/ppermute | solution.py:224
  107.4 21.0 %collective-permute-start.19 = (bf16[648,512]{1,0:T(8,128)(2,1)S(1)}, bf16[648,512]{1,0:T(8,128)(2,1)S(1)}, u32[]{:S(2)}, u32[]{:S(2)}) collective-permute-start(bf16[648,512]{1,0:T(8,128)(2,1)S(1)} %collective-permute-done.10.refs_10_), channel_id=1, source_target_pairs={{0,704},{64,0},{128,64},{192,128},{256,192},{320,256},{384,320},{4... | collective-permute-start | bytes 1990664 | tf_op jit(solution)/shard_map/ppermute | solution.py:217
  113.0 45.6 %collective-permute-start.1 = (bf16[96,4224]{1,0:T(8,128)(2,1)S(1)}, bf16[96,4224]{1,0:T(8,128)(2,1)S(1)}, u32[]{:S(2)}, u32[]{:S(2)}) collective-permute-start(bf16[96,4224]{1,0:T(8,128)(2,1)S(1)} %convolution_convert_fusion), channel_id=1, source_target_pairs={{0,50},{16,0},{32,16},{48,32},{2,48},{18,2},{34,18},{50,34},{1,51}... | collective-permute-start | bytes 2433032 | tf_op jit(solution)/shard_map/ppermute | solution.py:224
  115.2 21.5 %collective-permute-start.2 = (bf16[40,4224]{1,0:T(8,128)(2,1)S(1)}, bf16[40,4224]{1,0:T(8,128)(2,1)S(1)}, u32[]{:S(2)}, u32[]{:S(2)}) collective-permute-start(bf16[40,4224]{1,0:T(8,128)(2,1)S(1)} %convolution_convert_fusion.4), channel_id=1, source_target_pairs={{0,32},{16,48},{32,2},{48,18},{2,34},{18,50},{34,0},{50,16},{1,33}... | collective-permute-start | bytes 1013768 | tf_op jit(solution)/shard_map/ppermute | solution.py:224
  126.2 69.1 %collective-permute-start.21 = (bf16[648,512]{1,0:T(8,128)(2,1)}, bf16[648,512]{1,0:T(8,128)(2,1)}, u32[]{:S(2)}, u32[]{:S(2)}) collective-permute-start(bf16[648,512]{1,0:T(8,128)(2,1)} %collective-permute-done.14.refs_11_), channel_id=1, source_target_pairs={{0,64},{64,128},{128,192},{192,256},{256,320},{320,384},{384,448},... | collective-permute-start | bytes 1990664 | tf_op jit(solution)/shard_map/ppermute | solution.py:217
  128.5 30.0 %collective-permute-start.3 = (bf16[56,4224]{1,0:T(8,128)(2,1)S(1)}, bf16[56,4224]{1,0:T(8,128)(2,1)S(1)}, u32[]{:S(2)}, u32[]{:S(2)}) collective-permute-start(bf16[56,4224]{1,0:T(8,128)(2,1)S(1)} %convolution_convert_fusion.3), channel_id=1, source_target_pairs={{0,34},{16,50},{32,0},{48,16},{2,32},{18,48},{34,2},{50,18},{1,35}... | collective-permute-start | bytes 1419272 | tf_op jit(solution)/shard_map/ppermute | solution.py:224
  136.7 63.1 %collective-permute-start.20 = (bf16[648,256]{1,0:T(8,128)(2,1)}, bf16[648,256]{1,0:T(8,128)(2,1)}, u32[]{:S(2)}, u32[]{:S(2)}) collective-permute-start(bf16[648,256]{1,0:T(8,128)(2,1)} %slice.33), channel_id=1, source_target_pairs={{0,704},{64,0},{128,64},{192,128},{256,192},{320,256},{384,320},{4... | collective-permute-start | bytes 995336 | tf_op jit(solution)/shard_map/ppermute | solution.py:217
  186.2 40.5 %collective-permute-start.15 = (bf16[72,4096]{1,0:T(8,128)(2,1)}, bf16[72,4096]{1,0:T(8,128)(2,1)S(1)}, u32[]{:S(2)}, u32[]{:S(2)}) collective-permute-start(bf16[72,4096]{1,0:T(8,128)(2,1)} %get-tuple-element.49), channel_id=1, source_target_pairs={{0,50},{16,0},{32,16},{48,32},{2,48},{18,2},{34,18},{50,34},{1,51}... | collective-permute-start | bytes 1769480 | tf_op jit(solution)/shard_map/ppermute | solution.py:224
  188.1 38.6 %collective-permute-start.16 = (bf16[72,4096]{1,0:T(8,128)(2,1)}, bf16[72,4096]{1,0:T(8,128)(2,1)S(1)}, u32[]{:S(2)}, u32[]{:S(2)}) collective-permute-start(bf16[72,4096]{1,0:T(8,128)(2,1)} %get-tuple-element.50), channel_id=1, source_target_pairs={{0,16},{16,32},{32,48},{48,2},{2,18},{18,34},{34,50},{50,0},{1,17}... | collective-permute-start | bytes 1769480 | tf_op jit(solution)/shard_map/ppermute | solution.py:224
  192.1 28.8 %collective-permute-start.17 = (bf16[40,4096]{1,0:T(8,128)(2,1)}, bf16[40,4096]{1,0:T(8,128)(2,1)S(1)}, u32[]{:S(2)}, u32[]{:S(2)}) collective-permute-start(bf16[40,4096]{1,0:T(8,128)(2,1)} %get-tuple-element.51), channel_id=1, source_target_pairs={{0,34},{16,50},{32,0},{48,16},{2,32},{18,48},{34,2},{50,18},{1,35}... | collective-permute-start | bytes 983048 | tf_op jit(solution)/shard_map/ppermute | solution.py:224
  195.4 22.0 %collective-permute-start.18 = (bf16[32,4096]{1,0:T(8,128)(2,1)}, bf16[32,4096]{1,0:T(8,128)(2,1)S(1)}, u32[]{:S(2)}, u32[]{:S(2)}) collective-permute-start(bf16[32,4096]{1,0:T(8,128)(2,1)} %get-tuple-element.52), channel_id=1, source_target_pairs={{0,32},{16,48},{32,2},{48,18},{2,34},{18,50},{34,0},{50,16},{1,33}... | collective-permute-start | bytes 786440 | tf_op jit(solution)/shard_map/ppermute | solution.py:224
  199.9 10.2 %collective-permute-start.22 = (bf16[648,256]{1,0:T(8,128)(2,1)S(1)}, bf16[648,256]{1,0:T(8,128)(2,1)S(1)}, u32[]{:S(2)}, u32[]{:S(2)}) collective-permute-start(bf16[648,256]{1,0:T(8,128)(2,1)S(1)} %slice.34), channel_id=1, source_target_pairs={{0,64},{64,128},{128,192},{192,256},{256,320},{320,384},{384,448},... | collective-permute-start | bytes 995336 | tf_op jit(solution)/shard_map/ppermute | solution.py:217
  215.0 17.1 %collective-permute-start.23 = (bf16[24,4096]{1,0:T(8,128)(2,1)}, bf16[24,4096]{1,0:T(8,128)(2,1)S(1)}, u32[]{:S(2)}, u32[]{:S(2)}) collective-permute-start(bf16[24,4096]{1,0:T(8,128)(2,1)} %get-tuple-element.58), channel_id=1, source_target_pairs={{0,50},{16,0},{32,16},{48,32},{2,48},{18,2},{34,18},{50,34},{1,51}... | collective-permute-start | bytes 589832 | tf_op jit(solution)/shard_map/ppermute | solution.py:224
  217.4 14.7 %collective-permute-start.24 = (bf16[24,4096]{1,0:T(8,128)(2,1)}, bf16[24,4096]{1,0:T(8,128)(2,1)S(1)}, u32[]{:S(2)}, u32[]{:S(2)}) collective-permute-start(bf16[24,4096]{1,0:T(8,128)(2,1)} %get-tuple-element.59), channel_id=1, source_target_pairs={{0,16},{16,32},{32,48},{48,2},{2,18},{18,34},{34,50},{50,0},{1,17}... | collective-permute-start | bytes 589832 | tf_op jit(solution)/shard_map/ppermute | solution.py:224
  220.9 12.0 %collective-permute-start.25 = (bf16[24,4096]{1,0:T(8,128)(2,1)}, bf16[24,4096]{1,0:T(8,128)(2,1)S(1)}, u32[]{:S(2)}, u32[]{:S(2)}) collective-permute-start(bf16[24,4096]{1,0:T(8,128)(2,1)} %get-tuple-element.60), channel_id=1, source_target_pairs={{0,32},{16,48},{32,2},{48,18},{2,34},{18,50},{34,0},{50,16},{1,33}... | collective-permute-start | bytes 589832 | tf_op jit(solution)/shard_map/ppermute | solution.py:224
  (16 other events, 115.6 us)

commit v4 on v3

--- a/solution.py
+++ b/solution.py
@@ -21,6 +21,33 @@
 SCALE = math.log2(math.e) / math.sqrt(HD)
 
 
+def fetched(at, windows, held, sems):
+    def fetches(k):
+        pieces = windows[k]
+        width = held.shape[2] // len(pieces)
+        return [
+            pltpu.make_async_copy(
+                piece, held.at[k, :, n * width : (n + 1) * width], sems.at[k, n]
+            )
+            for n, piece in enumerate(pieces)
+        ]
+
+    @pl.when(at == 0)
+    def _():
+        for k in range(len(windows)):
+            for copy in fetches(k):
+                copy.start()
+
+    for k in range(len(windows)):
+
+        @pl.when(at == k)
+        def _(k=k):
+            for copy in fetches(k):
+                copy.wait()
+
+    return held.at[at]
+
+
 def attend_kernel(base, count, split, sources, groups_out, aliased, *refs):
     query_refs, place_refs = refs[:sources], refs[sources : 2 * sources]
     sizes = [1] * (count - split) + [2] * split
@@ -31,36 +58,30 @@
         at_ref += size
     at_ref += aliased
     out_refs = refs[at_ref : at_ref + len(groups_out)]
-    held, far, sems = refs[at_ref + len(groups_out) :]
+    far = refs[at_ref + len(groups_out)]
     at = pl.program_id(0)
     mixed = sources == 5
-
-    def fetches(k):
-        pieces = windows[k]
-        width = held.shape[2] // len(pieces)
-        return [
-            pltpu.make_async_copy(
-                piece, held.at[k, :, n * width : (n + 1) * width], sems.at[k, n]
-            )
-            for n, piece in enumerate(pieces)
-        ]
-
-    @pl.when(at == 0)
-    def _():
-        for k in range(count):
-            for copy in fetches(k):
-                copy.start()
-
-    for k in range(count):
-
-        @pl.when(at == k)
-        def _(k=k):
-            for copy in fetches(k):
-                copy.wait()
-
     even = ((base + at) & 1) == 0
-    window = held.at[at]
-    span = held.shape[1] - DOCS
+    if count > 2:
+        held, sems = refs[at_ref + len(groups_out) + 1 :]
+        window = fetched(at, windows, held, sems)
+        full = window.shape[0]
+
+        def columns(number, where):
+            return window[where, number * HD : (number + 1) * HD]
+
+    else:
+        full = windows[0][0].shape[0]
+
+        def columns(number, where):
+            pieces = []
+            for window in windows:
+                width = window[0].shape[1]
+                lane = number * HD % width
+                pieces.append(window[number * HD // width][where, lane : lane + HD])
+            return pieces[0] if count == 1 else jnp.where(at == 0, pieces[0], pieces[1])
+
+    span = full - DOCS
     slots = ROUNDS * R
     rows = COLS * slots
 
@@ -73,8 +94,8 @@
             last.astype(jnp.float32)
         ]
 
-    marks = window[span:, : 2 * HD].astype(jnp.float32)
-    starts = marks[:, :HD] * 16.0 + marks[:, HD:]
+    marks = slice(span, full)
+    starts = columns(0, marks).astype(jnp.float32) * 16.0 + columns(1, marks).astype(jnp.float32)
     place = jnp.concatenate(load(place_refs, slice(0, HD)), axis=0) + float(BEHIND * HD)
     first = jnp.zeros_like(place)
     for doc in range(DOCS):
@@ -89,8 +110,8 @@
     bias = jnp.concatenate(bias, axis=1)
     per_part = GROUPS // PARTS
     for head in range(KVH):
-        keys = window[:span, 2 * head * HD : (2 * head + 1) * HD]
-        values = window[:span, (2 * head + 1) * HD : (2 * head + 2) * HD]
+        keys = columns(2 * head, slice(0, span))
+        values = columns(2 * head + 1, slice(0, span))
         for part in range(PARTS):
             first_head = head * GROUPS + part * per_part
             heads = range(first_head, first_head + per_part)
@@ -171,14 +192,22 @@
             pl.BlockSpec((slots, HD), lambda i, spot=spot: (spot(i), width // HD))
             for spot in spots
         ]
-        + [anywhere] * (len(pieces) + len(kept)),
+        + [
+            anywhere if count > 2 else pl.BlockSpec(piece.shape, lambda i: (0, 0))
+            for piece in pieces
+        ]
+        + [anywhere] * len(kept),
         out_specs=out_specs,
         out_shape=out_shape,
-        scratch_shapes=[
-            pltpu.VMEM((count,) + shape, jnp.bfloat16),
-            pltpu.VMEM((slots, width), jnp.bfloat16),
-            pltpu.SemaphoreType.DMA((count, 2)),
-        ],
+        scratch_shapes=[pltpu.VMEM((slots, width), jnp.bfloat16)]
+        + (
+            [
+                pltpu.VMEM((count,) + shape, jnp.bfloat16),
+                pltpu.SemaphoreType.DMA((count, 2)),
+            ]
+            if count > 2
+            else []
+        ),
         input_output_aliases={known + n: n for n in range(len(kept))},
         compiler_params=pltpu.CompilerParams(dimension_semantics=("arbitrary",)),
     )(*sources, *sources, *pieces, *kept)
@@ -198,11 +227,11 @@
 
 def collect(select, backs, partial):
     rows, width = select.shape[0], backs[0].shape[1]
-    chunk = width // 4
+    chunk = width // 2
     whole = pl.BlockSpec((rows, chunk), lambda i: (0, i))
     return pl.pallas_call(
         lambda *refs: collect_kernel(len(partial), *refs),
-        grid=(4,),
+        grid=(2,),
         in_specs=[pl.BlockSpec(select.shape, lambda i: (0, 0))]
         + [whole] * len(partial)
         + [pl.BlockSpec((back.shape[0], chunk), lambda i: (0, i)) for back in backs],
@@ -325,8 +354,9 @@
 
     early_orders, late_orders = list(range(late_start)), list(range(late_start, planes))
     buffers = serve(early_orders[:3], early_orders, {})
-    for step in range(2, reach - 1):
-        buffers = serve([2 * step - 1, 2 * step], early_orders, buffers)
+    for orders in (early_orders[3:7], early_orders[7:]):
+        if orders:
+            buffers = serve(orders, early_orders, buffers)
     early_backs = give_back(buffers)
     buffers = serve(late_orders[:2], late_orders, {})
     buffers = serve(late_orders[2:], late_orders, buffers)

time: 239 us -> 233 us (0.975)
  Pallas kernels: 44 us -> 36.7 us
    pallas_call x6 -> x5, Pallas kernels: 35.7 us -> 30.9 us  [attend(): pl.pallas_call(lambda *refs: attend_kernel(base, count, split, len(source...]
    pallas_call x2, Pallas kernels: 8.29 us -> 5.8 us  [collect(): pl.pallas_call(lambda *refs: collect_kernel(len(partial), *refs), grid=(2...]
  transfers between devices with their start and end apart: 26 -> 26, of which waited for: 12 -> 12; matrix products, arithmetic and copies ran while one was open for 3% -> 3% of each run, Pallas kernels for 17% -> 15%
where the time goes in v4:
time: 233 us; the launch traced here: 232 us
  starting transfers between devices  122 us (52%)
  waiting for transfers between devices  60.1 us (26%)
  Pallas kernels  36.7 us (16%)
  local copies, waits for them, and re-layouts  7.57 us (3%)
  matrix products  2.58 us (1%)
  other arithmetic  2.54 us (1%)
    ppermute x11, starting transfers between devices, along_y(): return lax.ppermute(array, ('col', 'yh'), pairs)  58 us
    ppermute x12, starting transfers between devices, along_z(): lax.ppermute(array, 'z', [(i, (i + by) % planes) for i in range(planes)])  52.7 us
    pallas_call x5, Pallas kernels, attend(): pl.pallas_call(lambda *refs: attend_kernel(base, count, split, len(source...  30.9 us
    ppermute x12, waiting for transfers between devices, along_z(): lax.ppermute(array, 'z', [(i, (i + by) % planes) for i in range(planes)])  26.3 us
    ppermute x11, waiting for transfers between devices, along_y(): return lax.ppermute(array, ('col', 'yh'), pairs)  20.7 us
    ppermute x2, waiting for transfers between devices, along_x(): return lax.ppermute(array, 'x', [(i, i + by) for i in range(peers - by)])  7.12 us
    ppermute x1, starting transfers between devices, window_of(): other = lax.ppermute(joined, 'yh', [(0, 1), (1, 0)])  6.83 us
    ppermute x1, waiting for transfers between devices, window_of(): other = lax.ppermute(joined, 'yh', [(0, 1), (1, 0)])  5.92 us
  transfers between devices with their start and end apart: 26, of which 12 were waited for; matrix products, arithmetic and copies ran while one was open for 3% of the time, Pallas kernels for 15%

profile of v4, /device:TPU:12, one launch (start us, length us, event | category | flops | bytes accessed | tf_op | source)
XLA Modules:
  0.0 232.2 jit_solution(7868404467726637623)
XLA Ops:
  0.8 6.8 %collective-permute-start.4 = (bf16[128,512]{1,0:T(8,128)(2,1)S(1)}, bf16[128,512]{1,0:T(8,128)(2,1)S(1)}, u32[]{:S(2)}, u32[]{:S(2)}) collective-permute-start(bf16[128,512]{1,0:T(8,128)(2,1)S(1)} %pad_maximum_fusion.2), channel_id=1, source_target_pairs={{0,2},{2,0},{1,3},{3,1},{4,6},{6,4},{5,7},{7,5},{8,10},{10,8},{9,1... | collective-permute-start | bytes 393224 | tf_op jit(solution)/shard_map/ppermute | solution.py:266
  8.6 5.9 %collective-permute-done.4 = bf16[128,512]{1,0:T(8,128)(2,1)S(1)} collective-permute-done((bf16[128,512]{1,0:T(8,128)(2,1)S(1)}, bf16[128,512]{1,0:T(8,128)(2,1)S(1)}, u32[]{:S(2)}, u32[]{:S(2)}) %collective-permute-start.4) | collective-permute-done | bytes 131104 | tf_op jit(solution)/shard_map/ppermute | solution.py:266
  16.1 3.1 %collective-permute-start.6 = (bf16[256,512]{1,0:T(8,128)(2,1)S(1)}, bf16[256,512]{1,0:T(8,128)(2,1)S(1)}, u32[]{:S(2)}, u32[]{:S(2)}) collective-permute-start(bf16[256,512]{1,0:T(8,128)(2,1)S(1)} %pad_maximum_fusion.1), channel_id=1, source_target_pairs={{0,4},{4,8},{8,12},{1,5},{5,9},{9,13},{2,6},{6,10},{10,14},{3,7},{... | collective-permute-start | bytes 786440 | tf_op jit(solution)/shard_map/ppermute | solution.py:258
  19.2 4.4 %collective-permute-done.5 = bf16[128,512]{1,0:T(8,128)(2,1)S(1)} collective-permute-done((bf16[128,512]{1,0:T(8,128)(2,1)S(1)}, bf16[128,512]{1,0:T(8,128)(2,1)S(1)}, u32[]{:S(2)}, u32[]{:S(2)}) %collective-permute-start.5) | collective-permute-done | bytes 131104 | tf_op jit(solution)/shard_map/ppermute | solution.py:258
  23.6 2.7 %collective-permute-done.6 = bf16[256,512]{1,0:T(8,128)(2,1)S(1)} collective-permute-done((bf16[256,512]{1,0:T(8,128)(2,1)S(1)}, bf16[256,512]{1,0:T(8,128)(2,1)S(1)}, u32[]{:S(2)}, u32[]{:S(2)}) %collective-permute-start.6) | collective-permute-done | bytes 262176 | tf_op jit(solution)/shard_map/ppermute | solution.py:258
  26.6 14.6 %collective-permute-start.7 = (bf16[648,512]{1,0:T(8,128)(2,1)S(1)}, bf16[648,512]{1,0:T(8,128)(2,1)S(1)}, u32[]{:S(2)}, u32[]{:S(2)}) collective-permute-start(bf16[648,512]{1,0:T(8,128)(2,1)S(1)} %constant_dynamic-update-slice_fusion.refs_10_), channel_id=1, source_target_pairs={{0,704},{64,0},{128,64},{192,128},{256,192},{320,256},{384,320},{4... | collective-permute-start | bytes 1990664 | tf_op jit(solution)/shard_map/ppermute | solution.py:246
  43.1 7.5 %collective-permute-done.7.refs_11_ = bf16[648,512]{1,0:T(8,128)(2,1)S(1)} collective-permute-done((bf16[648,512]{1,0:T(8,128)(2,1)S(1)}, bf16[648,512]{1,0:T(8,128)(2,1)S(1)}, u32[]{:S(2)}, u32[]{:S(2)}) %collective-permute-start.7) | collective-permute-done | bytes 663584 | tf_op jit(solution)/shard_map/ppermute | solution.py:246
  50.6 5.6 %collective-permute-start.8 = (bf16[648,512]{1,0:T(8,128)(2,1)S(1)}, bf16[648,512]{1,0:T(8,128)(2,1)}, u32[]{:S(2)}, u32[]{:S(2)}) collective-permute-start(bf16[648,512]{1,0:T(8,128)(2,1)S(1)} %collective-permute-done.7.refs_11_), channel_id=1, source_target_pairs={{0,704},{64,0},{128,64},{192,128},{256,192},{320,256},{384,320},{4... | collective-permute-start | bytes 1990664 | tf_op jit(solution)/shard_map/ppermute | solution.py:246
  58.6 6.8 %collective-permute-done.8.refs_10_ = bf16[648,512]{1,0:T(8,128)(2,1)} collective-permute-done((bf16[648,512]{1,0:T(8,128)(2,1)S(1)}, bf16[648,512]{1,0:T(8,128)(2,1)}, u32[]{:S(2)}, u32[]{:S(2)}) %collective-permute-start.8) | collective-permute-done | bytes 663584 | tf_op jit(solution)/shard_map/ppermute | solution.py:246
  65.4 5.7 %collective-permute-start.9 = (bf16[648,512]{1,0:T(8,128)(2,1)}, bf16[648,512]{1,0:T(8,128)(2,1)S(1)}, u32[]{:S(2)}, u32[]{:S(2)}) collective-permute-start(bf16[648,512]{1,0:T(8,128)(2,1)} %collective-permute-done.8.refs_10_), channel_id=1, source_target_pairs={{0,704},{64,0},{128,64},{192,128},{256,192},{320,256},{384,320},{4... | collective-permute-start | bytes 1990664 | tf_op jit(solution)/shard_map/ppermute | solution.py:246
  73.6 8.4 %collective-permute-done.9.refs_12_ = bf16[648,512]{1,0:T(8,128)(2,1)S(1)} collective-permute-done((bf16[648,512]{1,0:T(8,128)(2,1)}, bf16[648,512]{1,0:T(8,128)(2,1)S(1)}, u32[]{:S(2)}, u32[]{:S(2)}) %collective-permute-start.9) | collective-permute-done | bytes 663584 | tf_op jit(solution)/shard_map/ppermute | solution.py:246
  82.0 5.5 %collective-permute-start.10 = (bf16[648,512]{1,0:T(8,128)(2,1)S(1)}, bf16[648,512]{1,0:T(8,128)(2,1)S(1)}, u32[]{:S(2)}, u32[]{:S(2)}) collective-permute-start(bf16[648,512]{1,0:T(8,128)(2,1)S(1)} %collective-permute-done.9.refs_12_), channel_id=1, source_target_pairs={{0,704},{64,0},{128,64},{192,128},{256,192},{320,256},{384,320},{4... | collective-permute-start | bytes 1990664 | tf_op jit(solution)/shard_map/ppermute | solution.py:246
  90.9 16.7 %collective-permute-start = (bf16[96,4224]{1,0:T(8,128)(2,1)S(1)}, bf16[96,4224]{1,0:T(8,128)(2,1)S(1)}, u32[]{:S(2)}, u32[]{:S(2)}) collective-permute-start(bf16[96,4224]{1,0:T(8,128)(2,1)S(1)} %convolution_convert_fusion.1), channel_id=1, source_target_pairs={{0,16},{16,32},{32,48},{48,2},{2,18},{18,34},{34,50},{50,0},{1,17}... | collective-permute-start | bytes 2433032 | tf_op jit(solution)/shard_map/ppermute | solution.py:253
  107.6 5.1 %collective-permute-start.19 = (bf16[648,512]{1,0:T(8,128)(2,1)S(1)}, bf16[648,512]{1,0:T(8,128)(2,1)S(1)}, u32[]{:S(2)}, u32[]{:S(2)}) collective-permute-start(bf16[648,512]{1,0:T(8,128)(2,1)S(1)} %collective-permute-done.10.refs_10_), channel_id=1, source_target_pairs={{0,704},{64,0},{128,64},{192,128},{256,192},{320,256},{384,320},{4... | collective-permute-start | bytes 1990664 | tf_op jit(solution)/shard_map/ppermute | solution.py:246
  115.5 11.1 %collective-permute-start.2 = (bf16[40,4224]{1,0:T(8,128)(2,1)S(1)}, bf16[40,4224]{1,0:T(8,128)(2,1)S(1)}, u32[]{:S(2)}, u32[]{:S(2)}) collective-permute-start(bf16[40,4224]{1,0:T(8,128)(2,1)S(1)} %convolution_convert_fusion.4), channel_id=1, source_target_pairs={{0,32},{16,48},{32,2},{48,18},{2,34},{18,50},{34,0},{50,16},{1,33}... | collective-permute-start | bytes 1013768 | tf_op jit(solution)/shard_map/ppermute | solution.py:253
  128.8 4.7 %collective-permute-start.3 = (bf16[56,4224]{1,0:T(8,128)(2,1)S(1)}, bf16[56,4224]{1,0:T(8,128)(2,1)S(1)}, u32[]{:S(2)}, u32[]{:S(2)}) collective-permute-start(bf16[56,4224]{1,0:T(8,128)(2,1)S(1)} %convolution_convert_fusion.3), channel_id=1, source_target_pairs={{0,34},{16,50},{32,0},{48,16},{2,32},{18,48},{34,2},{50,18},{1,35}... | collective-permute-start | bytes 1419272 | tf_op jit(solution)/shard_map/ppermute | solution.py:253
  134.3 2.8 %collective-permute-done.2.refs_3_.refs_8_ = bf16[40,4224]{1,0:T(8,128)(2,1)S(1)} collective-permute-done((bf16[40,4224]{1,0:T(8,128)(2,1)S(1)}, bf16[40,4224]{1,0:T(8,128)(2,1)S(1)}, u32[]{:S(2)}, u32[]{:S(2)}) %collective-permute-start.2) | collective-permute-done | bytes 337952 | tf_op jit(solution)/shard_map/ppermute | solution.py:253
  137.1 4.5 %collective-permute-start.20 = (bf16[648,256]{1,0:T(8,128)(2,1)}, bf16[648,256]{1,0:T(8,128)(2,1)}, u32[]{:S(2)}, u32[]{:S(2)}) collective-permute-start(bf16[648,256]{1,0:T(8,128)(2,1)} %slice.33), channel_id=1, source_target_pairs={{0,704},{64,0},{128,64},{192,128},{256,192},{320,256},{384,320},{4... | collective-permute-start | bytes 995336 | tf_op jit(solution)/shard_map/ppermute | solution.py:246
  142.9 16.0 %collective-permute-done.3.refs_4_.refs_9_.refs_3_.refs_7_ = bf16[56,4224]{1,0:T(8,128)(2,1)S(1)} collective-permute-done((bf16[56,4224]{1,0:T(8,128)(2,1)S(1)}, bf16[56,4224]{1,0:T(8,128)(2,1)S(1)}, u32[]{:S(2)}, u32[]{:S(2)}) %collective-permute-start.3) | collective-permute-done | bytes 473120 | tf_op jit(solution)/shard_map/ppermute | solution.py:253
  160.8 7.6 %shard_map.64 = (bf16[72,4096]{1,0:T(8,128)(2,1)}, bf16[72,4096]{1,0:T(8,128)(2,1)}, bf16[72,4096]{1,0:T(8,128)(2,1)}, bf16[40,4096]{1,0:T(8,128)(2,1)}, bf16[32,4096]{1,0:T(8,128)(2,1)}) custom-call(bf16[96,4224]{1,0:T(8,128)(2,1)} %convolution_convert_fusion.2.refs_0_.refs_5_.refs_4_, bf16[96,4224]{1,0:T(8,128)(2,1)} %copy-done, ...), custom_call_target="tpu_custom_call" | custom-call | tf_op jit(solution)/shard_map/pallas_call | solution.py:185
  168.4 9.2 %shard_map.65 = (bf16[72,4096]{1,0:T(8,128)(2,1)}, bf16[72,4096]{1,0:T(8,128)(2,1)}, bf16[72,4096]{1,0:T(8,128)(2,1)}, bf16[40,4096]{1,0:T(8,128)(2,1)}, bf16[32,4096]{1,0:T(8,128)(2,1)}) custom-call(bf16[96,4224]{1,0:T(8,128)(2,1)} %convolution_convert_fusion.2.refs_0_.refs_5_.refs_4_, ...), custom_call_target="tpu_custom_call", output_to_operand_aliasing={{0}: (14, {}), {1}: (15, {}), {2}: (16, {}), {3}: (17, {}),... | custom-call | tf_op jit(solution)/shard_map/pallas_call | solution.py:185
  177.6 5.5 %shard_map.66 = (bf16[72,4096]{1,0:T(8,128)(2,1)}, bf16[72,4096]{1,0:T(8,128)(2,1)}, bf16[72,4096]{1,0:T(8,128)(2,1)}, bf16[40,4096]{1,0:T(8,128)(2,1)}, bf16[32,4096]{1,0:T(8,128)(2,1)}) custom-call(bf16[96,4224]{1,0:T(8,128)(2,1)} %convolution_convert_fusion.2.refs_0_.refs_5_.refs_4_, ...), custom_call_target="tpu_custom_call", output_to_operand_aliasing={{0}: (12, {}), {1}: (13, {}), {2}: (14, {}), {3}: (15, {}),... | custom-call | tf_op jit(solution)/shard_map/pallas_call | solution.py:185
  185.0 3.9 %collective-permute-start.16 = (bf16[72,4096]{1,0:T(8,128)(2,1)}, bf16[72,4096]{1,0:T(8,128)(2,1)S(1)}, u32[]{:S(2)}, u32[]{:S(2)}) collective-permute-start(bf16[72,4096]{1,0:T(8,128)(2,1)} %get-tuple-element.40), channel_id=1, source_target_pairs={{0,16},{16,32},{32,48},{48,2},{2,18},{18,34},{34,50},{50,0},{1,17}... | collective-permute-start | bytes 1769480 | tf_op jit(solution)/shard_map/ppermute | solution.py:253
  189.0 3.3 %collective-permute-start.17 = (bf16[40,4096]{1,0:T(8,128)(2,1)}, bf16[40,4096]{1,0:T(8,128)(2,1)S(1)}, u32[]{:S(2)}, u32[]{:S(2)}) collective-permute-start(bf16[40,4096]{1,0:T(8,128)(2,1)} %get-tuple-element.41), channel_id=1, source_target_pairs={{0,34},{16,50},{32,0},{48,16},{2,32},{18,48},{34,2},{50,18},{1,35}... | collective-permute-start | bytes 983048 | tf_op jit(solution)/shard_map/ppermute | solution.py:253
  192.3 3.5 %collective-permute-start.18 = (bf16[32,4096]{1,0:T(8,128)(2,1)}, bf16[32,4096]{1,0:T(8,128)(2,1)S(1)}, u32[]{:S(2)}, u32[]{:S(2)}) collective-permute-start(bf16[32,4096]{1,0:T(8,128)(2,1)} %get-tuple-element.42), channel_id=1, source_target_pairs={{0,32},{16,48},{32,2},{48,18},{2,34},{18,50},{34,0},{50,16},{1,33}... | collective-permute-start | bytes 786440 | tf_op jit(solution)/shard_map/ppermute | solution.py:253
  199.6 5.3 %shard_map.68 = (bf16[24,4096]{1,0:T(8,128)(2,1)}, bf16[24,4096]{1,0:T(8,128)(2,1)}, bf16[24,4096]{1,0:T(8,128)(2,1)}, bf16[24,4096]{1,0:T(8,128)(2,1)}) custom-call(bf16[96,4224]{1,0:T(8,128)(2,1)} %convolution_convert_fusion.2.refs_0_.refs_5_.refs_4_, bf16[96,4224]{1,0:T(8,128)(2,1)} %copy-done, bf16[96,4224]{1,0:T(8,128)(2,1)} %copy-done.1, ...), custom_call_target="tpu_custom_call" | custom-call | tf_op jit(solution)/shard_map/pallas_call | solution.py:185
  207.7 3.4 %shard_map.69 = (bf16[24,4096]{1,0:T(8,128)(2,1)}, bf16[24,4096]{1,0:T(8,128)(2,1)}, bf16[24,4096]{1,0:T(8,128)(2,1)}, bf16[24,4096]{1,0:T(8,128)(2,1)}) custom-call(bf16[96,4224]{1,0:T(8,128)(2,1)} %convolution_convert_fusion.2.refs_0_.refs_5_.refs_4_, ...), custom_call_target="tpu_custom_call", output_to_operand_aliasing={{0}: (10, {}), {1}: (11, {}), {2}: (12, {}), {3}: (13, {})} | custom-call | tf_op jit(solution)/shard_map/pallas_call | solution.py:185
  211.1 2.4 %collective-permute-start.23 = (bf16[24,4096]{1,0:T(8,128)(2,1)}, bf16[24,4096]{1,0:T(8,128)(2,1)S(1)}, u32[]{:S(2)}, u32[]{:S(2)}) collective-permute-start(bf16[24,4096]{1,0:T(8,128)(2,1)} %get-tuple-element.48), channel_id=1, source_target_pairs={{0,50},{16,0},{32,16},{48,32},{2,48},{18,2},{34,18},{50,34},{1,51}... | collective-permute-start | bytes 589832 | tf_op jit(solution)/shard_map/ppermute | solution.py:253
  213.5 3.5 %collective-permute-start.24 = (bf16[24,4096]{1,0:T(8,128)(2,1)}, bf16[24,4096]{1,0:T(8,128)(2,1)S(1)}, u32[]{:S(2)}, u32[]{:S(2)}) collective-permute-start(bf16[24,4096]{1,0:T(8,128)(2,1)} %get-tuple-element.49), channel_id=1, source_target_pairs={{0,16},{16,32},{32,48},{48,2},{2,18},{18,34},{34,50},{50,0},{1,17}... | collective-permute-start | bytes 589832 | tf_op jit(solution)/shard_map/ppermute | solution.py:253
  217.0 5.1 %collective-permute-start.25 = (bf16[24,4096]{1,0:T(8,128)(2,1)}, bf16[24,4096]{1,0:T(8,128)(2,1)S(1)}, u32[]{:S(2)}, u32[]{:S(2)}) collective-permute-start(bf16[24,4096]{1,0:T(8,128)(2,1)} %get-tuple-element.50), channel_id=1, source_target_pairs={{0,32},{16,48},{32,2},{48,18},{2,34},{18,50},{34,0},{50,16},{1,33}... | collective-permute-start | bytes 589832 | tf_op jit(solution)/shard_map/ppermute | solution.py:253
  223.8 3.2 %shard_map.67.refs_1_ = bf16[128,4096]{1,0:T(8,128)(2,1)} custom-call(bf16[128,288]{1,0:T(8,128)(2,1)} %fusion.refs_0_, bf16[72,4096]{1,0:T(8,128)(2,1)} %get-tuple-element.38.refs_1_, bf16[72,4096]{1,0:T(8,128)(2,1)} %copy-done.12, bf16[72,4096]{1,0:T(8,128)(2,1)} %copy-done.13, bf16[40,4096]{1,0:T(8,128)(2,1)} %copy-done.15, bf16[32,4096]{1,0:T(8,128)(2,1)} %copy-done.16), custom_call_target="tpu_custom_call" | custom-call | tf_op jit(solution)/shard_map/pallas_call | solution.py:232
  229.6 2.6 %shard_map.70 = bf16[128,4096]{1,0:T(8,128)(2,1)} custom-call(bf16[128,96]{1,0:T(8,128)(2,1)} %fusion.1.refs_0_, bf16[128,4096]{1,0:T(8,128)(2,1)} %shard_map.67.refs_1_, bf16[24,4096]{1,0:T(8,128)(2,1)} %get-tuple-element.47.refs_2_, bf16[24,4096]{1,0:T(8,128)(2,1)} %copy-done.17, bf16[24,4096]{1,0:T(8,128)(2,1)} %copy-done.18, bf16[24,4096]{1,0:T(8,128)(2,1)} %copy-done.19), custom_call_target="tpu_custom_call" | custom-call | tf_op jit(solution)/shard_map/pallas_call | solution.py:232
  (107 shorter events, 35.3 us)
Async XLA Ops:
  0.8 13.7 %collective-permute-start.4 = (bf16[128,512]{1,0:T(8,128)(2,1)S(1)}, bf16[128,512]{1,0:T(8,128)(2,1)S(1)}, u32[]{:S(2)}, u32[]{:S(2)}) collective-permute-start(bf16[128,512]{1,0:T(8,128)(2,1)S(1)} %pad_maximum_fusion.2), channel_id=1, source_target_pairs={{0,2},{2,0},{1,3},{3,1},{4,6},{6,4},{5,7},{7,5},{8,10},{10,8},{9,1... | collective-permute-start | bytes 393224 | tf_op jit(solution)/shard_map/ppermute | solution.py:266
  14.6 41.6 %copy-start.20 = (s32[1,1,32]{2,1,0:T(1,128)S(1)}, s32[1,1,32]{2,1,0:T(1,128)}, u32[]{:S(2)}) copy-start(s32[1,1,32]{2,1,0:T(1,128)} %param.7) | copy-start | bytes 388
  14.6 43.8 %copy-start.21 = (s32[1,1,32]{2,1,0:T(1,128)S(1)}, s32[1,1,32]{2,1,0:T(1,128)}, u32[]{:S(2)}) copy-start(s32[1,1,32]{2,1,0:T(1,128)} %param.8) | copy-start | bytes 388
  14.6 75.9 %copy-start.4 = (bf16[1,1,128,4096]{3,2,1,0:T(8,128)(2,1)S(1)}, bf16[1,1,128,4096]{3,2,1,0:T(8,128)(2,1)}, u32[]{:S(2)}) copy-start(bf16[1,1,128,4096]{3,2,1,0:T(8,128)(2,1)} %param.6) | copy-start | bytes 3145732
  14.6 9.0 %collective-permute-start.5 = (bf16[128,512]{1,0:T(8,128)(2,1)S(1)}, bf16[128,512]{1,0:T(8,128)(2,1)S(1)}, u32[]{:S(2)}, u32[]{:S(2)}) collective-permute-start(bf16[128,512]{1,0:T(8,128)(2,1)S(1)} %get-tuple-element.62), channel_id=1, source_target_pairs={{0,8},{4,12},{1,9},{5,13},{2,10},{6,14},{3,11},{7,15},{16,24},{20,... | collective-permute-start | bytes 393224 | tf_op jit(solution)/shard_map/ppermute | solution.py:258
  16.1 10.3 %collective-permute-start.6 = (bf16[256,512]{1,0:T(8,128)(2,1)S(1)}, bf16[256,512]{1,0:T(8,128)(2,1)S(1)}, u32[]{:S(2)}, u32[]{:S(2)}) collective-permute-start(bf16[256,512]{1,0:T(8,128)(2,1)S(1)} %pad_maximum_fusion.1), channel_id=1, source_target_pairs={{0,4},{4,8},{8,12},{1,5},{5,9},{9,13},{2,6},{6,10},{10,14},{3,7},{... | collective-permute-start | bytes 786440 | tf_op jit(solution)/shard_map/ppermute | solution.py:258
  26.6 63.9 %copy-start.6 = (bf16[648,512]{1,0:T(8,128)(2,1)}, bf16[648,512]{1,0:T(8,128)(2,1)S(1)}, u32[]{:S(2)}) copy-start(bf16[648,512]{1,0:T(8,128)(2,1)S(1)} %constant_dynamic-update-slice_fusion.refs_10_) | copy-start | bytes 1990660
  26.6 24.1 %collective-permute-start.7 = (bf16[648,512]{1,0:T(8,128)(2,1)S(1)}, bf16[648,512]{1,0:T(8,128)(2,1)S(1)}, u32[]{:S(2)}, u32[]{:S(2)}) collective-permute-start(bf16[648,512]{1,0:T(8,128)(2,1)S(1)} %constant_dynamic-update-slice_fusion.refs_10_), channel_id=1, source_target_pairs={{0,704},{64,0},{128,64},{192,128},{256,192},{320,256},{384,320},{4... | collective-permute-start | bytes 1990664 | tf_op jit(solution)/shard_map/ppermute | solution.py:246
  41.2 15.3 %collective-permute-start.11 = (bf16[648,512]{1,0:T(8,128)(2,1)S(1)}, bf16[648,512]{1,0:T(8,128)(2,1)S(1)}, u32[]{:S(2)}, u32[]{:S(2)}) collective-permute-start(bf16[648,512]{1,0:T(8,128)(2,1)S(1)} %constant_dynamic-update-slice_fusion.refs_10_), channel_id=1, source_target_pairs={{0,64},{64,128},{128,192},{192,256},{256,320},{320,384},{384,448},... | collective-permute-start | bytes 1990664 | tf_op jit(solution)/shard_map/ppermute | solution.py:246
  50.6 39.9 %copy-start.7 = (bf16[648,512]{1,0:T(8,128)(2,1)}, bf16[648,512]{1,0:T(8,128)(2,1)S(1)}, u32[]{:S(2)}) copy-start(bf16[648,512]{1,0:T(8,128)(2,1)S(1)} %collective-permute-done.7.refs_11_) | copy-start | bytes 1990660
  50.6 14.8 %collective-permute-start.8 = (bf16[648,512]{1,0:T(8,128)(2,1)S(1)}, bf16[648,512]{1,0:T(8,128)(2,1)}, u32[]{:S(2)}, u32[]{:S(2)}) collective-permute-start(bf16[648,512]{1,0:T(8,128)(2,1)S(1)} %collective-permute-done.7.refs_11_), channel_id=1, source_target_pairs={{0,704},{64,0},{128,64},{192,128},{256,192},{320,256},{384,320},{4... | collective-permute-start | bytes 1990664 | tf_op jit(solution)/shard_map/ppermute | solution.py:246
  56.4 56.3 %copy-start.8 = (bf16[648,512]{1,0:T(8,128)(2,1)}, bf16[648,512]{1,0:T(8,128)(2,1)S(1)}, u32[]{:S(2)}) copy-start(bf16[648,512]{1,0:T(8,128)(2,1)S(1)} %collective-permute-done.11.refs_12_) | copy-start | bytes 1990660
  56.5 15.2 %collective-permute-start.12 = (bf16[648,512]{1,0:T(8,128)(2,1)S(1)}, bf16[648,512]{1,0:T(8,128)(2,1)}, u32[]{:S(2)}, u32[]{:S(2)}) collective-permute-start(bf16[648,512]{1,0:T(8,128)(2,1)S(1)} %collective-permute-done.11.refs_12_), channel_id=1, source_target_pairs={{0,64},{64,128},{128,192},{192,256},{256,320},{320,384},{384,448},... | collective-permute-start | bytes 1990664 | tf_op jit(solution)/shard_map/ppermute | solution.py:246
  65.4 16.6 %collective-permute-start.9 = (bf16[648,512]{1,0:T(8,128)(2,1)}, bf16[648,512]{1,0:T(8,128)(2,1)S(1)}, u32[]{:S(2)}, u32[]{:S(2)}) collective-permute-start(bf16[648,512]{1,0:T(8,128)(2,1)} %collective-permute-done.8.refs_10_), channel_id=1, source_target_pairs={{0,704},{64,0},{128,64},{192,128},{256,192},{320,256},{384,320},{4... | collective-permute-start | bytes 1990664 | tf_op jit(solution)/shard_map/ppermute | solution.py:246
  71.7 16.8 %collective-permute-start.13 = (bf16[648,512]{1,0:T(8,128)(2,1)}, bf16[648,512]{1,0:T(8,128)(2,1)S(1)}, u32[]{:S(2)}, u32[]{:S(2)}) collective-permute-start(bf16[648,512]{1,0:T(8,128)(2,1)} %collective-permute-done.12.refs_11_), channel_id=1, source_target_pairs={{0,64},{64,128},{128,192},{192,256},{256,320},{320,384},{384,448},... | collective-permute-start | bytes 1990664 | tf_op jit(solution)/shard_map/ppermute | solution.py:246
  82.0 25.6 %collective-permute-start.10 = (bf16[648,512]{1,0:T(8,128)(2,1)S(1)}, bf16[648,512]{1,0:T(8,128)(2,1)S(1)}, u32[]{:S(2)}, u32[]{:S(2)}) collective-permute-start(bf16[648,512]{1,0:T(8,128)(2,1)S(1)} %collective-permute-done.9.refs_12_), channel_id=1, source_target_pairs={{0,704},{64,0},{128,64},{192,128},{256,192},{320,256},{384,320},{4... | collective-permute-start | bytes 1990664 | tf_op jit(solution)/shard_map/ppermute | solution.py:246
  88.5 38.1 %collective-permute-start.14 = (bf16[648,512]{1,0:T(8,128)(2,1)S(1)}, bf16[648,512]{1,0:T(8,128)(2,1)}, u32[]{:S(2)}, u32[]{:S(2)}) collective-permute-start(bf16[648,512]{1,0:T(8,128)(2,1)S(1)} %collective-permute-done.13.refs_13_), channel_id=1, source_target_pairs={{0,64},{64,128},{128,192},{192,256},{256,320},{320,384},{384,448},... | collective-permute-start | bytes 1990664 | tf_op jit(solution)/shard_map/ppermute | solution.py:246
  90.9 68.0 %collective-permute-start = (bf16[96,4224]{1,0:T(8,128)(2,1)S(1)}, bf16[96,4224]{1,0:T(8,128)(2,1)S(1)}, u32[]{:S(2)}, u32[]{:S(2)}) collective-permute-start(bf16[96,4224]{1,0:T(8,128)(2,1)S(1)} %convolution_convert_fusion.1), channel_id=1, source_target_pairs={{0,16},{16,32},{32,48},{48,2},{2,18},{18,34},{34,50},{50,0},{1,17}... | collective-permute-start | bytes 2433032 | tf_op jit(solution)/shard_map/ppermute | solution.py:253
  107.6 21.2 %collective-permute-start.19 = (bf16[648,512]{1,0:T(8,128)(2,1)S(1)}, bf16[648,512]{1,0:T(8,128)(2,1)S(1)}, u32[]{:S(2)}, u32[]{:S(2)}) collective-permute-start(bf16[648,512]{1,0:T(8,128)(2,1)S(1)} %collective-permute-done.10.refs_10_), channel_id=1, source_target_pairs={{0,704},{64,0},{128,64},{192,128},{256,192},{320,256},{384,320},{4... | collective-permute-start | bytes 1990664 | tf_op jit(solution)/shard_map/ppermute | solution.py:246
  113.2 45.7 %collective-permute-start.1 = (bf16[96,4224]{1,0:T(8,128)(2,1)S(1)}, bf16[96,4224]{1,0:T(8,128)(2,1)S(1)}, u32[]{:S(2)}, u32[]{:S(2)}) collective-permute-start(bf16[96,4224]{1,0:T(8,128)(2,1)S(1)} %convolution_convert_fusion), channel_id=1, source_target_pairs={{0,50},{16,0},{32,16},{48,32},{2,48},{18,2},{34,18},{50,34},{1,51}... | collective-permute-start | bytes 2433032 | tf_op jit(solution)/shard_map/ppermute | solution.py:253
  115.5 21.6 %collective-permute-start.2 = (bf16[40,4224]{1,0:T(8,128)(2,1)S(1)}, bf16[40,4224]{1,0:T(8,128)(2,1)S(1)}, u32[]{:S(2)}, u32[]{:S(2)}) collective-permute-start(bf16[40,4224]{1,0:T(8,128)(2,1)S(1)} %convolution_convert_fusion.4), channel_id=1, source_target_pairs={{0,32},{16,48},{32,2},{48,18},{2,34},{18,50},{34,0},{50,16},{1,33}... | collective-permute-start | bytes 1013768 | tf_op jit(solution)/shard_map/ppermute | solution.py:253
  126.6 65.7 %collective-permute-start.21 = (bf16[648,512]{1,0:T(8,128)(2,1)}, bf16[648,512]{1,0:T(8,128)(2,1)}, u32[]{:S(2)}, u32[]{:S(2)}) collective-permute-start(bf16[648,512]{1,0:T(8,128)(2,1)} %collective-permute-done.14.refs_11_), channel_id=1, source_target_pairs={{0,64},{64,128},{128,192},{192,256},{256,320},{320,384},{384,448},... | collective-permute-start | bytes 1990664 | tf_op jit(solution)/shard_map/ppermute | solution.py:246
  128.8 30.0 %collective-permute-start.3 = (bf16[56,4224]{1,0:T(8,128)(2,1)S(1)}, bf16[56,4224]{1,0:T(8,128)(2,1)S(1)}, u32[]{:S(2)}, u32[]{:S(2)}) collective-permute-start(bf16[56,4224]{1,0:T(8,128)(2,1)S(1)} %convolution_convert_fusion.3), channel_id=1, source_target_pairs={{0,34},{16,50},{32,0},{48,16},{2,32},{18,48},{34,2},{50,18},{1,35}... | collective-permute-start | bytes 1419272 | tf_op jit(solution)/shard_map/ppermute | solution.py:253
  137.1 59.6 %collective-permute-start.20 = (bf16[648,256]{1,0:T(8,128)(2,1)}, bf16[648,256]{1,0:T(8,128)(2,1)}, u32[]{:S(2)}, u32[]{:S(2)}) collective-permute-start(bf16[648,256]{1,0:T(8,128)(2,1)} %slice.33), channel_id=1, source_target_pairs={{0,704},{64,0},{128,64},{192,128},{256,192},{320,256},{384,320},{4... | collective-permute-start | bytes 995336 | tf_op jit(solution)/shard_map/ppermute | solution.py:246
  183.1 39.7 %collective-permute-start.15 = (bf16[72,4096]{1,0:T(8,128)(2,1)}, bf16[72,4096]{1,0:T(8,128)(2,1)S(1)}, u32[]{:S(2)}, u32[]{:S(2)}) collective-permute-start(bf16[72,4096]{1,0:T(8,128)(2,1)} %get-tuple-element.39), channel_id=1, source_target_pairs={{0,50},{16,0},{32,16},{48,32},{2,48},{18,2},{34,18},{50,34},{1,51}... | collective-permute-start | bytes 1769480 | tf_op jit(solution)/shard_map/ppermute | solution.py:253
  185.0 37.7 %collective-permute-start.16 = (bf16[72,4096]{1,0:T(8,128)(2,1)}, bf16[72,4096]{1,0:T(8,128)(2,1)S(1)}, u32[]{:S(2)}, u32[]{:S(2)}) collective-permute-start(bf16[72,4096]{1,0:T(8,128)(2,1)} %get-tuple-element.40), channel_id=1, source_target_pairs={{0,16},{16,32},{32,48},{48,2},{2,18},{18,34},{34,50},{50,0},{1,17}... | collective-permute-start | bytes 1769480 | tf_op jit(solution)/shard_map/ppermute | solution.py:253
  189.0 28.0 %collective-permute-start.17 = (bf16[40,4096]{1,0:T(8,128)(2,1)}, bf16[40,4096]{1,0:T(8,128)(2,1)S(1)}, u32[]{:S(2)}, u32[]{:S(2)}) collective-permute-start(bf16[40,4096]{1,0:T(8,128)(2,1)} %get-tuple-element.41), channel_id=1, source_target_pairs={{0,34},{16,50},{32,0},{48,16},{2,32},{18,48},{34,2},{50,18},{1,35}... | collective-permute-start | bytes 983048 | tf_op jit(solution)/shard_map/ppermute | solution.py:253
  192.3 21.2 %collective-permute-start.18 = (bf16[32,4096]{1,0:T(8,128)(2,1)}, bf16[32,4096]{1,0:T(8,128)(2,1)S(1)}, u32[]{:S(2)}, u32[]{:S(2)}) collective-permute-start(bf16[32,4096]{1,0:T(8,128)(2,1)} %get-tuple-element.42), channel_id=1, source_target_pairs={{0,32},{16,48},{32,2},{48,18},{2,34},{18,50},{34,0},{50,16},{1,33}... | collective-permute-start | bytes 786440 | tf_op jit(solution)/shard_map/ppermute | solution.py:253
  196.7 10.2 %collective-permute-start.22 = (bf16[648,256]{1,0:T(8,128)(2,1)S(1)}, bf16[648,256]{1,0:T(8,128)(2,1)S(1)}, u32[]{:S(2)}, u32[]{:S(2)}) collective-permute-start(bf16[648,256]{1,0:T(8,128)(2,1)S(1)} %slice.34), channel_id=1, source_target_pairs={{0,64},{64,128},{128,192},{192,256},{256,320},{320,384},{384,448},... | collective-permute-start | bytes 995336 | tf_op jit(solution)/shard_map/ppermute | solution.py:246
  211.1 15.9 %collective-permute-start.23 = (bf16[24,4096]{1,0:T(8,128)(2,1)}, bf16[24,4096]{1,0:T(8,128)(2,1)S(1)}, u32[]{:S(2)}, u32[]{:S(2)}) collective-permute-start(bf16[24,4096]{1,0:T(8,128)(2,1)} %get-tuple-element.48), channel_id=1, source_target_pairs={{0,50},{16,0},{32,16},{48,32},{2,48},{18,2},{34,18},{50,34},{1,51}... | collective-permute-start | bytes 589832 | tf_op jit(solution)/shard_map/ppermute | solution.py:253
  213.5 13.5 %collective-permute-start.24 = (bf16[24,4096]{1,0:T(8,128)(2,1)}, bf16[24,4096]{1,0:T(8,128)(2,1)S(1)}, u32[]{:S(2)}, u32[]{:S(2)}) collective-permute-start(bf16[24,4096]{1,0:T(8,128)(2,1)} %get-tuple-element.49), channel_id=1, source_target_pairs={{0,16},{16,32},{32,48},{48,2},{2,18},{18,34},{34,50},{50,0},{1,17}... | collective-permute-start | bytes 589832 | tf_op jit(solution)/shard_map/ppermute | solution.py:253
  217.0 12.0 %collective-permute-start.25 = (bf16[24,4096]{1,0:T(8,128)(2,1)}, bf16[24,4096]{1,0:T(8,128)(2,1)S(1)}, u32[]{:S(2)}, u32[]{:S(2)}) collective-permute-start(bf16[24,4096]{1,0:T(8,128)(2,1)} %get-tuple-element.50), channel_id=1, source_target_pairs={{0,32},{16,48},{32,2},{48,18},{2,34},{18,50},{34,0},{50,16},{1,33}... | collective-permute-start | bytes 589832 | tf_op jit(solution)/shard_map/ppermute | solution.py:253
  (16 other events, 119.0 us)
